TPU v7x, 32 devices: a whole 2x2x4 slice. The times are simulated.
32 devices in a mesh: dp: 4 (over y, core), seq: 8 (over z, x).
Axes of the slice: x: 2, y: 2, z: 4, core: 2. Of those that a mesh axis runs over, the one named last changes fastest.
Arguments:
- inputs: bfloat16 [2, 1024, 4, 1280], P(None, 'seq', 'dp'), may hold values from -6 to 6
- cotangent: bfloat16 [2, 1024, 4, 1280], P(None, 'seq', 'dp'), may hold values from -6 to 6
- attention_gain: bfloat16 [1280], P(('dp', 'seq')), may hold values from 0.5 to 1.5
- query_weight: bfloat16 [1280, 1280], P(('dp', 'seq')), may hold values from -0.15625 to 0.15625
- query_bias: bfloat16 [1280], P(('dp', 'seq')), may hold values from -3 to 3
- key_weight: bfloat16 [1280, 1280], P(('dp', 'seq')), may hold values from -0.15625 to 0.15625
- value_weight: bfloat16 [1280, 1280], P(('dp', 'seq')), may hold values from -0.15625 to 0.15625
- value_bias: bfloat16 [1280], P(('dp', 'seq')), may hold values from -3 to 3
- output_weight: bfloat16 [1280, 1280], P(('dp', 'seq')), may hold values from -1.25 to 1.25
- output_bias: bfloat16 [1280], P(('dp', 'seq')), may hold values from -3 to 3
- feedforward_gain: bfloat16 [1280], P(('dp', 'seq')), may hold values from 0.5 to 1.5
- hidden_weight: bfloat16 [1280, 1280], P(('dp', 'seq')), may hold values from -0.15625 to 0.15625
- hidden_bias: bfloat16 [1280], P(('dp', 'seq')), may hold values from -3 to 3
- project_weight: bfloat16 [1280, 1280], P(('dp', 'seq')), may hold values from -0.15625 to 0.15625
- project_bias: bfloat16 [1280], P(('dp', 'seq')), may hold values from -3 to 3
- depth_scale: bfloat16 [80], replicated, may hold values from -1 to 1
Outputs:
- outputs: bfloat16 [2, 1024, 4, 1280], P(None, 'seq', 'dp')
- inputs_gradient: bfloat16 [2, 1024, 4, 1280], P(None, 'seq', 'dp')
- attention_gain_gradient: float32 [1280], P(('dp', 'seq'))
- query_weight_gradient: float32 [1280, 1280], P(('dp', 'seq'))
- query_bias_gradient: float32 [1280], P(('dp', 'seq'))
- key_weight_gradient: float32 [1280, 1280], P(('dp', 'seq'))
- value_weight_gradient: float32 [1280, 1280], P(('dp', 'seq'))
- value_bias_gradient: float32 [1280], P(('dp', 'seq'))
- output_weight_gradient: float32 [1280, 1280], P(('dp', 'seq'))
- output_bias_gradient: float32 [1280], P(('dp', 'seq'))
- feedforward_gain_gradient: float32 [1280], P(('dp', 'seq'))
- hidden_weight_gradient: float32 [1280, 1280], P(('dp', 'seq'))
- hidden_bias_gradient: float32 [1280], P(('dp', 'seq'))
- project_weight_gradient: float32 [1280, 1280], P(('dp', 'seq'))
- project_bias_gradient: float32 [1280], P(('dp', 'seq'))
- depth_scale_gradient: float32 [80], replicated
All inputs are finite; a program needn't handle non-finite values.
Results may differ from a plain program's by a relative error of at most 0.019.
Values may be sent and summed in bfloat16 or wider, within the bound.
A program may use at most 256 MiB of HBM per device.

v0:
```python
import math

import jax
import jax.numpy as jnp
from jax import lax
from jax.sharding import PartitionSpec as P

HEADS = 16
HEAD_DIM = 80
ATT_BLOCK = 256


SOFT_BASE = 1.442695041
EPSILON = 1e-06


def fetch_layer(shards):
    return (
        lax.all_gather(shards[0], ("dp", "seq"), axis=0, tiled=True),
        lax.all_gather(shards[1], ("dp", "seq"), axis=0, tiled=True),
        lax.all_gather(shards[2], ("dp", "seq"), axis=0, tiled=True),
        lax.all_gather(shards[3], ("dp", "seq"), axis=0, tiled=True),
        lax.all_gather(shards[4], ("dp", "seq"), axis=0, tiled=True),
        lax.all_gather(shards[5], ("dp", "seq"), axis=0, tiled=True),
        lax.all_gather(shards[6], ("dp", "seq"), axis=0, tiled=True),
        lax.all_gather(shards[7], ("dp", "seq"), axis=0, tiled=True),
        lax.all_gather(shards[8], ("dp", "seq"), axis=0, tiled=True),
        lax.all_gather(shards[9], ("dp", "seq"), axis=0, tiled=True),
        lax.all_gather(shards[10], ("dp", "seq"), axis=0, tiled=True),
        lax.all_gather(shards[11], ("dp", "seq"), axis=0, tiled=True),
        lax.all_gather(shards[12], ("dp", "seq"), axis=0, tiled=True),
    )


def arrange(first, second):
    return (
        first[0],
        first[1],
        first[2],
        first[3],
        second[0],
        second[1],
        second[2],
        second[3],
        first[4],
        first[5],
        first[6],
        second[4],
        second[5],
    )


def spread_each(grads):
    first = (
        lax.psum_scatter(grads[0], ("dp", "seq"), scatter_dimension=0, tiled=True),
        lax.psum_scatter(grads[1], ("dp", "seq"), scatter_dimension=0, tiled=True),
        lax.psum_scatter(grads[2], ("dp", "seq"), scatter_dimension=0, tiled=True),
        lax.psum_scatter(grads[3], ("dp", "seq"), scatter_dimension=0, tiled=True),
        lax.psum_scatter(grads[8], ("dp", "seq"), scatter_dimension=0, tiled=True),
        lax.psum_scatter(grads[9], ("dp", "seq"), scatter_dimension=0, tiled=True),
        lax.psum_scatter(grads[10], ("dp", "seq"), scatter_dimension=0, tiled=True),
    )
    second = (
        lax.psum_scatter(grads[4], ("dp", "seq"), scatter_dimension=0, tiled=True),
        lax.psum_scatter(grads[5], ("dp", "seq"), scatter_dimension=0, tiled=True),
        lax.psum_scatter(grads[6], ("dp", "seq"), scatter_dimension=0, tiled=True),
        lax.psum_scatter(grads[7], ("dp", "seq"), scatter_dimension=0, tiled=True),
        lax.psum_scatter(grads[11], ("dp", "seq"), scatter_dimension=0, tiled=True),
        lax.psum_scatter(grads[12], ("dp", "seq"), scatter_dimension=0, tiled=True),
    )
    return arrange(first, second)


def masked_weights(queries, key_block, key_start, query_place):
    scores = jnp.einsum("tshd,kshd->shtk", queries, key_block, preferred_element_type=jnp.float32)
    key_place = key_start + jnp.arange(key_block.shape[0], dtype=jnp.int32)
    allowed = key_place[None, :] // ATT_BLOCK <= query_place[:, None] // ATT_BLOCK
    return jnp.where(allowed[None, None], jnp.exp(scores), 0.0)


def rms_scale(values):
    return lax.rsqrt(jnp.mean(values * values, axis=-1, keepdims=True) + EPSILON)


def block_count(key_limit, span, length):
    return jnp.minimum((key_limit + span - 1) // span, length // span)


def forward(source, whole, query_place, key_limit, rate_full):
    (
        norm_one,
        query_mat,
        query_add,
        key_mat,
        value_mat,
        value_add,
        output_mat,
        output_add,
        norm_two,
        hidden_mat,
        hidden_add,
        project_mat,
        project_add,
    ) = whole
    tokens, seqs, width = source.shape
    depth = width // HEADS
    rows = tokens * seqs
    xfloat = source.astype(jnp.float32).reshape(rows, width)
    inv_one = rms_scale(xfloat)
    normed = (xfloat * inv_one * norm_one).astype(jnp.bfloat16)
    query_pre = jnp.dot(normed, query_mat, preferred_element_type=jnp.float32) + query_add
    queries = (query_pre * rate_full).astype(jnp.bfloat16)
    keys = jnp.dot(normed, key_mat, preferred_element_type=jnp.float32).astype(jnp.bfloat16)
    values = (jnp.dot(normed, value_mat, preferred_element_type=jnp.float32) + value_add).astype(
        jnp.bfloat16
    )
    all_keys, all_values = (
        lax.all_gather(keys.reshape(tokens, seqs, width), "seq", axis=0, tiled=True),
        lax.all_gather(values.reshape(tokens, seqs, width), "seq", axis=0, tiled=True),
    )
    length = all_keys.shape[0]
    key_heads = all_keys.reshape(length, seqs, HEADS, depth)
    value_heads = all_values.reshape(length, seqs, HEADS, depth)
    query_heads = queries.reshape(tokens, seqs, HEADS, depth)
    span = math.gcd(length, 512)

    def add_block(index, carry):
        numer, total = carry
        start = index * span
        key_block = lax.dynamic_slice_in_dim(key_heads, start, span, 0)
        value_block = lax.dynamic_slice_in_dim(value_heads, start, span, 0)
        weights = masked_weights(query_heads, key_block, start, query_place)
        numer = numer + jnp.einsum(
            "shtk,kshd->tshd",
            weights.astype(jnp.bfloat16),
            value_block,
            preferred_element_type=jnp.float32,
        )
        total = total + jnp.sum(weights, axis=-1)
        return (numer, total)

    start_carry = (
        jnp.zeros((tokens, seqs, HEADS, depth), jnp.float32),
        jnp.zeros((seqs, HEADS, tokens), jnp.float32),
    )
    numer, total = lax.fori_loop(0, block_count(key_limit, span, length), add_block, start_carry)
    total_rows = jnp.transpose(total, (2, 0, 1))
    attended = numer / total_rows[..., None]
    mixed = attended.reshape(rows, width).astype(jnp.bfloat16)
    residual = xfloat + (
        jnp.dot(mixed, output_mat, preferred_element_type=jnp.float32) + output_add
    )
    inv_two = rms_scale(residual)
    second = (residual * inv_two * norm_two).astype(jnp.bfloat16)
    hidden_pre = jnp.dot(second, hidden_mat, preferred_element_type=jnp.float32) + hidden_add
    active = jax.nn.silu(hidden_pre).astype(jnp.bfloat16)
    result = (
        residual + (jnp.dot(active, project_mat, preferred_element_type=jnp.float32) + project_add)
    ).astype(jnp.bfloat16)
    saved = (
        xfloat,
        inv_one,
        normed,
        query_pre,
        query_heads,
        key_heads,
        value_heads,
        attended,
        total_rows,
        mixed,
        residual,
        inv_two,
        second,
        hidden_pre,
        active,
    )
    return (saved, result.reshape(tokens, seqs, width))


def backward(saved, slope, whole, query_place, key_limit, rate_full):
    (
        norm_one,
        query_mat,
        query_add,
        key_mat,
        value_mat,
        value_add,
        output_mat,
        output_add,
        norm_two,
        hidden_mat,
        hidden_add,
        project_mat,
        project_add,
    ) = whole
    (
        xfloat,
        inv_one,
        normed,
        query_pre,
        query_heads,
        key_heads,
        value_heads,
        attended,
        total_rows,
        mixed,
        residual,
        inv_two,
        second,
        hidden_pre,
        active,
    ) = saved
    tokens, seqs, width = slope.shape
    depth = width // HEADS
    rows = tokens * seqs
    length = key_heads.shape[0]
    upper = slope.reshape(rows, width)
    project_grad = jnp.einsum("rf,rd->fd", active, upper, preferred_element_type=jnp.float32)
    project_bias_grad = jnp.sum(upper.astype(jnp.float32), axis=0)
    active_grad = jnp.einsum("rd,fd->rf", upper, project_mat, preferred_element_type=jnp.float32)
    logistic = jax.nn.sigmoid(hidden_pre)
    hidden_grad = (active_grad * logistic * (1.0 + hidden_pre * (1.0 - logistic))).astype(
        jnp.bfloat16
    )
    hidden_mat_grad = jnp.einsum(
        "rd,rf->df", second, hidden_grad, preferred_element_type=jnp.float32
    )
    hidden_bias_grad = jnp.sum(hidden_grad.astype(jnp.float32), axis=0)
    second_grad = jnp.einsum(
        "rf,df->rd", hidden_grad, hidden_mat, preferred_element_type=jnp.float32
    )
    normal_two = residual * inv_two
    scaled_two = second_grad * norm_two
    norm_two_grad = jnp.sum(second_grad * normal_two, axis=0)
    residual_grad = upper.astype(jnp.float32) + inv_two * (
        scaled_two - normal_two * jnp.mean(scaled_two * normal_two, axis=-1, keepdims=True)
    )
    branch_grad = residual_grad.astype(jnp.bfloat16)
    output_mat_grad = jnp.einsum(
        "rd,re->de", mixed, branch_grad, preferred_element_type=jnp.float32
    )
    output_bias_grad = jnp.sum(branch_grad.astype(jnp.float32), axis=0)
    mixed_grad = jnp.einsum(
        "re,de->rd", branch_grad, output_mat, preferred_element_type=jnp.float32
    ).astype(jnp.bfloat16)
    mixed_heads = mixed_grad.reshape(tokens, seqs, HEADS, depth).astype(jnp.float32)
    scaled_grad = (mixed_heads / total_rows[..., None]).astype(jnp.bfloat16)
    centre_rows = jnp.sum(mixed_heads * attended, axis=-1) / total_rows
    centre = jnp.transpose(centre_rows, (1, 2, 0))

    def score_slopes(weights, value_block):
        dots = jnp.einsum(
            "tshd,kshd->shtk", scaled_grad, value_block, preferred_element_type=jnp.float32
        )
        return (weights * (dots - centre[..., None])).astype(jnp.bfloat16)

    span = math.gcd(length, 512)

    def query_block(index, accum):
        start = index * span
        key_block = lax.dynamic_slice_in_dim(key_heads, start, span, 0)
        value_block = lax.dynamic_slice_in_dim(value_heads, start, span, 0)
        weights = masked_weights(query_heads, key_block, start, query_place)
        return accum + jnp.einsum(
            "shtk,kshd->tshd",
            score_slopes(weights, value_block),
            key_block,
            preferred_element_type=jnp.float32,
        )

    query_grad = lax.fori_loop(
        0,
        block_count(key_limit, span, length),
        query_block,
        jnp.zeros((tokens, seqs, HEADS, depth), jnp.float32),
    )
    count = lax.axis_size("seq") * tokens
    piece = math.gcd(count, 512)

    def one_piece(index):
        begin = index * piece

        def compute(begin_at):
            key_block = lax.dynamic_slice_in_dim(key_heads, begin_at, piece, 0)
            value_block = lax.dynamic_slice_in_dim(value_heads, begin_at, piece, 0)
            weights = masked_weights(query_heads, key_block, begin_at, query_place)
            slopes = score_slopes(weights, value_block)
            key_part = jnp.einsum(
                "shtk,tshd->kshd", slopes, query_heads, preferred_element_type=jnp.float32
            )
            value_part = jnp.einsum(
                "shtk,tshd->kshd",
                weights.astype(jnp.bfloat16),
                scaled_grad,
                preferred_element_type=jnp.float32,
            )
            return jnp.concatenate(
                [key_part.reshape(piece, seqs, width), value_part.reshape(piece, seqs, width)],
                axis=-1,
            )

        def nothing(begin_at):
            return jnp.zeros((piece, seqs, 2 * width), jnp.float32)

        return lax.cond(begin < key_limit, compute, nothing, begin)

    pieces = lax.map(one_piece, jnp.arange(count // piece, dtype=jnp.int32))
    key_sums = lax.psum_scatter(
        pieces.reshape(count, seqs, 2 * width).astype(jnp.bfloat16),
        "seq",
        scatter_dimension=0,
        tiled=True,
    ).astype(jnp.float32)
    key_grad = key_sums[..., :width].reshape(rows, width).astype(jnp.bfloat16)
    value_grad = key_sums[..., width:].reshape(rows, width).astype(jnp.bfloat16)
    query_flat = query_grad.reshape(rows, width)
    scale_part = jnp.sum((query_flat * query_pre).reshape(rows, HEADS, depth), axis=(0, 1))
    query_slope = (query_flat * rate_full).astype(jnp.bfloat16)
    query_mat_grad = jnp.einsum(
        "rd,re->de", normed, query_slope, preferred_element_type=jnp.float32
    )
    query_bias_grad = jnp.sum(query_slope.astype(jnp.float32), axis=0)
    key_mat_grad = jnp.einsum("rd,re->de", normed, key_grad, preferred_element_type=jnp.float32)
    value_mat_grad = jnp.einsum("rd,re->de", normed, value_grad, preferred_element_type=jnp.float32)
    value_bias_grad = jnp.sum(value_grad.astype(jnp.float32), axis=0)
    normed_grad = (
        jnp.einsum("re,de->rd", query_slope, query_mat, preferred_element_type=jnp.float32)
        + jnp.einsum("re,de->rd", key_grad, key_mat, preferred_element_type=jnp.float32)
        + jnp.einsum("re,de->rd", value_grad, value_mat, preferred_element_type=jnp.float32)
    )
    normal_one = xfloat * inv_one
    scaled_one = normed_grad * norm_one
    norm_one_grad = jnp.sum(normed_grad * normal_one, axis=0)
    source_grad = residual_grad + inv_one * (
        scaled_one - normal_one * jnp.mean(scaled_one * normal_one, axis=-1, keepdims=True)
    )
    grads = (
        norm_one_grad,
        query_mat_grad,
        query_bias_grad,
        key_mat_grad,
        value_mat_grad,
        value_bias_grad,
        output_mat_grad,
        output_bias_grad,
        norm_two_grad,
        hidden_mat_grad,
        hidden_bias_grad,
        project_grad,
        project_bias_grad,
    )
    return (grads, scale_part, source_grad.astype(jnp.bfloat16).reshape(tokens, seqs, width))


def on_device(
    inputs,
    cotangent,
    attention_gain,
    query_weight,
    query_bias,
    key_weight,
    value_weight,
    value_bias,
    output_weight,
    output_bias,
    feedforward_gain,
    hidden_weight,
    hidden_bias,
    project_weight,
    project_bias,
    depth_scale,
):
    shards = (
        attention_gain,
        query_weight,
        query_bias,
        key_weight,
        value_weight,
        value_bias,
        output_weight,
        output_bias,
        feedforward_gain,
        hidden_weight,
        hidden_bias,
        project_weight,
        project_bias,
    )
    tokens = inputs.shape[1]
    first_place = lax.axis_index("seq") * tokens
    query_place = first_place + jnp.arange(tokens, dtype=jnp.int32)
    key_limit = ((first_place + tokens - 1) // ATT_BLOCK + 1) * ATT_BLOCK
    depth_float = depth_scale.astype(jnp.float32)
    rate_full = jnp.tile(SOFT_BASE / math.sqrt(HEAD_DIM) * jax.nn.softplus(depth_float), HEADS)
    results = []
    source_grads = []
    owned = None
    scale_total = jnp.zeros((HEAD_DIM,), jnp.float32)
    for micro in range(inputs.shape[0]):
        whole = fetch_layer(shards)
        saved, result = forward(inputs[micro], whole, query_place, key_limit, rate_full)
        results.append(result)
        whole = fetch_layer(shards)
        grads, scale_part, source_grad = backward(
            saved, cotangent[micro], whole, query_place, key_limit, rate_full
        )
        source_grads.append(source_grad)
        scale_total = scale_total + scale_part
        shares = spread_each(grads)
        owned = shares if owned is None else jax.tree.map(jnp.add, owned, shares)
    scale_summed = lax.psum(scale_total, ("dp", "seq"))
    depth_grad = scale_summed * (SOFT_BASE / math.sqrt(HEAD_DIM)) * jax.nn.sigmoid(depth_float)
    return (
        jnp.stack(results, axis=0),
        jnp.stack(source_grads, axis=0),
        owned[0],
        owned[1],
        owned[2],
        owned[3],
        owned[4],
        owned[5],
        owned[6],
        owned[7],
        owned[8],
        owned[9],
        owned[10],
        owned[11],
        owned[12],
        depth_grad,
    )


def solution(mesh):
    in_specs = (
        P(None, "seq", "dp", None),
        P(None, "seq", "dp", None),
        P(("dp", "seq")),
        P(("dp", "seq"), None),
        P(("dp", "seq")),
        P(("dp", "seq"), None),
        P(("dp", "seq"), None),
        P(("dp", "seq")),
        P(("dp", "seq"), None),
        P(("dp", "seq")),
        P(("dp", "seq")),
        P(("dp", "seq"), None),
        P(("dp", "seq")),
        P(("dp", "seq"), None),
        P(("dp", "seq")),
        P(),
    )
    out_specs = (
        P(None, "seq", "dp", None),
        P(None, "seq", "dp", None),
        P(("dp", "seq")),
        P(("dp", "seq"), None),
        P(("dp", "seq")),
        P(("dp", "seq"), None),
        P(("dp", "seq"), None),
        P(("dp", "seq")),
        P(("dp", "seq"), None),
        P(("dp", "seq")),
        P(("dp", "seq")),
        P(("dp", "seq"), None),
        P(("dp", "seq")),
        P(("dp", "seq"), None),
        P(("dp", "seq")),
        P(),
    )
    return jax.shard_map(
        on_device, mesh=mesh, in_specs=in_specs, out_specs=out_specs, check_vma=False
    )
```

profile of v0, /device:TPU:0, one launch (start us, length us, event | category | flops | bytes accessed | tf_op | source)
XLA Modules:
  0.0 1807.8 jit_solution(11737675136650935059)
XLA Ops:
  15.4 42.9 %all-reduce.15 = (bf16[1280]{0:T(1024)(128)(2,1)S(1)}, bf16[1280]{0:T(1024)(128)(2,1)S(1)}, bf16[1280]{0:T(1024)(128)(2,1)S(1)}, bf16[1280]{0:T(1024)(128)(2,1)S...) all-reduce(bf16[1280]{0:T(1024)(128)(2,1)S(1)} %dynamic-update-slic, ...), channel_id=1, replica_groups=mesh['dp'=4,'seq'=8] {'dp','seq'}, use_global_device_ids=true, to_apply=%add.1 | all-reduce | flops 8960 | bytes 35840
  59.6 13.7 all-gather.17.cloned.1.call-done
  76.8 57.7 %all-gather.15.cloned.1.call-done = bf16[1280,1280]{1,0:T(8,128)(2,1)} async-done(((bf16[40,1280]{1,0:T(8,128)(2,1)}), bf16[1280,1280]{1,0:T(8,128)(2,1)}) %all-gather.15.cloned.1.call-update) | async-done | bytes 3276816 | tf_op jit(solution)/shard_map/all_gather | solution.py:23
  146.7 48.9 %all-gather.19.cloned.1.call-done = bf16[1280,1280]{1,0:T(8,128)(2,1)} async-done(((bf16[40,1280]{1,0:T(8,128)(2,1)}), bf16[1280,1280]{1,0:T(8,128)(2,1)}) %all-gather.19.cloned.1.call-update) | async-done | bytes 3276816 | tf_op jit(solution)/shard_map/all_gather | solution.py:20
  200.5 50.2 %all-gather.33.cloned.1.call-done = bf16[1024,1280]{1,0:T(8,128)(2,1)} async-done(((bf16[128,1280]{1,0:T(8,128)(2,1)}), bf16[1024,1280]{1,0:T(8,128)(2,1)}) %all-gather.33.cloned.1.call-update) | async-done | bytes 2621456 | tf_op jit(solution)/shard_map/all_gather | solution.py:118
  253.7 52.6 %all-gather.31.cloned.1.call-done = bf16[1024,1280]{1,0:T(8,128)(2,1)} async-done(((bf16[128,1280]{1,0:T(8,128)(2,1)}), bf16[1024,1280]{1,0:T(8,128)(2,1)}) %all-gather.31.cloned.1.call-update) | async-done | bytes 2621456 | tf_op jit(solution)/shard_map/all_gather | solution.py:119
  317.8 49.5 %all-gather.21.cloned.1.call-done = bf16[1280,1280]{1,0:T(8,128)(2,1)} async-done(((bf16[40,1280]{1,0:T(8,128)(2,1)}), bf16[1280,1280]{1,0:T(8,128)(2,1)}) %all-gather.21.cloned.1.call-update) | async-done | bytes 3276816 | tf_op jit(solution)/shard_map/all_gather | solution.py:25
  370.9 51.6 %all-gather.27.cloned.1.call-done = bf16[1024,1280]{1,0:T(8,128)(2,1)} async-done(((bf16[128,1280]{1,0:T(8,128)(2,1)}), bf16[1024,1280]{1,0:T(8,128)(2,1)}) %all-gather.27.cloned.1.call-update) | async-done | bytes 2621456 | tf_op jit(solution)/shard_map/all_gather | solution.py:119
  427.0 50.7 %all-gather.29.cloned.1.call-done = bf16[1024,1280]{1,0:T(8,128)(2,1)} async-done(((bf16[128,1280]{1,0:T(8,128)(2,1)}), bf16[1024,1280]{1,0:T(8,128)(2,1)}) %all-gather.29.cloned.1.call-update) | async-done | bytes 2621456 | tf_op jit(solution)/shard_map/all_gather | solution.py:118
  491.0 47.8 %all-gather.23.cloned.1.call-done = bf16[1280,1280]{1,0:T(8,128)(2,1)} async-done(((bf16[40,1280]{1,0:T(8,128)(2,1)}), bf16[1280,1280]{1,0:T(8,128)(2,1)}) %all-gather.23.cloned.1.call-update) | async-done | bytes 3276816 | tf_op jit(solution)/shard_map/all_gather | solution.py:28
  544.1 55.7 %all-gather.25.cloned.1.call-done = bf16[1280,1280]{1,0:T(8,128)(2,1)} async-done(((bf16[40,1280]{1,0:T(8,128)(2,1)}), bf16[1280,1280]{1,0:T(8,128)(2,1)}) %all-gather.25.cloned.1.call-update) | async-done | bytes 3276816 | tf_op jit(solution)/shard_map/all_gather | solution.py:30
  621.1 29.4 %while.86 = (s32[]{:T(128)}, bf16[2,512,1,2560]{3,1,0,2:T(8,128)(2,1)}, s32[2]{0:T(128)S(1)}, s32[]{:T(128)}, bf16[1024,1,16,80]{0,3,2,1:T(8,128)(2,1)S(1)}, /*i...) while((s32[]{:T(128)}, ...), condition=%wide.region_17.18_spmd.clone, body=%wide.region_14.17_spmd.clone.sunk | while | flops 682698752 | bytes 62601616 | solution.py:307
  622.7 13.3 conditional.6
  626.5 6.2 fusion.34
  662.7 39.7 %while.87 = (s32[]{:T(128)}, bf16[2,512,1,2560]{3,1,0,2:T(8,128)(2,1)}, s32[2]{0:T(128)S(1)}, s32[]{:T(128)}, bf16[1024,1,16,80]{0,3,2,1:T(8,128)(2,1)}, /*index...) while((s32[]{:T(128)}, ...), condition=%wide.region_27.28_spmd.clone, body=%wide.region_24.27_spmd.clone.sunk | while | flops 682698752 | bytes 50805076 | solution.py:307
  673.9 14.5 conditional.7
  674.1 5.2 fusion.64
  679.3 5.7 fusion.61
  722.8 8.4 while.91
  725.7 5.3 fusion.391
  732.1 9.7 while.90
  736.6 5.2 fusion.383
  750.0 15.5 reduce-scatter.9.cloned.1.call-done
  770.2 101.3 %reduce-scatter.11.cloned.1.call-done = bf16[128,1,2560]{2,0,1:T(8,128)(2,1)} async-done(((bf16[1024,1,2560]{2,0,1:T(8,128)(2,1)}), bf16[128,1,2560]{2,0,1:T(8,128)(2,1)}) %reduce-scatter.11.cloned.1.call-update) | async-done | bytes 655376 | tf_op jit(solution)/shard_map/reduce_scatter | solution.py:308
  871.5 6.8 convolution_add_fusion.4
  903.5 44.7 %all-reduce.14 = (f32[1280]{0:T(1024)S(1)}, f32[1280]{0:T(1024)S(1)}, f32[1280]{0:T(1024)S(1)}, f32[1280]{0:T(1024)S(1)}, f32[1280]{0:T(1024)S(1)}, /*index=5*/f...) all-reduce(f32[1280]{0:T(1024)S(1)} %add.638, ...), channel_id=21, replica_groups=mesh['dp'=4,'seq'=8] {'dp','seq'}, use_global_device_ids=true, to_apply=%region_31.32.clone | all-reduce | flops 9040 | bytes 72320
  954.1 73.1 %reduce-scatter.21.cloned.1.call-done = f32[40,1280]{1,0:T(8,128)} async-done(((f32[1280,1280]{1,0:T(8,128)}), f32[40,1280]{1,0:T(8,128)}) %reduce-scatter.21.cloned.1.call-update) | async-done | bytes 204816 | tf_op jit(solution)/shard_map/reduce_scatter | solution.py:60
  1027.2 156.0 %reduce-scatter.19.cloned.1.call-done = f32[40,1280]{1,0:T(8,128)} async-done(((f32[1280,1280]{1,0:T(8,128)}), f32[40,1280]{1,0:T(8,128)}) %reduce-scatter.19.cloned.1.call-update) | async-done | bytes 204816 | tf_op jit(solution)/shard_map/reduce_scatter | solution.py:66
  1183.1 154.9 %reduce-scatter.23.cloned.1.call-done = f32[40,1280]{1,0:T(8,128)} async-done(((f32[1280,1280]{1,0:T(8,128)}), f32[40,1280]{1,0:T(8,128)}) %reduce-scatter.23.cloned.1.call-update) | async-done | bytes 204816 | tf_op jit(solution)/shard_map/reduce_scatter | solution.py:68
  1338.0 154.3 %reduce-scatter.13.cloned.1.call-done = f32[40,1280]{1,0:T(8,128)} async-done(((f32[1280,1280]{1,0:T(8,128)}), f32[40,1280]{1,0:T(8,128)}) %reduce-scatter.13.cloned.1.call-update) | async-done | bytes 204816 | tf_op jit(solution)/shard_map/reduce_scatter | solution.py:56
  1492.3 153.7 %reduce-scatter.15.cloned.1.call-done = f32[40,1280]{1,0:T(8,128)} async-done(((f32[1280,1280]{1,0:T(8,128)}), f32[40,1280]{1,0:T(8,128)}) %reduce-scatter.15.cloned.1.call-update) | async-done | bytes 204816 | tf_op jit(solution)/shard_map/reduce_scatter | solution.py:58
  1646.0 154.5 %reduce-scatter.17.cloned.1.call-done = f32[40,1280]{1,0:T(8,128)} async-done(((f32[1280,1280]{1,0:T(8,128)}), f32[40,1280]{1,0:T(8,128)}) %reduce-scatter.17.cloned.1.call-update) | async-done | bytes 204816 | tf_op jit(solution)/shard_map/reduce_scatter | solution.py:64
  (378 shorter events, 223.2 us)
Async XLA Ops:
  7.2 127.3 %copy-start.6 = (bf16[2,128,1,1280]{3,1,2,0:T(8,128)(2,1)S(1)}, bf16[2,128,1,1280]{3,1,2,0:T(8,128)(2,1)}, u32[]{:S(2)}) copy-start(bf16[2,128,1,1280]{3,1,2,0:T(8,128)(2,1)} %param.32) | copy-start | bytes 1966084
  7.2 66.1 %all-gather.17.cloned.1.call-start = ((), (), s32[]{:S(2)}) async-start(), calls=%async_computation.9 | async-start | bytes 3379200 | tf_op jit(solution)/shard_map/all_gather | solution.py:22
  7.9 126.6 %all-gather.15.cloned.1.call-start = ((), (), s32[]{:S(2)}) async-start(), calls=%async_computation.8 | async-start | bytes 3379200 | tf_op jit(solution)/shard_map/all_gather | solution.py:23
  8.7 187.0 %all-gather.19.cloned.1.call-start = ((), (), s32[]{:S(2)}) async-start(), calls=%async_computation.10 | async-start | bytes 3379200 | tf_op jit(solution)/shard_map/all_gather | solution.py:20
  9.4 241.3 %all-gather.33.cloned.1.call-start = ((), (), s32[]{:S(2)}) async-start(), calls=%async_computation.19 | async-start | bytes 2949120 | tf_op jit(solution)/shard_map/all_gather | solution.py:118
  58.3 140.1 %copy-start.49 = (f32[1280]{0:T(1024)}, f32[1280]{0:T(1024)S(1)}, u32[]{:S(2)}) copy-start(f32[1280]{0:T(1024)S(1)} %convert_element_type.383) | copy-start | bytes 15364
  59.6 136.0 %copy-start.70 = (f32[128]{0:T(128)}, f32[128]{0:T(128)S(1)}, u32[]{:S(2)}) copy-start(f32[128]{0:T(128)S(1)} %add_rsqrt_fusion.1) | copy-start | bytes 1540
  76.7 229.6 %all-gather.31.cloned.1.call-start = ((), (), s32[]{:S(2)}) async-start(), calls=%async_computation.18 | async-start | bytes 2949120 | tf_op jit(solution)/shard_map/all_gather | solution.py:119
  137.8 229.5 %all-gather.21.cloned.1.call-start = ((), (), s32[]{:S(2)}) async-start(), calls=%async_computation.11 | async-start | bytes 3379200 | tf_op jit(solution)/shard_map/all_gather | solution.py:25
  138.4 284.2 %all-gather.27.cloned.1.call-start = ((), (), s32[]{:S(2)}) async-start(), calls=%async_computation.16 | async-start | bytes 2949120 | tf_op jit(solution)/shard_map/all_gather | solution.py:119
  138.4 59.9 %copy-start.62 = (f32[128]{0:T(128)}, f32[128]{0:T(128)S(1)}, u32[]{:S(2)}) copy-start(f32[128]{0:T(128)S(1)} %add_rsqrt_fusion.3) | copy-start | bytes 1540
  141.8 336.0 %all-gather.29.cloned.1.call-start = ((), (), s32[]{:S(2)}) async-start(), calls=%async_computation.17 | async-start | bytes 2949120 | tf_op jit(solution)/shard_map/all_gather | solution.py:118
  145.1 393.7 %all-gather.23.cloned.1.call-start = ((), (), s32[]{:S(2)}) async-start(), calls=%async_computation.12 | async-start | bytes 3379200 | tf_op jit(solution)/shard_map/all_gather | solution.py:28
  145.9 453.9 %all-gather.25.cloned.1.call-start = ((), (), s32[]{:S(2)}) async-start(), calls=%async_computation.13 | async-start | bytes 3379200 | tf_op jit(solution)/shard_map/all_gather | solution.py:30
  146.5 619.0 %reduce-scatter.9.cloned.1.call-start = ((), (), s32[]{:S(2)}) async-start(), calls=%async_computation.14 | async-start | bytes 5898240 | tf_op jit(solution)/shard_map/reduce_scatter | solution.py:308
  146.6 53.5 %copy-start.75 = (f32[80]{0:T(128)}, f32[80]{0:T(128)S(1)}, u32[]{:S(2)}) copy-start(f32[80]{0:T(128)S(1)} %fusion.280) | copy-start | bytes 964
  146.7 53.3 %copy-start.60 = (f32[1280]{0:T(1024)}, f32[1280]{0:T(1024)S(1)}, u32[]{:S(2)}) copy-start(f32[1280]{0:T(1024)S(1)} %mul.380) | copy-start | bytes 15364
  315.5 111.5 %copy-start = (bf16[1024,1,16,80]{0,3,2,1:T(8,128)(2,1)}, bf16[1024,1,16,80]{0,3,2,1:T(8,128)(2,1)S(1)}, u32[]{:S(2)}) copy-start(bf16[1024,1,16,80]{0,3,2,1:T(8,128)(2,1)S(1)} %get-tuple-element.1916) | copy-start | bytes 7864324
  650.5 12.2 copy-start.4
  650.6 221.0 %reduce-scatter.11.cloned.1.call-start = ((), (), s32[]{:S(2)}) async-start(), calls=%async_computation.15 | async-start | bytes 5898240 | tf_op jit(solution)/shard_map/reduce_scatter | solution.py:308
  702.5 324.7 %reduce-scatter.21.cloned.1.call-start = ((), (), s32[]{:S(2)}) async-start(), calls=%async_computation.24 | async-start | bytes 6758400 | tf_op jit(solution)/shard_map/reduce_scatter | solution.py:60
  708.6 474.5 %reduce-scatter.19.cloned.1.call-start = ((), (), s32[]{:S(2)}) async-start(), calls=%async_computation.23 | async-start | bytes 6758400 | tf_op jit(solution)/shard_map/reduce_scatter | solution.py:66
  714.6 623.4 %reduce-scatter.23.cloned.1.call-start = ((), (), s32[]{:S(2)}) async-start(), calls=%async_computation.25 | async-start | bytes 6758400 | tf_op jit(solution)/shard_map/reduce_scatter | solution.py:68
  720.8 771.5 %reduce-scatter.13.cloned.1.call-start = ((), (), s32[]{:S(2)}) async-start(), calls=%async_computation.20 | async-start | bytes 6758400 | tf_op jit(solution)/shard_map/reduce_scatter | solution.py:56
  732.1 9.7 copy-start.76
  732.1 11.7 copy-start.50
  732.1 11.7 copy-start.63
  749.9 896.1 %reduce-scatter.15.cloned.1.call-start = ((), (), s32[]{:S(2)}) async-start(), calls=%async_computation.21 | async-start | bytes 6758400 | tf_op jit(solution)/shard_map/reduce_scatter | solution.py:58
  878.4 922.2 %reduce-scatter.17.cloned.1.call-start = ((), (), s32[]{:S(2)}) async-start(), calls=%async_computation.22 | async-start | bytes 6758400 | tf_op jit(solution)/shard_map/reduce_scatter | solution.py:64
  901.9 50.4 %copy-start.80 = (bf16[80]{0:T(256)(128)(2,1)S(1)}, bf16[80]{0:T(256)(128)(2,1)}, u32[]{:S(2)}) copy-start(bf16[80]{0:T(256)(128)(2,1)} %param.47) | copy-start | bytes 484
  901.9 50.9 %copy-start.34 = (f32[128,1280]{1,0:T(8,128)S(1)}, f32[128,1280]{1,0:T(8,128)}, u32[]{:S(2)}) copy-start(f32[128,1280]{1,0:T(8,128)} %get-tuple-element.1310) | copy-start | bytes 1966084
  901.9 50.9 %copy-start.37 = (f32[128,1280]{1,0:T(8,128)S(1)}, f32[128,1280]{1,0:T(8,128)}, u32[]{:S(2)}) copy-start(f32[128,1280]{1,0:T(8,128)} %copy-done.35) | copy-start | bytes 1966084
  (69 other events, 179.5 us)
Sparse Core Ops, SparseCore 0:
  10.8 62.4 all-gather.16
  76.2 58.2 all-gather.14
  137.3 58.2 all-gather.18
  197.7 53.0 all-gather.32
  253.3 52.9 all-gather.30
  309.0 58.2 all-gather.20
  369.5 53.0 all-gather.26
  424.7 52.9 all-gather.28
  480.6 58.2 all-gather.22
  541.5 58.2 all-gather.24
  650.7 114.6 reduce-scatter.8
  768.9 102.6 reduce-scatter.10
  874.4 152.7 reduce-scatter.20
  1029.9 153.1 reduce-scatter.18
  1185.9 152.1 reduce-scatter.22
  1340.8 151.4 reduce-scatter.12
  1495.0 150.9 reduce-scatter.14
  1648.7 151.7 reduce-scatter.16
where the time goes:
time: 1820 us; the launch traced here: 1810 us
  waiting for transfers between devices  1450 us (80%)
  matrix products  143 us (8%)
  blocking collectives  87.6 us (5%)
  local copies, waits for them, and re-layouts  81.9 us (5%)
  other arithmetic  19.7 us (1%)
    reduce_scatter x1, waiting for transfers between devices, spread_each(): lax.psum_scatter(grads[6], ('dp', 'seq'), scatter_dimension=0, tiled=True)  156 us
    reduce_scatter x1, waiting for transfers between devices, spread_each(): lax.psum_scatter(grads[11], ('dp', 'seq'), scatter_dimension=0, tiled=True)  155 us
    reduce_scatter x1, waiting for transfers between devices, spread_each(): lax.psum_scatter(grads[4], ('dp', 'seq'), scatter_dimension=0, tiled=True)  155 us
    reduce_scatter x1, waiting for transfers between devices, spread_each(): lax.psum_scatter(grads[1], ('dp', 'seq'), scatter_dimension=0, tiled=True)  154 us
    reduce_scatter x1, waiting for transfers between devices, spread_each(): lax.psum_scatter(grads[3], ('dp', 'seq'), scatter_dimension=0, tiled=True)  154 us
    reduce_scatter x2, waiting for transfers between devices, backward(): lax.psum_scatter(pieces.reshape(count, seqs, 2 * width).astype(jnp.bfloat...  117 us
    all_gather x2, waiting for transfers between devices, forward(): lax.all_gather(values.reshape(tokens, seqs, width), 'seq', axis=0, tiled=...  104 us
    all_gather x2, waiting for transfers between devices, forward(): lax.all_gather(keys.reshape(tokens, seqs, width), 'seq', axis=0, tiled=True)  101 us
  transfers between devices with their start and end apart: 18, of which 18 were waited for; matrix products, arithmetic and copies ran while one was open for 10% of the time, Pallas kernels for 0%

commit v1 on v0

v1 whole, which is shorter than its diff:
```python
import functools
import itertools
import math

import jax
import jax.numpy as jnp
from jax import lax
from jax.experimental import pallas as pl
from jax.experimental.pallas import tpu as pltpu
from jax.sharding import PartitionSpec as P

HEADS = 16
HEAD_DIM = 80
ATT_BLOCK = 256
SOFT_BASE = 1.442695041
EPSILON = 1e-06
MESH = pl.DeviceIdType.MESH
VMEM_BYTES = 60 * 1024 * 1024


class Place:
    def __init__(self, dp, seq):
        self.cores = 2 if dp % 2 == 0 else 1
        self.lines = dp // self.cores
        self.levels = 4 if seq % 4 == 0 else seq
        self.across = seq // self.levels
        self.sizes = {
            "y": self.lines,
            "c": self.cores,
            "z": self.levels,
            "x": self.across,
        }

    def here(self):
        dp = lax.axis_index("dp")
        seq = lax.axis_index("seq")
        return {
            "y": dp // self.cores,
            "c": dp % self.cores,
            "z": seq // self.across,
            "x": seq % self.across,
        }

    def shift(self, spot, axis, step):
        moved = dict(spot)
        moved[axis] = lax.rem(spot[axis] + step, self.sizes[axis])
        return moved

    def device(self, spot):
        return (
            spot["y"] * self.cores + spot["c"],
            spot["z"] * self.across + spot["x"],
        )

    def grid(self):
        return (self.lines, self.cores, self.levels, self.across)

    def copies(self, halves):
        sizes = self.sizes
        return (sizes["z"] - 1) + halves * (sizes["x"] + sizes["y"] + sizes["c"] - 3)

    def greet(self, spot):
        barrier = pltpu.get_barrier_semaphore()
        count = 0
        for axis in "zxyc":
            for step in range(1, self.sizes[axis]):
                pl.semaphore_signal(
                    barrier,
                    inc=1,
                    device_id=self.device(self.shift(spot, axis, step)),
                    device_id_type=MESH,
                )
                count += 1
        pl.semaphore_wait(barrier, count)


def halves_of(cols):
    if cols % 256 == 0:
        return ((slice(0, cols // 2), "xy"), (slice(cols // 2, cols), "yx"))
    return ((slice(0, cols), "xy"),)


class Sender:
    def __init__(self, place, spot, send_sem, recv_sem):
        self.place = place
        self.spot = spot
        self.send_sem = send_sem
        self.recv_sem = recv_sem
        self.count = itertools.count()
        self.open = {}
        self.every = []

    def go(self, key, axis, source, target):
        made = []
        for step in range(1, self.place.sizes[axis]):
            at = next(self.count)
            peer = self.place.shift(self.spot, axis, step)
            copy = pltpu.make_async_remote_copy(
                src_ref=source(peer),
                dst_ref=target(step),
                send_sem=self.send_sem.at[at],
                recv_sem=self.recv_sem.at[at],
                device_id=self.place.device(peer),
                device_id_type=MESH,
            )
            copy.start()
            made.append(copy)
        self.open[key] = made
        self.every.extend(made)

    def landed(self, key):
        for copy in self.open[key]:
            copy.wait_recv()

    def finish(self):
        for copy in self.every:
            copy.wait_send()


def gather_kernel(place, count, *refs):
    shards, wholes = refs[:count], refs[count : 2 * count]
    own_sem, send_sem, recv_sem = refs[2 * count :]
    spot = place.here()
    y, c, z, x = (spot[k] for k in "yczx")
    own = []
    for n in range(count):
        copy = pltpu.make_async_copy(shards[n], wholes[n].at[y, c, z, x], own_sem.at[n])
        copy.start()
        own.append(copy)
    place.greet(spot)
    out = Sender(place, spot, send_sem, recv_sem)

    def one(n):
        part = wholes[n].at[y, c, z, x]
        out.go((n, "z"), "z", lambda peer: shards[n], lambda step: part)

    def two(n):
        out.landed((n, "z"))
        own[n].wait()
        for half, (cols, order) in enumerate(halves_of(shards[n].shape[-1])):
            part = wholes[n].at[y, c, :, x, :, cols]
            out.go((n, half, 2), order[0], lambda peer: part, lambda step: part)

    def three(n):
        for half, (cols, order) in enumerate(halves_of(shards[n].shape[-1])):
            out.landed((n, half, 2))
            if order == "xy":
                part = wholes[n].at[y, c, :, :, :, cols]
            else:
                part = wholes[n].at[:, c, :, x, :, cols]
            out.go((n, half, 3), order[1], lambda peer: part, lambda step: part)

    def four(n):
        for half, (cols, order) in enumerate(halves_of(shards[n].shape[-1])):
            out.landed((n, half, 3))
            part = wholes[n].at[:, c, :, :, :, cols]
            out.go((n, half, 4), "c", lambda peer: part, lambda step: part)

    def five(n):
        for half in range(len(halves_of(shards[n].shape[-1]))):
            out.landed((n, half, 4))

    ahead = 2
    for n in range(min(ahead, count)):
        one(n)
    for step in range(count + 3):
        if step < count:
            two(step)
        if step + ahead < count:
            one(step + ahead)
        for stage, late in ((three, 1), (four, 2), (five, 3)):
            if 0 <= step - late < count:
                stage(step - late)
    out.finish()


def gather_whole(place, shards, collective_id):
    count = len(shards)
    copies = sum(place.copies(len(halves_of(s.shape[-1]))) for s in shards)
    return pl.pallas_call(
        functools.partial(gather_kernel, place, count),
        out_shape=[jax.ShapeDtypeStruct(place.grid() + s.shape, s.dtype) for s in shards],
        in_specs=[pl.BlockSpec(memory_space=pl.ANY)] * count,
        out_specs=[pl.BlockSpec(memory_space=pl.ANY)] * count,
        scratch_shapes=[
            pltpu.SemaphoreType.DMA((count,)),
            pltpu.SemaphoreType.DMA((copies,)),
            pltpu.SemaphoreType.DMA((copies,)),
        ],
        compiler_params=pltpu.CompilerParams(
            collective_id=collective_id, has_side_effects=True
        ),
        name="gather_whole",
    )(*shards)


def scatter_kernel(place, count, *refs):
    parts, totals = refs[:count], refs[count : 2 * count]
    rest = list(refs[2 * count :])
    sums = [rest.pop(0) for _ in range(count)]
    cores = [rest.pop(0) for _ in range(count)]
    seconds, thirds, fourths = [], [], []
    for n in range(count):
        halves = halves_of(parts[n].shape[-1])
        seconds.append([rest.pop(0) for _ in halves])
        thirds.append([rest.pop(0) for _ in halves])
        fourths.append(rest.pop(0))
    own_sem, send_sem, recv_sem = rest
    spot = place.here()
    y, c, z, x = (spot[k] for k in "yczx")
    own = []
    for n in range(count):
        copy = pltpu.make_async_copy(parts[n].at[:, c], sums[n], own_sem.at[n])
        copy.start()
        own.append(copy)
    place.greet(spot)
    out = Sender(place, spot, send_sem, recv_sem)
    lines, _, levels, across = place.grid()

    def total(values):
        result = values[0].astype(jnp.float32)
        for value in values[1:]:
            result = result + value.astype(jnp.float32)
        return result

    def one(n):
        out.go(
            (n, 1), "c", lambda peer: parts[n].at[:, peer["c"]], lambda step: cores[n]
        )

    def two(n):
        own[n].wait()
        out.landed((n, 1))
        if place.cores > 1:

            @pl.loop(0, lines * levels * across)
            def _(at):
                where = (at // (levels * across), (at // across) % levels, at % across)
                sums[n][where] = total([sums[n][where], cores[n][where]]).astype(
                    sums[n].dtype
                )

        for half, (cols, order) in enumerate(halves_of(parts[n].shape[-1])):
            if order == "xy":
                out.go(
                    (n, half, 2),
                    "y",
                    lambda peer: sums[n].at[peer["y"], :, :, :, cols],
                    lambda step: seconds[n][half].at[step - 1],
                )
            else:
                out.go(
                    (n, half, 2),
                    "x",
                    lambda peer: sums[n].at[:, :, peer["x"], :, cols],
                    lambda step: seconds[n][half].at[step - 1],
                )

    def three(n):
        for half, (cols, order) in enumerate(halves_of(parts[n].shape[-1])):
            out.landed((n, half, 2))
            box = seconds[n][half]
            if order == "xy":

                @pl.loop(0, levels * across)
                def _(at):
                    zz, xx = at // across, at % across
                    values = [sums[n][y, zz, xx, :, cols]]
                    values += [box[k, zz, xx] for k in range(lines - 1)]
                    sums[n][y, zz, xx, :, cols] = total(values).astype(sums[n].dtype)

                out.go(
                    (n, half, 3),
                    "x",
                    lambda peer: sums[n].at[y, :, peer["x"], :, cols],
                    lambda step: thirds[n][half].at[step - 1],
                )
            else:

                @pl.loop(0, lines * levels)
                def _(at):
                    yy, zz = at // levels, at % levels
                    values = [sums[n][yy, zz, x, :, cols]]
                    values += [box[k, yy, zz] for k in range(across - 1)]
                    sums[n][yy, zz, x, :, cols] = total(values).astype(sums[n].dtype)

                out.go(
                    (n, half, 3),
                    "y",
                    lambda peer: sums[n].at[peer["y"], :, x, :, cols],
                    lambda step: thirds[n][half].at[step - 1],
                )

    def four(n):
        for half, (cols, order) in enumerate(halves_of(parts[n].shape[-1])):
            out.landed((n, half, 3))
            box = thirds[n][half]

            @pl.loop(0, levels)
            def _(zz):
                values = [sums[n][y, zz, x, :, cols]]
                values += [box[k, zz] for k in range(box.shape[0])]
                sums[n][y, zz, x, :, cols] = total(values).astype(sums[n].dtype)

        out.go(
            (n, 4),
            "z",
            lambda peer: sums[n].at[y, peer["z"], x],
            lambda step: fourths[n].at[step - 1],
        )

    def five(n):
        out.landed((n, 4))
        values = [sums[n][y, z, x]] + [fourths[n][k] for k in range(levels - 1)]
        totals[n][...] = total(values)

    for step in range(count + 4):
        for stage, late in ((one, 0), (two, 1), (three, 2), (four, 3), (five, 4)):
            if 0 <= step - late < count:
                stage(step - late)
    out.finish()


def scatter_sum(place, parts, collective_id):
    count = len(parts)
    lines, cores, levels, across = place.grid()
    boxes = []
    copies = 0
    for p in parts:
        rows, cols = p.shape[-2:]
        halves = halves_of(cols)
        copies += (levels - 1) + (cores - 1) + len(halves) * (lines + across - 2)
        for piece, order in halves:
            wide = piece.stop - piece.start
            first = (lines - 1, levels, across) if order == "xy" else (across - 1, lines, levels)
            later = (across - 1, levels) if order == "xy" else (lines - 1, levels)
            boxes.append(pltpu.VMEM(first + (rows, wide), p.dtype))
            boxes.append(pltpu.VMEM(later + (rows, wide), p.dtype))
        if len(halves) == 2:
            boxes[-3], boxes[-2] = boxes[-2], boxes[-3]
        boxes.append(pltpu.VMEM((levels - 1, rows, cols), p.dtype))
    block = [pltpu.VMEM((lines, levels, across) + p.shape[-2:], p.dtype) for p in parts]
    return pl.pallas_call(
        functools.partial(scatter_kernel, place, count),
        out_shape=[jax.ShapeDtypeStruct(p.shape[-2:], jnp.float32) for p in parts],
        in_specs=[pl.BlockSpec(memory_space=pl.ANY)] * count,
        out_specs=[pl.BlockSpec(memory_space=pltpu.VMEM)] * count,
        scratch_shapes=block
        + block
        + boxes
        + [
            pltpu.SemaphoreType.DMA((count,)),
            pltpu.SemaphoreType.DMA((copies,)),
            pltpu.SemaphoreType.DMA((copies,)),
        ],
        compiler_params=pltpu.CompilerParams(
            collective_id=collective_id,
            has_side_effects=True,
            vmem_limit_bytes=VMEM_BYTES,
        ),
        name="scatter_sum",
    )(*parts)


def swap_kernel(devices, count, *refs):
    sent, got = refs[:count], refs[count : 2 * count]
    own_sem, send_sem, recv_sem = refs[2 * count :]
    dp, me = lax.axis_index("dp"), lax.axis_index("seq")
    own = []
    for n in range(count):
        copy = pltpu.make_async_copy(sent[n].at[me], got[n].at[me], own_sem.at[n])
        copy.start()
        own.append(copy)
    barrier = pltpu.get_barrier_semaphore()
    for step in range(1, devices):
        pl.semaphore_signal(
            barrier,
            inc=1,
            device_id=(dp, lax.rem(me + step, devices)),
            device_id_type=MESH,
        )
    pl.semaphore_wait(barrier, devices - 1)
    copies = []
    for n in range(count):
        for step in range(1, devices):
            peer = lax.rem(me + step, devices)
            copy = pltpu.make_async_remote_copy(
                src_ref=sent[n].at[peer],
                dst_ref=got[n].at[me],
                send_sem=send_sem.at[n, step - 1],
                recv_sem=recv_sem.at[n, step - 1],
                device_id=(dp, peer),
                device_id_type=MESH,
            )
            copy.start()
            copies.append(copy)
    for copy in own:
        copy.wait()
    for copy in copies:
        copy.wait()


def swap_heads(arrays, devices, collective_id):
    count = len(arrays)
    return pl.pallas_call(
        functools.partial(swap_kernel, devices, count),
        out_shape=[jax.ShapeDtypeStruct(a.shape, a.dtype) for a in arrays],
        in_specs=[pl.BlockSpec(memory_space=pl.ANY)] * count,
        out_specs=[pl.BlockSpec(memory_space=pl.ANY)] * count,
        scratch_shapes=[
            pltpu.SemaphoreType.DMA((count,)),
            pltpu.SemaphoreType.DMA((count, devices - 1)),
            pltpu.SemaphoreType.DMA((count, devices - 1)),
        ],
        compiler_params=pltpu.CompilerParams(
            collective_id=collective_id, has_side_effects=True
        ),
        name="swap_heads",
    )(*arrays)


def side_by_side(ref):
    return jnp.concatenate([ref[s] for s in range(ref.shape[0])], axis=1)


def dot_first(left, right):
    return lax.dot_general(
        left, right, (((0,), (0,)), ((), ())), preferred_element_type=jnp.float32
    )


def dot_last(left, right):
    return lax.dot_general(
        left, right, (((1,), (1,)), ((), ())), preferred_element_type=jnp.float32
    )


def attend_kernel(q_ref, k_ref, v_ref, o_ref, full_ref, sum_ref):
    tokens = q_ref.shape[-1]
    each = ATT_BLOCK // tokens
    keys, values = side_by_side(k_ref), side_by_side(v_ref)
    for block in range(q_ref.shape[0] // each):
        first = block * each
        limit = (block + 1) * ATT_BLOCK
        queries = jnp.concatenate([q_ref[first + s] for s in range(each)], axis=1)
        weights = jnp.exp(dot_first(keys[:, :limit], queries))
        sums = jnp.sum(weights, axis=0, keepdims=True)
        mixed = jnp.dot(
            values[:, :limit],
            weights.astype(jnp.bfloat16),
            preferred_element_type=jnp.float32,
        )
        mixed = mixed / sums
        sum_ref[0, 0, :, pl.ds(block * ATT_BLOCK, ATT_BLOCK)] = sums
        for s in range(each):
            piece = mixed[:, s * tokens : (s + 1) * tokens]
            full_ref[first + s] = piece
            o_ref[first + s] = piece.astype(jnp.bfloat16)


def attend_specs(devices, tokens):
    piece = pl.BlockSpec((devices, HEAD_DIM, tokens), lambda m, h: (0, h, m))
    sums = pl.BlockSpec((1, 1, 1, devices * tokens), lambda m, h: (m, h, 0, 0))
    return piece, sums


def attend(queries, keys, values, tokens):
    devices, rows, cols = queries.shape
    grid = (cols // tokens, rows // HEAD_DIM)
    piece, sums = attend_specs(devices, tokens)
    return pl.pallas_call(
        attend_kernel,
        grid=grid,
        out_shape=[
            jax.ShapeDtypeStruct(queries.shape, jnp.bfloat16),
            jax.ShapeDtypeStruct(queries.shape, jnp.float32),
            jax.ShapeDtypeStruct(grid + (1, devices * tokens), jnp.float32),
        ],
        in_specs=[piece] * 3,
        out_specs=[piece, piece, sums],
        compiler_params=pltpu.CompilerParams(vmem_limit_bytes=VMEM_BYTES),
        name="attend",
    )(queries, keys, values)


def slopes_kernel(
    q_ref, k_ref, v_ref, do_ref, full_ref, sum_ref, rate_ref, dq_ref, dk_ref, dv_ref
):
    tokens = q_ref.shape[-1]
    each = ATT_BLOCK // tokens
    keys, values = side_by_side(k_ref), side_by_side(v_ref)
    rate = rate_ref[...]
    key_total = value_total = None
    for block in reversed(range(q_ref.shape[0] // each)):
        first = block * each
        limit = (block + 1) * ATT_BLOCK

        def pick(ref):
            return jnp.concatenate([ref[first + s] for s in range(each)], axis=1)

        queries = pick(q_ref)
        slope = pick(do_ref).astype(jnp.float32)
        sums = sum_ref[0, 0, :, pl.ds(block * ATT_BLOCK, ATT_BLOCK)]
        scaled = (slope / sums).astype(jnp.bfloat16)
        centre = jnp.sum(slope * pick(full_ref), axis=0, keepdims=True) / sums
        weights = jnp.exp(dot_first(keys[:, :limit], queries))
        dots = dot_first(values[:, :limit], scaled)
        slopes = (weights * (dots - centre)).astype(jnp.bfloat16)
        weights = weights.astype(jnp.bfloat16)
        query_part = jnp.dot(keys[:, :limit], slopes, preferred_element_type=jnp.float32)
        query_part = (query_part * rate).astype(jnp.bfloat16)
        for s in range(each):
            dq_ref[first + s] = query_part[:, s * tokens : (s + 1) * tokens]
        key_part = dot_last(queries, slopes)
        value_part = dot_last(scaled, weights)
        if key_total is None:
            key_total, value_total = key_part, value_part
        else:
            key_total = jnp.concatenate(
                [key_total[:, :limit] + key_part, key_total[:, limit:]], axis=1
            )
            value_total = jnp.concatenate(
                [value_total[:, :limit] + value_part, value_total[:, limit:]], axis=1
            )
    for s in range(q_ref.shape[0]):
        cols = slice(s * tokens, (s + 1) * tokens)
        dk_ref[s] = key_total[:, cols].astype(jnp.bfloat16)
        dv_ref[s] = value_total[:, cols].astype(jnp.bfloat16)


def slopes(queries, keys, values, slope, full, sums, rate, tokens):
    devices, rows, cols = queries.shape
    grid = (cols // tokens, rows // HEAD_DIM)
    piece, sum_spec = attend_specs(devices, tokens)
    return pl.pallas_call(
        slopes_kernel,
        grid=grid,
        out_shape=[jax.ShapeDtypeStruct(queries.shape, jnp.bfloat16)] * 3,
        in_specs=[piece] * 5
        + [sum_spec, pl.BlockSpec((HEAD_DIM, 1), lambda m, h: (0, 0))],
        out_specs=[piece] * 3,
        compiler_params=pltpu.CompilerParams(vmem_limit_bytes=VMEM_BYTES),
        name="slopes",
    )(queries, keys, values, slope, full, sums, rate)


def rms_scale(values):
    return lax.rsqrt(jnp.mean(values * values, axis=-1, keepdims=True) + EPSILON)


def contract(spec, left, right):
    return jnp.einsum(spec, left, right, preferred_element_type=jnp.float32)


def on_device(place, devices, *args):
    inputs, cotangent = args[:2]
    (
        norm_one,
        query_mat,
        query_add,
        key_mat,
        value_mat,
        value_add,
        output_mat,
        output_add,
        norm_two,
        hidden_mat,
        hidden_add,
        project_mat,
        project_add,
    ) = args[2:15]
    depth = args[15].astype(jnp.float32)
    micro, tokens, seqs, width = inputs.shape
    rows = micro * tokens * seqs
    vectors = (norm_one, query_add, value_add, output_add, norm_two, hidden_add, project_add)
    share = norm_one.shape[0]
    small = jnp.pad(jnp.stack(vectors), ((0, 16 - len(vectors)), (0, 128 - share)))
    mats = (query_mat, key_mat, value_mat, output_mat, hidden_mat, project_mat)
    gathered = gather_whole(place, (small,) + mats, 0)
    small = gathered[0].reshape(-1, 16, 128)[:, : len(vectors), :share]
    small = small.transpose(1, 0, 2).reshape(len(vectors), width).astype(jnp.float32)
    gain_one, query_add, value_add, output_add, gain_two, hidden_add, project_add = small
    query_mat, key_mat, value_mat, output_mat, hidden_mat, project_mat = (
        g.reshape(width, width) for g in gathered[1:]
    )

    def to_rows(array):
        return array.transpose(0, 2, 1, 3).reshape(rows, width)

    def from_rows(array):
        return array.reshape(micro, seqs, tokens, width).transpose(0, 2, 1, 3)

    rate = SOFT_BASE / math.sqrt(HEAD_DIM) * jax.nn.softplus(depth)
    rate_full = jnp.tile(rate, HEADS)[:, None]
    xfloat = to_rows(inputs).astype(jnp.float32)
    inv_one = rms_scale(xfloat)
    normed = (xfloat * inv_one * gain_one).astype(jnp.bfloat16)
    query_pre = contract("df,rd->fr", query_mat, normed) + query_add[:, None]
    queries = (query_pre * rate_full).astype(jnp.bfloat16)
    keys = contract("df,rd->fr", key_mat, normed).astype(jnp.bfloat16)
    values = (contract("df,rd->fr", value_mat, normed) + value_add[:, None]).astype(jnp.bfloat16)

    def split(array):
        return array.reshape(devices, width // devices, rows)

    q_in, k_in, v_in = swap_heads([split(queries), split(keys), split(values)], devices, 1)
    mixed, full, sums = attend(q_in, k_in, v_in, tokens)
    (mixed,) = swap_heads([mixed], devices, 2)
    mixed = mixed.reshape(width, rows)
    residual = xfloat + (contract("fr,fd->rd", mixed, output_mat) + output_add)
    inv_two = rms_scale(residual)
    second = (residual * inv_two * gain_two).astype(jnp.bfloat16)
    hidden_pre = contract("rd,df->rf", second, hidden_mat) + hidden_add
    active = jax.nn.silu(hidden_pre).astype(jnp.bfloat16)
    result = residual + (contract("rf,fd->rd", active, project_mat) + project_add)
    result = from_rows(result.astype(jnp.bfloat16))

    upper = to_rows(cotangent)
    project_grad = contract("rf,rd->fd", active, upper)
    project_bias_grad = jnp.sum(upper.astype(jnp.float32), axis=0)
    active_grad = contract("rd,fd->rf", upper, project_mat)
    logistic = jax.nn.sigmoid(hidden_pre)
    hidden_grad = (active_grad * logistic * (1.0 + hidden_pre * (1.0 - logistic))).astype(
        jnp.bfloat16
    )
    hidden_mat_grad = contract("rd,rf->df", second, hidden_grad)
    hidden_bias_grad = jnp.sum(hidden_grad.astype(jnp.float32), axis=0)
    second_grad = contract("rf,df->rd", hidden_grad, hidden_mat)
    normal_two = residual * inv_two
    scaled_two = second_grad * gain_two
    norm_two_grad = jnp.sum(second_grad * normal_two, axis=0)
    residual_grad = upper.astype(jnp.float32) + inv_two * (
        scaled_two - normal_two * jnp.mean(scaled_two * normal_two, axis=-1, keepdims=True)
    )
    branch_grad = residual_grad.astype(jnp.bfloat16)
    output_mat_grad = contract("fr,rd->fd", mixed, branch_grad)
    output_bias_grad = jnp.sum(branch_grad.astype(jnp.float32), axis=0)
    mixed_grad = contract("fd,rd->fr", output_mat, branch_grad).astype(jnp.bfloat16)

    (do_in,) = swap_heads([split(mixed_grad)], devices, 3)
    slopes_out = slopes(q_in, k_in, v_in, do_in, full, sums, rate[:, None], tokens)
    query_slope, key_grad, value_grad = (
        a.reshape(width, rows) for a in swap_heads(slopes_out, devices, 4)
    )
    query_float = query_slope.astype(jnp.float32)
    scale_part = jnp.sum(query_float / rate_full * query_pre, axis=1)
    scale_part = jnp.sum(scale_part.reshape(HEADS, HEAD_DIM), axis=0)
    query_mat_grad = contract("rd,fr->df", normed, query_slope)
    query_bias_grad = jnp.sum(query_float, axis=1)
    key_mat_grad = contract("rd,fr->df", normed, key_grad)
    value_mat_grad = contract("rd,fr->df", normed, value_grad)
    value_bias_grad = jnp.sum(value_grad.astype(jnp.float32), axis=1)
    normed_grad = (
        contract("fr,df->rd", query_slope, query_mat)
        + contract("fr,df->rd", key_grad, key_mat)
        + contract("fr,df->rd", value_grad, value_mat)
    )
    normal_one = xfloat * inv_one
    scaled_one = normed_grad * gain_one
    norm_one_grad = jnp.sum(normed_grad * normal_one, axis=0)
    source_grad = residual_grad + inv_one * (
        scaled_one - normal_one * jnp.mean(scaled_one * normal_one, axis=-1, keepdims=True)
    )
    source_grad = from_rows(source_grad.astype(jnp.bfloat16))

    vector_grads = jnp.stack(
        (
            norm_one_grad,
            query_bias_grad,
            value_bias_grad,
            output_bias_grad,
            norm_two_grad,
            hidden_bias_grad,
            project_bias_grad,
        )
    )
    vector_grads = vector_grads.reshape(7, -1, share).transpose(1, 0, 2)
    vector_grads = jnp.pad(vector_grads, ((0, 0), (0, 0), (0, 128 - share)))
    scale_row = jnp.pad(scale_part, (0, 128 - HEAD_DIM))
    scale_row = jnp.broadcast_to(scale_row, (vector_grads.shape[0], 1, 128))
    vector_grads = jnp.concatenate([vector_grads, scale_row], axis=1)
    vector_grads = vector_grads.reshape(place.grid() + (8, 128))
    mat_grads = (
        project_grad,
        hidden_mat_grad,
        output_mat_grad,
        query_mat_grad,
        key_mat_grad,
        value_mat_grad,
    )
    parts = [
        g.astype(jnp.bfloat16).reshape(place.grid() + (share, width)) for g in mat_grads
    ]
    if share % 8 == 0:
        summed = scatter_sum(place, parts + [vector_grads], 5)
        shares, vector_sums = summed[:-1], summed[-1]
    else:
        (vector_sums,) = scatter_sum(place, [vector_grads], 5)
        shares = [scatter_sum(place, [p], 6)[0] for p in parts]
    project_grad, hidden_mat_grad, output_mat_grad = shares[:3]
    query_mat_grad, key_mat_grad, value_mat_grad = shares[3:]
    g_one, g_query, g_value, g_output, g_two, g_hidden, g_project = (
        vector_sums[n, :share] for n in range(7)
    )
    scale_summed = vector_sums[7, :HEAD_DIM]
    depth_grad = scale_summed * (SOFT_BASE / math.sqrt(HEAD_DIM)) * jax.nn.sigmoid(depth)
    return (
        result,
        source_grad,
        g_one,
        query_mat_grad,
        g_query,
        key_mat_grad,
        value_mat_grad,
        g_value,
        output_mat_grad,
        g_output,
        g_two,
        hidden_mat_grad,
        g_hidden,
        project_grad,
        g_project,
        depth_grad,
    )


def solution(mesh):
    both = ("dp", "seq")
    token, vector, matrix = P(None, "seq", "dp", None), P(both), P(both, None)
    weights = (
        vector,
        matrix,
        vector,
        matrix,
        matrix,
        vector,
        matrix,
        vector,
        vector,
        matrix,
        vector,
        matrix,
        vector,
    )
    specs = (token, token) + weights + (P(),)
    place = Place(mesh.shape["dp"], mesh.shape["seq"])
    return jax.shard_map(
        functools.partial(on_device, place, mesh.shape["seq"]),
        mesh=mesh,
        in_specs=specs,
        out_specs=specs,
        check_vma=False,
    )
```

time: 1820 us -> 431 us (0.24)
  waiting for transfers between devices: 1450 us -> 0 us
  Pallas kernels: 0 us -> 359 us
  matrix products: 143 us -> 46.2 us
  blocking collectives: 87.6 us -> 0 us
  local copies, waits for them, and re-layouts: 81.9 us -> 14.7 us
    reduce_scatter x8 -> x0, waiting for transfers between devices: 963 us -> none  [the longest x1 156 us: spread_each(): lax.psum_scatter(grads[6], ('dp', 'seq'), scatter_dimension=0, tiled=True)]
    all_gather x10 -> x0, waiting for transfers between devices: 478 us -> none  [the longest x2 104 us: forward(): lax.all_gather(values.reshape(tokens, seqs, width), 'seq', axis=0, tiled=...]
    pallas_call x0 -> x8, Pallas kernels: none -> 359 us  [the longest x4 130 us: swap_heads(): pl.pallas_call(functools.partial(swap_kernel, devices, count), out_shape=...]
    dot_general x50 -> x18, matrix products: 143 us -> 46.2 us  [contract(): return jnp.einsum(spec, left, right, preferred_element_type=jnp.float32)]
    unnamed x2 -> x0, blocking collectives: 87.6 us -> none
    dynamic_update_slice x8 -> x0, local copies, waits for them, and re-layouts: 25.3 us -> none  [backward(): pieces = lax.map(one_piece, jnp.arange(count // piece, dtype=jnp.int32))]
  transfers between devices with their start and end apart: 18 -> 0, of which waited for: 18 -> 0; matrix products, arithmetic and copies ran while one was open for 10% -> 0% of each run, Pallas kernels for 0% -> 0%
where the time goes in v1:
time: 431 us
  Pallas kernels  359 us (83%)
  matrix products  46.2 us (11%)
  local copies, waits for them, and re-layouts  14.7 us (3%)
  other arithmetic  9.6 us (2%)
    pallas_call x4, Pallas kernels, swap_heads(): pl.pallas_call(functools.partial(swap_kernel, devices, count), out_shape=...  130 us
    pallas_call x1, Pallas kernels, scatter_sum(): pl.pallas_call(functools.partial(scatter_kernel, place, count), out_shape...  106 us
    pallas_call x1, Pallas kernels, gather_whole(): pl.pallas_call(functools.partial(gather_kernel, place, count), out_shape=...  105 us
    dot_general x18, matrix products, contract(): return jnp.einsum(spec, left, right, preferred_element_type=jnp.float32)  46.2 us
    pallas_call x1, Pallas kernels, slopes(): pl.pallas_call(slopes_kernel, grid=grid, out_shape=[jax.ShapeDtypeStruct(...  10.9 us
    unnamed x52, local copies, waits for them, and re-layouts  9.13 us

profile of v1, /device:TPU:0, one launch (start us, length us, event | category | flops | bytes accessed | tf_op | source)
XLA Modules:
  0.0 430.8 jit_solution(8260288327431350804)
XLA Ops:
  2.1 105.3 %gather_whole.1 = (bf16[2,2,4,2,16,128]{5,4,3,2,1,0:T(8,128)(2,1)}, bf16[2,2,4,2,40,1280]{5,4,3,2,1,0:T(8,128)(2,1)}, bf16[2,2,4,2,40,1280]{5,4,3,2,1,0:T(8,128)...) custom-call(bf16[16,128]{1,0:T(8,128)(2,1)} %pad.12.refs_0_, ...), custom_call_target="tpu_custom_call" | custom-call | tf_op jit(solution)/shard_map/gather_whole/pallas_call | solution.py:180
  110.1 4.6 %multiply_convert_fusion.2 = (bf16[1280,256]{1,0:T(8,128)(2,1)}, f32[1280,256]{1,0:T(8,128)}) fusion(f32[1280]{0:T(1024)S(1)} %mul.163, f32[1280]{0:T(1024)S(1)} %add.108, bf16[1280,1280]{1,0:T(8,128)(2,1)} %bitcast.152, bf16[256,1280]{1,0:T(8,128)(2,1)S(1)} %bitcast.110), kind=kOutput, calls=%fused_computation.40 | convolution fusion | flops 839843840 | bytes 5908480 | tf_op jit(solution)/shard_map/df,rd->fr/dot_general | solution.py:552
  114.7 1.9 convolution_convert_fusion.7
  116.7 3.9 fusion.5
  120.6 47.4 %swap_heads.4 = (bf16[8,160,256]{2,1,0:T(8,128)(2,1)}, bf16[8,160,256]{2,1,0:T(8,128)(2,1)}, bf16[8,160,256]{2,1,0:T(8,128)(2,1)}) custom-call(bf16[8,160,256]{2,1,0:T(8,128)(2,1)} %bitcast.137, bf16[8,160,256]{2,1,0:T(8,128)(2,1)} %bitcast.138, bf16[8,160,256]{2,1,0:T(8,128)(2,1)} %bitcast.139), custom_call_target="tpu_custom_call" | custom-call | tf_op jit(solution)/shard_map/swap_heads/pallas_call | solution.py:405
  168.0 7.2 %attend.1 = (bf16[8,160,256]{2,1,0:T(8,128)(2,1)}, f32[8,160,256]{2,1,0:T(8,128)}, f32[2,2,1,1024]{3,2,1,0:T(1,128)}) custom-call(bf16[8,160,256]{2,1,0:T(8,128)(2,1)} %get-tuple-element.46.q_ref, bf16[8,160,256]{2,1,0:T(8,128)(2,1)} %get-tuple-element.47.k_ref, bf16[8,160,256]{2,1,0:T(8,128)(2,1)} %get-tuple-element.48.v_ref), custom_call_target="tpu_custom_call" | custom-call | tf_op jit(solution)/shard_map/attend/pallas_call | solution.py:471
  175.3 18.6 %swap_heads.5 = bf16[8,160,256]{2,1,0:T(8,128)(2,1)} custom-call(bf16[8,160,256]{2,1,0:T(8,128)(2,1)} %get-tuple-element.49.refs_0_), custom_call_target="tpu_custom_call" | custom-call | tf_op jit(solution)/shard_map/swap_heads/pallas_call | solution.py:405
  193.9 3.3 multiply_reduce_fusion.5
  197.5 3.3 convolution_add_fusion.3
  200.8 2.0 fusion.6
  202.9 1.2 convert_reduce_fusion.1
  204.8 1.3 multiply_reduce_fusion.1
  206.1 1.9 convert_reduce_fusion.2
  208.4 1.9 convolution_convert_fusion.6
  210.3 18.3 %swap_heads.6.do_ref = bf16[8,160,256]{2,1,0:T(8,128)(2,1)} custom-call(bf16[8,160,256]{2,1,0:T(8,128)(2,1)} %bitcast.136), custom_call_target="tpu_custom_call" | custom-call | tf_op jit(solution)/shard_map/swap_heads/pallas_call | solution.py:405
  229.4 10.9 %slopes.1 = (bf16[8,160,256]{2,1,0:T(8,128)(2,1)}, bf16[8,160,256]{2,1,0:T(8,128)(2,1)}, bf16[8,160,256]{2,1,0:T(8,128)(2,1)}) custom-call(bf16[8,160,256]{2,1,0:T(8,128)(2,1)} %get-tuple-element.46.q_ref, bf16[8,160,256]{2,1,0:T(8,128)(2,1)} %get-tuple-element.47.k_ref, bf16[8,160,256]{2,1,0:T(8,128)(2,1)} %get-tuple-element.48.v_ref, ...), custom_call_target="tpu_custom_call" | custom-call | tf_op jit(solution)/shard_map/slopes/pallas_call | solution.py:535
  240.2 45.2 %swap_heads.7 = (bf16[8,160,256]{2,1,0:T(8,128)(2,1)}, bf16[8,160,256]{2,1,0:T(8,128)(2,1)}, bf16[8,160,256]{2,1,0:T(8,128)(2,1)}) custom-call(bf16[8,160,256]{2,1,0:T(8,128)(2,1)} %get-tuple-element.55.refs_0_, bf16[8,160,256]{2,1,0:T(8,128)(2,1)} %get-tuple-element.56.refs_1_, bf16[8,160,256]{2,1,0:T(8,128)(2,1)} %get-tuple-element.57.refs_2_), custom_call_target="tpu_custom_call" | custom-call | tf_op jit(solution)/shard_map/swap_heads/pallas_call | solution.py:405
  285.5 3.3 fusion.11
  291.0 1.4 multiply_reduce_fusion.2
  292.4 1.3 add_convert_fusion
  293.7 3.0 convolution_convert_fusion.5
  296.7 2.9 convolution_convert_fusion.4
  299.6 2.8 convolution_convert_fusion.3
  302.4 2.8 convolution_convert_fusion.2
  305.2 2.7 convolution_convert_fusion.1
  307.9 2.8 convolution_convert_fusion
  312.3 1.8 multiply_reduce_fusion
  314.9 106.3 %scatter_sum.1 = (f32[40,1280]{1,0:T(8,128)}, f32[40,1280]{1,0:T(8,128)}, f32[40,1280]{1,0:T(8,128)}, f32[40,1280]{1,0:T(8,128)}, f32[40,1280]{1,0:T(8,128)}, /*index=5*/f32[40,1280]{1,0:T(8,128)}, f32[8,128]{1,0:T(8,128)}) custom-call(bf16[2,2,4,2,40,1280]{5,4,3,2,1,0:T(8,128)(2,1)} %bitcast.126, bf16[2,2,4,2,40,1280]{5,4,3,2,1,0:T(8,128)(2,1)} %bitcast.120, ...), custom_call_target="tpu_custom_call" | custom-call | tf_op jit(solution)/shard_map/scatter_sum/pallas_call | solution.py:343
  421.2 1.5 slice_bitcast_fusion
  423.9 1.6 copy.44
  425.5 1.6 copy.45
  427.1 1.6 copy.46
  (88 shorter events, 14.0 us)
Async XLA Ops:
  0.6 109.0 %copy-start = (bf16[2,128,1,1280]{3,1,2,0:T(8,128)(2,1)S(1)}, bf16[2,128,1,1280]{3,1,2,0:T(8,128)(2,1)}, u32[]{:S(2)}) copy-start(bf16[2,128,1,1280]{3,1,2,0:T(8,128)(2,1)} %param.16) | copy-start | bytes 1966084
  110.1 4.6 %copy-start.5 = (bf16[2,2,4,2,40,1280]{5,4,3,2,1,0:T(8,128)(2,1)S(1)}, bf16[2,2,4,2,40,1280]{5,4,3,2,1,0:T(8,128)(2,1)}, u32[]{:S(2)}) copy-start(bf16[2,2,4,2,40,1280]{5,4,3,2,1,0:T(8,128)(2,1)} %get-tuple-element.44) | copy-start | bytes 9830404
  197.2 6.9 %copy-start.2 = (f32[256,1280]{1,0:T(8,128)}, f32[256,1280]{1,0:T(8,128)S(1)}, u32[]{:S(2)}) copy-start(f32[256,1280]{1,0:T(8,128)S(1)} %get-tuple-element.125) | copy-start | bytes 3932164
  197.5 3.3 copy-start.19
  200.8 2.1 copy-start.21
  200.8 2.1 copy-start.8
  202.9 1.9 copy-start.18
  204.1 2.0 copy-start.11
  206.1 2.3 copy-start.17
  210.3 18.3 %copy-start.20 = (bf16[80]{0:T(256)(128)(2,1)S(1)}, bf16[80]{0:T(256)(128)(2,1)}, u32[]{:S(2)}) copy-start(bf16[80]{0:T(256)(128)(2,1)} %param.31) | copy-start | bytes 484
  285.5 3.4 copy-start.6
  285.5 3.4 copy-start.7
  288.9 1.1 copy-start.9
  288.9 2.1 copy-start.16
  292.4 1.3 copy-start.22
  293.7 3.0 copy-start.3
  293.7 3.0 copy-start.12
  296.7 2.9 copy-start.4
  299.6 2.8 copy-start.1
  307.9 2.9 copy-start.10
  421.2 7.6 %copy-start.15 = (f32[40,1280]{1,0:T(8,128)S(1)}, f32[40,1280]{1,0:T(8,128)}, u32[]{:S(2)}) copy-start(f32[40,1280]{1,0:T(8,128)} %get-tuple-element.156) | copy-start | bytes 614404
  421.2 8.3 %copy-start.14 = (f32[40,1280]{1,0:T(8,128)S(1)}, f32[40,1280]{1,0:T(8,128)}, u32[]{:S(2)}) copy-start(f32[40,1280]{1,0:T(8,128)} %get-tuple-element.159) | copy-start | bytes 614404
  421.2 8.9 %copy-start.13 = (f32[40,1280]{1,0:T(8,128)S(1)}, f32[40,1280]{1,0:T(8,128)}, u32[]{:S(2)}) copy-start(f32[40,1280]{1,0:T(8,128)} %get-tuple-element.161) | copy-start | bytes 614404

commit v2 on v1

v2 whole, which is shorter than its diff:
```python
import functools
import itertools
import math

import jax
import jax.numpy as jnp
from jax import lax
from jax.experimental import pallas as pl
from jax.experimental.pallas import tpu as pltpu
from jax.sharding import PartitionSpec as P

HEADS = 16
HEAD_DIM = 80
ATT_BLOCK = 256
SOFT_BASE = 1.442695041
EPSILON = 1e-06
MESH = pl.DeviceIdType.MESH
VMEM_BYTES = 60 * 1024 * 1024


class Place:
    def __init__(self, dp, seq):
        self.cores = 2 if dp % 2 == 0 else 1
        self.lines = dp // self.cores
        self.levels = 4 if seq % 4 == 0 else seq
        self.across = seq // self.levels
        self.sizes = {
            "y": self.lines,
            "c": self.cores,
            "z": self.levels,
            "x": self.across,
        }

    def here(self):
        dp = lax.axis_index("dp")
        seq = lax.axis_index("seq")
        return {
            "y": dp // self.cores,
            "c": dp % self.cores,
            "z": seq // self.across,
            "x": seq % self.across,
        }

    def shift(self, spot, axis, step):
        moved = dict(spot)
        moved[axis] = lax.rem(spot[axis] + step, self.sizes[axis])
        return moved

    def device(self, spot):
        return (
            spot["y"] * self.cores + spot["c"],
            spot["z"] * self.across + spot["x"],
        )

    def grid(self):
        return (self.lines, self.cores, self.levels, self.across)

    def greet(self, spot, wide):
        barrier = pltpu.get_barrier_semaphore()
        dp, seq = self.device(spot)
        peers = [
            self.device(self.shift(spot, axis, step))
            for axis in ("yc" if wide else "zxyc")
            for step in range(1, self.sizes[axis])
        ]
        if wide:
            devices = self.levels * self.across
            peers += [(dp, lax.rem(seq + step, devices)) for step in range(1, devices)]
        for peer in peers:
            pl.semaphore_signal(barrier, inc=1, device_id=peer, device_id_type=MESH)
        pl.semaphore_wait(barrier, len(peers))


def halves_of(cols, lean):
    if lean and cols % 640 == 0:
        cut = cols * 4 // 5
    elif cols % 256 == 0:
        cut = cols // 2
    else:
        return ((slice(0, cols), "xy"),)
    return ((slice(0, cut), "xy"), (slice(cut, cols), "yx"))


def chunks_of(rows):
    if rows % 8 == 0 and rows >= 32:
        cut = rows // 32 * 16
        return (slice(0, cut), slice(cut, rows))
    return (slice(0, rows),)


class Sender:
    def __init__(self, place, spot, send_sem, recv_sem):
        self.place = place
        self.spot = spot
        self.send_sem = send_sem
        self.recv_sem = recv_sem
        self.count = itertools.count()
        self.open = {}
        self.every = []

    def put(self, key, device, source, target):
        at = next(self.count)
        copy = pltpu.make_async_remote_copy(
            src_ref=source,
            dst_ref=target,
            send_sem=self.send_sem.at[at],
            recv_sem=self.recv_sem.at[at],
            device_id=device,
            device_id_type=MESH,
        )
        copy.start()
        self.open.setdefault(key, []).append(copy)
        self.every.append(copy)

    def go(self, key, axis, source, target):
        self.open[key] = []
        for step in range(1, self.place.sizes[axis]):
            peer = self.place.shift(self.spot, axis, step)
            self.put(key, self.place.device(peer), source(peer), target(step))

    def landed(self, key):
        for copy in self.open[key]:
            copy.wait_recv()

    def finish(self):
        for copy in self.every:
            copy.wait_send()


class Gather:
    def __init__(self, place, spot, lean, shards, wholes, own_sem):
        self.place, self.spot, self.lean = place, spot, lean
        self.shards, self.wholes = shards, wholes
        self.jobs = [(n, r) for n, s in enumerate(shards) for r in chunks_of(s.shape[0])]
        y, c, z, x = (spot[k] for k in "yczx")
        self.own = []
        for n, shard in enumerate(shards):
            copy = pltpu.make_async_copy(shard, wholes[n].at[y, c, z, x], own_sem[n])
            copy.start()
            self.own.append(copy)

    def run(self, out):
        shards, wholes = self.shards, self.wholes
        y, c, z, x = (self.spot[k] for k in "yczx")
        filled = set()

        def halves(n):
            return enumerate(halves_of(shards[n].shape[-1], self.lean))

        def one(job, n, rows):
            part = wholes[n].at[y, c, z, x, rows]
            out.go((job, "z"), "z", lambda peer: shards[n].at[rows], lambda step: part)

        def two(job, n, rows):
            out.landed((job, "z"))
            if n not in filled:
                filled.add(n)
                self.own[n].wait()
            for half, (cols, order) in halves(n):
                part = wholes[n].at[y, c, :, x, rows, cols]
                out.go((job, half, 2), order[0], lambda peer: part, lambda step: part)

        def three(job, n, rows):
            for half, (cols, order) in halves(n):
                out.landed((job, half, 2))
                if order == "xy":
                    part = wholes[n].at[y, c, :, :, rows, cols]
                else:
                    part = wholes[n].at[:, c, :, x, rows, cols]
                out.go((job, half, 3), order[1], lambda peer: part, lambda step: part)

        def four(job, n, rows):
            for half, (cols, order) in halves(n):
                out.landed((job, half, 3))
                part = wholes[n].at[:, c, :, :, rows, cols]
                out.go((job, half, 4), "c", lambda peer: part, lambda step: part)

        def five(job, n, rows):
            for half, _ in halves(n):
                out.landed((job, half, 4))

        jobs = [(("gather", at),) + job for at, job in enumerate(self.jobs)]
        ahead = min(3, len(jobs))
        for job in jobs[:ahead]:
            one(*job)
        for step in range(len(jobs) + 3):
            if step < len(jobs):
                two(*jobs[step])
            if step + ahead < len(jobs):
                one(*jobs[step + ahead])
            for stage, late in ((three, 1), (four, 2), (five, 3)):
                if 0 <= step - late < len(jobs):
                    stage(*jobs[step - late])


def total(values):
    result = values[0].astype(jnp.float32)
    for value in values[1:]:
        result = result + value.astype(jnp.float32)
    return result


class Scatter:
    def __init__(self, place, spot, lean, parts, totals, boxes, own_sem):
        self.place, self.spot, self.lean = place, spot, lean
        self.parts, self.totals = parts, totals
        self.jobs = [(n, r) for n, p in enumerate(parts) for r in chunks_of(p.shape[-2])]
        self.own_sem = own_sem
        self.sums, self.cores, self.seconds, self.thirds, self.fourths = [], [], [], [], []
        self.results, self.own = [], []
        for n, part in enumerate(parts):
            self.sums.append(boxes.pop(0))
            self.cores.append(boxes.pop(0))
            halves = halves_of(part.shape[-1], lean)
            self.seconds.append([boxes.pop(0) for _ in halves])
            self.thirds.append([boxes.pop(0) for _ in halves])
            self.fourths.append(boxes.pop(0))
            self.results.append(boxes.pop(0))
            copy = pltpu.make_async_copy(
                part.at[:, spot["c"]], self.sums[n], own_sem[n]
            )
            copy.start()
            self.own.append(copy)

    def run(self, out):
        place, parts, sums = self.place, self.parts, self.sums
        cores, results = self.cores, self.results
        y, c, z, x = (self.spot[k] for k in "yczx")
        lines, _, levels, across = place.grid()
        filled = set()

        def halves(n):
            return enumerate(halves_of(parts[n].shape[-1], self.lean))

        def one(job, n, rows):
            out.go(
                (job, 1),
                "c",
                lambda peer: parts[n].at[:, peer["c"], :, :, rows],
                lambda step: cores[n].at[:, :, :, rows],
            )

        def two(job, n, rows):
            if n not in filled:
                filled.add(n)
                self.own[n].wait()
            out.landed((job, 1))
            if place.cores > 1:

                @pl.loop(0, lines * levels * across)
                def _(at):
                    where = (at // (levels * across), (at // across) % levels, at % across)
                    sums[n][where + (rows,)] = total(
                        [sums[n][where + (rows,)], cores[n][where + (rows,)]]
                    ).astype(sums[n].dtype)

            for half, (cols, order) in halves(n):
                box = self.seconds[n][half]
                if order == "xy":
                    out.go(
                        (job, half, 2),
                        "y",
                        lambda peer: sums[n].at[peer["y"], :, :, rows, cols],
                        lambda step: box.at[step - 1, :, :, rows],
                    )
                else:
                    out.go(
                        (job, half, 2),
                        "x",
                        lambda peer: sums[n].at[:, :, peer["x"], rows, cols],
                        lambda step: box.at[step - 1, :, :, rows],
                    )

        def three(job, n, rows):
            for half, (cols, order) in halves(n):
                out.landed((job, half, 2))
                box, later = self.seconds[n][half], self.thirds[n][half]
                if order == "xy":

                    @pl.loop(0, levels * across)
                    def _(at):
                        zz, xx = at // across, at % across
                        values = [sums[n][y, zz, xx, rows, cols]]
                        values += [box[k, zz, xx, rows] for k in range(lines - 1)]
                        sums[n][y, zz, xx, rows, cols] = total(values).astype(sums[n].dtype)

                    out.go(
                        (job, half, 3),
                        "x",
                        lambda peer: sums[n].at[y, :, peer["x"], rows, cols],
                        lambda step: later.at[step - 1, :, rows],
                    )
                else:

                    @pl.loop(0, lines * levels)
                    def _(at):
                        yy, zz = at // levels, at % levels
                        values = [sums[n][yy, zz, x, rows, cols]]
                        values += [box[k, yy, zz, rows] for k in range(across - 1)]
                        sums[n][yy, zz, x, rows, cols] = total(values).astype(sums[n].dtype)

                    out.go(
                        (job, half, 3),
                        "y",
                        lambda peer: sums[n].at[peer["y"], :, x, rows, cols],
                        lambda step: later.at[step - 1, :, rows],
                    )

        def four(job, n, rows):
            for half, (cols, order) in halves(n):
                out.landed((job, half, 3))
                box = self.thirds[n][half]

                @pl.loop(0, levels)
                def _(zz):
                    values = [sums[n][y, zz, x, rows, cols]]
                    values += [box[k, zz, rows] for k in range(box.shape[0])]
                    sums[n][y, zz, x, rows, cols] = total(values).astype(sums[n].dtype)

            out.go(
                (job, 4),
                "z",
                lambda peer: sums[n].at[y, peer["z"], x, rows],
                lambda step: self.fourths[n].at[step - 1, rows],
            )

        def five(job, n, rows):
            out.landed((job, 4))
            values = [sums[n][y, z, x, rows]]
            values += [self.fourths[n][k, rows] for k in range(levels - 1)]
            results[n][rows] = total(values)

        jobs = [(("scatter", at),) + job for at, job in enumerate(self.jobs)]
        for step in range(len(jobs) + 4):
            for stage, late in ((one, 0), (two, 1), (three, 2), (four, 3), (five, 4)):
                if 0 <= step - late < len(jobs):
                    stage(*jobs[step - late])
        last = []
        for n, result in enumerate(results):
            copy = pltpu.make_async_copy(result, self.totals[n], self.own_sem[n])
            copy.start()
            last.append(copy)
        for copy in last:
            copy.wait()


def scatter_boxes(place, part, lean):
    lines, _, levels, across = place.grid()
    rows, cols = part.shape[-2:]
    block = pltpu.VMEM((lines, levels, across, rows, cols), part.dtype)
    first, later = [], []
    for piece, order in halves_of(cols, lean):
        size = (rows, piece.stop - piece.start)
        steps = (lines - 1, across - 1) if order == "xy" else (across - 1, lines - 1)
        middle = (levels, across) if order == "xy" else (lines, levels)
        first.append(pltpu.VMEM((steps[0],) + middle + size, part.dtype))
        later.append(pltpu.VMEM((steps[1], levels) + size, part.dtype))
    last = pltpu.VMEM((levels - 1, rows, cols), part.dtype)
    return [block, block] + first + later + [last, pltpu.VMEM((rows, cols), jnp.float32)]


def move_kernel(place, counts, lean, *refs):
    refs = list(refs)
    swaps, gathers, scatters = counts
    whole = swaps + gathers + scatters
    ins, outs, rest = refs[:whole], refs[whole : 2 * whole], refs[2 * whole :]
    own_sem, send_sem, recv_sem = rest[-3:]
    spot = place.here()
    dp, me = place.device(spot)
    devices = place.levels * place.across
    sent, got = ins[:swaps], outs[:swaps]
    own = []
    for n in range(swaps):
        copy = pltpu.make_async_copy(sent[n].at[me], got[n].at[me], own_sem.at[n])
        copy.start()
        own.append(copy)
    cut = swaps + gathers
    gather = Gather(
        place, spot, lean, ins[swaps:cut], outs[swaps:cut], [own_sem.at[n] for n in range(swaps, cut)]
    )
    scatter = Scatter(
        place, spot, lean, ins[cut:], outs[cut:], rest[:-3], [own_sem.at[n] for n in range(cut, whole)]
    )
    place.greet(spot, swaps > 0)
    out = Sender(place, spot, send_sem, recv_sem)
    for n in range(swaps):
        for step in range(1, devices):
            peer = lax.rem(me + step, devices)
            out.put("swap", (dp, peer), sent[n].at[peer], got[n].at[me])
    gather.run(out)
    scatter.run(out)
    for copy in own:
        copy.wait()
    if swaps:
        out.landed("swap")
    out.finish()


def move(place, collective_id, swaps=(), gathers=(), scatters=()):
    lean = len(swaps) > 0
    copies = len(swaps) * (place.levels * place.across - 1)
    boxes = []
    lines, cores, levels, across = place.grid()
    for shard in gathers:
        count = (levels - 1) + len(halves_of(shard.shape[-1], lean)) * (
            across + lines + cores - 3
        )
        copies += len(chunks_of(shard.shape[0])) * count
    for part in scatters:
        count = (levels - 1) + (cores - 1)
        count += len(halves_of(part.shape[-1], lean)) * (lines + across - 2)
        copies += len(chunks_of(part.shape[-2])) * count
        boxes += scatter_boxes(place, part, lean)
    shapes = [jax.ShapeDtypeStruct(a.shape, a.dtype) for a in swaps]
    shapes += [jax.ShapeDtypeStruct(place.grid() + s.shape, s.dtype) for s in gathers]
    shapes += [jax.ShapeDtypeStruct(p.shape[-2:], jnp.float32) for p in scatters]
    return pl.pallas_call(
        functools.partial(
            move_kernel, place, (len(swaps), len(gathers), len(scatters)), lean
        ),
        out_shape=shapes,
        in_specs=[pl.BlockSpec(memory_space=pl.ANY)] * len(shapes),
        out_specs=[pl.BlockSpec(memory_space=pl.ANY)] * len(shapes),
        scratch_shapes=boxes
        + [
            pltpu.SemaphoreType.DMA((len(shapes),)),
            pltpu.SemaphoreType.DMA((copies,)),
            pltpu.SemaphoreType.DMA((copies,)),
        ],
        compiler_params=pltpu.CompilerParams(
            collective_id=collective_id,
            has_side_effects=True,
            vmem_limit_bytes=VMEM_BYTES,
        ),
        name=f"move_{collective_id}",
    )(*swaps, *gathers, *scatters)


def side_by_side(ref):
    return jnp.concatenate([ref[s] for s in range(ref.shape[0])], axis=1)


def dot_first(left, right):
    return lax.dot_general(
        left, right, (((0,), (0,)), ((), ())), preferred_element_type=jnp.float32
    )


def dot_last(left, right):
    return lax.dot_general(
        left, right, (((1,), (1,)), ((), ())), preferred_element_type=jnp.float32
    )


def attend_kernel(q_ref, k_ref, v_ref, o_ref, full_ref, sum_ref):
    tokens = q_ref.shape[-1]
    each = ATT_BLOCK // tokens
    keys, values = side_by_side(k_ref), side_by_side(v_ref)
    for block in range(q_ref.shape[0] // each):
        first = block * each
        limit = (block + 1) * ATT_BLOCK
        queries = jnp.concatenate([q_ref[first + s] for s in range(each)], axis=1)
        weights = jnp.exp(dot_first(keys[:, :limit], queries))
        sums = jnp.sum(weights, axis=0, keepdims=True)
        mixed = jnp.dot(
            values[:, :limit],
            weights.astype(jnp.bfloat16),
            preferred_element_type=jnp.float32,
        )
        mixed = mixed / sums
        sum_ref[0, 0, :, pl.ds(block * ATT_BLOCK, ATT_BLOCK)] = sums
        for s in range(each):
            piece = mixed[:, s * tokens : (s + 1) * tokens]
            full_ref[first + s] = piece
            o_ref[first + s] = piece.astype(jnp.bfloat16)


def attend_specs(devices, tokens):
    piece = pl.BlockSpec((devices, HEAD_DIM, tokens), lambda m, h: (0, h, m))
    sums = pl.BlockSpec((1, 1, 1, devices * tokens), lambda m, h: (m, h, 0, 0))
    return piece, sums


def attend(queries, keys, values, tokens):
    devices, rows, cols = queries.shape
    grid = (cols // tokens, rows // HEAD_DIM)
    piece, sums = attend_specs(devices, tokens)
    return pl.pallas_call(
        attend_kernel,
        grid=grid,
        out_shape=[
            jax.ShapeDtypeStruct(queries.shape, jnp.bfloat16),
            jax.ShapeDtypeStruct(queries.shape, jnp.float32),
            jax.ShapeDtypeStruct(grid + (1, devices * tokens), jnp.float32),
        ],
        in_specs=[piece] * 3,
        out_specs=[piece, piece, sums],
        compiler_params=pltpu.CompilerParams(vmem_limit_bytes=VMEM_BYTES),
        name="attend",
    )(queries, keys, values)


def slopes_kernel(
    q_ref, k_ref, v_ref, do_ref, full_ref, sum_ref, rate_ref, dq_ref, dk_ref, dv_ref
):
    tokens = q_ref.shape[-1]
    each = ATT_BLOCK // tokens
    keys, values = side_by_side(k_ref), side_by_side(v_ref)
    rate = rate_ref[...]
    key_total = value_total = None
    for block in reversed(range(q_ref.shape[0] // each)):
        first = block * each
        limit = (block + 1) * ATT_BLOCK

        def pick(ref):
            return jnp.concatenate([ref[first + s] for s in range(each)], axis=1)

        queries = pick(q_ref)
        slope = pick(do_ref).astype(jnp.float32)
        sums = sum_ref[0, 0, :, pl.ds(block * ATT_BLOCK, ATT_BLOCK)]
        scaled = (slope / sums).astype(jnp.bfloat16)
        centre = jnp.sum(slope * pick(full_ref), axis=0, keepdims=True) / sums
        weights = jnp.exp(dot_first(keys[:, :limit], queries))
        dots = dot_first(values[:, :limit], scaled)
        slopes = (weights * (dots - centre)).astype(jnp.bfloat16)
        weights = weights.astype(jnp.bfloat16)
        query_part = jnp.dot(keys[:, :limit], slopes, preferred_element_type=jnp.float32)
        query_part = (query_part * rate).astype(jnp.bfloat16)
        for s in range(each):
            dq_ref[first + s] = query_part[:, s * tokens : (s + 1) * tokens]
        key_part = dot_last(queries, slopes)
        value_part = dot_last(scaled, weights)
        if key_total is None:
            key_total, value_total = key_part, value_part
        else:
            key_total = jnp.concatenate(
                [key_total[:, :limit] + key_part, key_total[:, limit:]], axis=1
            )
            value_total = jnp.concatenate(
                [value_total[:, :limit] + value_part, value_total[:, limit:]], axis=1
            )
    for s in range(q_ref.shape[0]):
        cols = slice(s * tokens, (s + 1) * tokens)
        dk_ref[s] = key_total[:, cols].astype(jnp.bfloat16)
        dv_ref[s] = value_total[:, cols].astype(jnp.bfloat16)


def slopes(queries, keys, values, slope, full, sums, rate, tokens):
    devices, rows, cols = queries.shape
    grid = (cols // tokens, rows // HEAD_DIM)
    piece, sum_spec = attend_specs(devices, tokens)
    return pl.pallas_call(
        slopes_kernel,
        grid=grid,
        out_shape=[jax.ShapeDtypeStruct(queries.shape, jnp.bfloat16)] * 3,
        in_specs=[piece] * 5
        + [sum_spec, pl.BlockSpec((HEAD_DIM, 1), lambda m, h: (0, 0))],
        out_specs=[piece] * 3,
        compiler_params=pltpu.CompilerParams(vmem_limit_bytes=VMEM_BYTES),
        name="slopes",
    )(queries, keys, values, slope, full, sums, rate)


def rms_scale(values):
    return lax.rsqrt(jnp.mean(values * values, axis=-1, keepdims=True) + EPSILON)


def contract(spec, left, right):
    return jnp.einsum(spec, left, right, preferred_element_type=jnp.float32)


def on_device(place, devices, *args):
    inputs, cotangent = args[:2]
    (
        norm_one,
        query_mat,
        query_add,
        key_mat,
        value_mat,
        value_add,
        output_mat,
        output_add,
        norm_two,
        hidden_mat,
        hidden_add,
        project_mat,
        project_add,
    ) = args[2:15]
    depth = args[15].astype(jnp.float32)
    micro, tokens, seqs, width = inputs.shape
    rows = micro * tokens * seqs
    vectors = (norm_one, query_add, value_add, output_add, norm_two, hidden_add, project_add)
    share = norm_one.shape[0]
    small = jnp.pad(jnp.stack(vectors), ((0, 16 - len(vectors)), (0, 128 - share)))
    gathered = move(place, 0, gathers=(small, query_mat, key_mat, value_mat))
    small = gathered[0].reshape(-1, 16, 128)[:, : len(vectors), :share]
    small = small.transpose(1, 0, 2).reshape(len(vectors), width).astype(jnp.float32)
    gain_one, query_add, value_add, output_add, gain_two, hidden_add, project_add = small
    query_mat, key_mat, value_mat = (g.reshape(width, width) for g in gathered[1:])

    def to_rows(array):
        return array.transpose(0, 2, 1, 3).reshape(rows, width)

    def from_rows(array):
        return array.reshape(micro, seqs, tokens, width).transpose(0, 2, 1, 3)

    rate = SOFT_BASE / math.sqrt(HEAD_DIM) * jax.nn.softplus(depth)
    rate_full = jnp.tile(rate, HEADS)[:, None]
    xfloat = to_rows(inputs).astype(jnp.float32)
    inv_one = rms_scale(xfloat)
    normed = (xfloat * inv_one * gain_one).astype(jnp.bfloat16)
    query_pre = contract("df,rd->fr", query_mat, normed) + query_add[:, None]
    queries = (query_pre * rate_full).astype(jnp.bfloat16)
    keys = contract("df,rd->fr", key_mat, normed).astype(jnp.bfloat16)
    values = (contract("df,rd->fr", value_mat, normed) + value_add[:, None]).astype(jnp.bfloat16)

    def split(array):
        return array.reshape(devices, width // devices, rows)

    q_in, k_in, v_in, output_mat, hidden_mat = move(
        place, 1, (split(queries), split(keys), split(values)), (output_mat, hidden_mat)
    )
    output_mat, hidden_mat = (g.reshape(width, width) for g in (output_mat, hidden_mat))
    mixed, full, sums = attend(q_in, k_in, v_in, tokens)
    mixed, project_mat = move(place, 2, (mixed,), (project_mat,))
    mixed, project_mat = mixed.reshape(width, rows), project_mat.reshape(width, width)
    residual = xfloat + (contract("fr,fd->rd", mixed, output_mat) + output_add)
    inv_two = rms_scale(residual)
    second = (residual * inv_two * gain_two).astype(jnp.bfloat16)
    hidden_pre = contract("rd,df->rf", second, hidden_mat) + hidden_add
    active = jax.nn.silu(hidden_pre).astype(jnp.bfloat16)
    result = residual + (contract("rf,fd->rd", active, project_mat) + project_add)
    result = from_rows(result.astype(jnp.bfloat16))

    upper = to_rows(cotangent)
    project_grad = contract("rf,rd->fd", active, upper)
    project_bias_grad = jnp.sum(upper.astype(jnp.float32), axis=0)
    active_grad = contract("rd,fd->rf", upper, project_mat)
    logistic = jax.nn.sigmoid(hidden_pre)
    hidden_grad = (active_grad * logistic * (1.0 + hidden_pre * (1.0 - logistic))).astype(
        jnp.bfloat16
    )
    hidden_mat_grad = contract("rd,rf->df", second, hidden_grad)
    hidden_bias_grad = jnp.sum(hidden_grad.astype(jnp.float32), axis=0)
    second_grad = contract("rf,df->rd", hidden_grad, hidden_mat)
    normal_two = residual * inv_two
    scaled_two = second_grad * gain_two
    norm_two_grad = jnp.sum(second_grad * normal_two, axis=0)
    residual_grad = upper.astype(jnp.float32) + inv_two * (
        scaled_two - normal_two * jnp.mean(scaled_two * normal_two, axis=-1, keepdims=True)
    )
    branch_grad = residual_grad.astype(jnp.bfloat16)
    output_mat_grad = contract("fr,rd->fd", mixed, branch_grad)
    output_bias_grad = jnp.sum(branch_grad.astype(jnp.float32), axis=0)
    mixed_grad = contract("fd,rd->fr", output_mat, branch_grad).astype(jnp.bfloat16)

    def as_parts(*grads):
        return tuple(
            g.astype(jnp.bfloat16).reshape(place.grid() + (share, width)) for g in grads
        )

    merged = share % 8 == 0
    early = as_parts(project_grad) if merged else ()
    do_in, *early = move(place, 3, (split(mixed_grad),), (), early)
    slopes_out = slopes(q_in, k_in, v_in, do_in, full, sums, rate[:, None], tokens)
    middle = as_parts(hidden_mat_grad, output_mat_grad) if merged else ()
    query_slope, key_grad, value_grad, *middle = move(place, 4, slopes_out, (), middle)
    query_slope, key_grad, value_grad = (
        a.reshape(width, rows) for a in (query_slope, key_grad, value_grad)
    )
    query_float = query_slope.astype(jnp.float32)
    scale_part = jnp.sum(query_float / rate_full * query_pre, axis=1)
    scale_part = jnp.sum(scale_part.reshape(HEADS, HEAD_DIM), axis=0)
    query_mat_grad = contract("rd,fr->df", normed, query_slope)
    query_bias_grad = jnp.sum(query_float, axis=1)
    key_mat_grad = contract("rd,fr->df", normed, key_grad)
    value_mat_grad = contract("rd,fr->df", normed, value_grad)
    value_bias_grad = jnp.sum(value_grad.astype(jnp.float32), axis=1)
    normed_grad = (
        contract("fr,df->rd", query_slope, query_mat)
        + contract("fr,df->rd", key_grad, key_mat)
        + contract("fr,df->rd", value_grad, value_mat)
    )
    normal_one = xfloat * inv_one
    scaled_one = normed_grad * gain_one
    norm_one_grad = jnp.sum(normed_grad * normal_one, axis=0)
    source_grad = residual_grad + inv_one * (
        scaled_one - normal_one * jnp.mean(scaled_one * normal_one, axis=-1, keepdims=True)
    )
    source_grad = from_rows(source_grad.astype(jnp.bfloat16))

    vector_grads = jnp.stack(
        (
            norm_one_grad,
            query_bias_grad,
            value_bias_grad,
            output_bias_grad,
            norm_two_grad,
            hidden_bias_grad,
            project_bias_grad,
        )
    )
    vector_grads = vector_grads.reshape(7, -1, share).transpose(1, 0, 2)
    vector_grads = jnp.pad(vector_grads, ((0, 0), (0, 0), (0, 128 - share)))
    scale_row = jnp.pad(scale_part, (0, 128 - HEAD_DIM))
    scale_row = jnp.broadcast_to(scale_row, (vector_grads.shape[0], 1, 128))
    vector_grads = jnp.concatenate([vector_grads, scale_row], axis=1)
    vector_grads = vector_grads.reshape(place.grid() + (8, 128))
    late = as_parts(query_mat_grad, key_mat_grad, value_mat_grad)
    if merged:
        *late, vector_sums = move(place, 5, scatters=late + (vector_grads,))
    else:
        (vector_sums,) = move(place, 5, scatters=(vector_grads,))
        early = as_parts(project_grad, hidden_mat_grad, output_mat_grad)
        early, *middle = ([move(place, 6, scatters=(p,))[0] for p in early])
        early = [early]
        late = [move(place, 6, scatters=(p,))[0] for p in late]
    (project_grad,) = early
    hidden_mat_grad, output_mat_grad = middle
    query_mat_grad, key_mat_grad, value_mat_grad = late
    g_one, g_query, g_value, g_output, g_two, g_hidden, g_project = (
        vector_sums[n, :share] for n in range(7)
    )
    scale_summed = vector_sums[7, :HEAD_DIM]
    depth_grad = scale_summed * (SOFT_BASE / math.sqrt(HEAD_DIM)) * jax.nn.sigmoid(depth)
    return (
        result,
        source_grad,
        g_one,
        query_mat_grad,
        g_query,
        key_mat_grad,
        value_mat_grad,
        g_value,
        output_mat_grad,
        g_output,
        g_two,
        hidden_mat_grad,
        g_hidden,
        project_grad,
        g_project,
        depth_grad,
    )


def solution(mesh):
    both = ("dp", "seq")
    token, vector, matrix = P(None, "seq", "dp", None), P(both), P(both, None)
    weights = (
        vector,
        matrix,
        vector,
        matrix,
        matrix,
        vector,
        matrix,
        vector,
        vector,
        matrix,
        vector,
        matrix,
        vector,
    )
    specs = (token, token) + weights + (P(),)
    place = Place(mesh.shape["dp"], mesh.shape["seq"])
    return jax.shard_map(
        functools.partial(on_device, place, mesh.shape["seq"]),
        mesh=mesh,
        in_specs=specs,
        out_specs=specs,
        check_vma=False,
    )
```

time: 431 us -> 451 us (1.046)
  Pallas kernels: 359 us -> 378 us
    pallas_call x6, Pallas kernels: 341 us -> 360 us  [move(): pl.pallas_call(functools.partial(move_kernel, place, (len(swaps), len(gat...]
    unnamed x52 -> x44, local copies, waits for them, and re-layouts: 9.13 us -> 9.08 us
where the time goes in v2:
time: 451 us; the launch traced here: 450 us
  Pallas kernels  378 us (84%)
  matrix products  47.5 us (11%)
  local copies, waits for them, and re-layouts  14.6 us (3%)
  other arithmetic  9.59 us (2%)
    pallas_call x6, Pallas kernels, move(): pl.pallas_call(functools.partial(move_kernel, place, (len(swaps), len(gat...  360 us
    dot_general x18, matrix products, contract(): return jnp.einsum(spec, left, right, preferred_element_type=jnp.float32)  47.5 us
    pallas_call x1, Pallas kernels, slopes(): pl.pallas_call(slopes_kernel, grid=grid, out_shape=[jax.ShapeDtypeStruct(...  10.8 us
    unnamed x44, local copies, waits for them, and re-layouts  9.08 us

profile of v2, /device:TPU:0, one launch (start us, length us, event | category | flops | bytes accessed | tf_op | source)
XLA Modules:
  0.0 450.5 jit_solution(11256013366242690766)
XLA Ops:
  2.1 60.1 %move_0.1 = (bf16[2,2,4,2,16,128]{5,4,3,2,1,0:T(8,128)(2,1)}, bf16[2,2,4,2,40,1280]{5,4,3,2,1,0:T(8,128)(2,1)}, bf16[2,2,4,2,40,1280]{5,4,3,2,1,0:T(8,128)(2,1)}, bf16[2,2,4,2,40,1280]{5,4,3,2,1,0:T(8,128)(2,1)}) custom-call(bf16[16,128]{1,0:T(8,128)(2,1)} %pad.12.refs_0_, bf16[40,1280]{1,0:T(8,128)(2,1)} %refs_1_.2, bf16[40,1280]{1,0:T(8,128)(2,1)} %refs_2_.1, ...), custom_call_target="tpu_custom_call" | custom-call | tf_op jit(solution)/shard_map/move_0/pallas_call | solution.py:417
  64.9 4.6 %multiply_convert_fusion.2 = (bf16[1280,256]{1,0:T(8,128)(2,1)}, f32[1280,256]{1,0:T(8,128)}) fusion(f32[1280]{0:T(1024)S(1)} %mul.163, f32[1280]{0:T(1024)S(1)} %add.108, bf16[1280,1280]{1,0:T(8,128)(2,1)} %bitcast.152, bf16[256,1280]{1,0:T(8,128)(2,1)S(1)} %bitcast.110), kind=kOutput, calls=%fused_computation.40 | convolution fusion | flops 839843840 | bytes 5908480 | tf_op jit(solution)/shard_map/df,rd->fr/dot_general | solution.py:569
  69.5 1.9 convolution_convert_fusion.7
  71.5 3.9 fusion.5
  75.4 95.2 %move_1.1 = (bf16[8,160,256]{2,1,0:T(8,128)(2,1)}, bf16[8,160,256]{2,1,0:T(8,128)(2,1)}, bf16[8,160,256]{2,1,0:T(8,128)(2,1)}, bf16[2,2,4,2,40,1280]{5,4,3,2,1,0:T(8,128)(2,1)}, bf16[2,2,4,2,40,1280]{5,4,3,2,1,0:T(8,128)(2,1)}) custom-call(bf16[8,160,256]{2,1,0:T(8,128)(2,1)} %bitcast.136, bf16[8,160,256]{2,1,0:T(8,128)(2,1)} %bitcast.137, ...), custom_call_target="tpu_custom_call" | custom-call | tf_op jit(solution)/shard_map/move_1/pallas_call | solution.py:417
  170.6 7.2 %attend.1 = (bf16[8,160,256]{2,1,0:T(8,128)(2,1)}, f32[8,160,256]{2,1,0:T(8,128)}, f32[2,2,1,1024]{3,2,1,0:T(1,128)}) custom-call(bf16[8,160,256]{2,1,0:T(8,128)(2,1)} %get-tuple-element.48.q_ref, bf16[8,160,256]{2,1,0:T(8,128)(2,1)} %get-tuple-element.49.k_ref, bf16[8,160,256]{2,1,0:T(8,128)(2,1)} %get-tuple-element.50.v_ref), custom_call_target="tpu_custom_call" | custom-call | tf_op jit(solution)/shard_map/attend/pallas_call | solution.py:488
  177.8 48.8 %move_2.1 = (bf16[8,160,256]{2,1,0:T(8,128)(2,1)}, bf16[2,2,4,2,40,1280]{5,4,3,2,1,0:T(8,128)(2,1)}) custom-call(bf16[8,160,256]{2,1,0:T(8,128)(2,1)} %get-tuple-element.51.refs_0_, bf16[40,1280]{1,0:T(8,128)(2,1)} %refs_1_.3), custom_call_target="tpu_custom_call" | custom-call | tf_op jit(solution)/shard_map/move_2/pallas_call | solution.py:417
  226.6 3.3 multiply_reduce_fusion.5
  230.2 3.2 convolution_add_fusion.3
  233.4 2.1 fusion.6
  235.5 1.2 convert_reduce_fusion.1
  238.7 1.9 convert_reduce_fusion.2
  241.0 1.9 convolution_convert_fusion.6
  242.9 3.0 convolution_convert_fusion.5
  245.9 34.4 %move_3.1 = (bf16[8,160,256]{2,1,0:T(8,128)(2,1)}, f32[40,1280]{1,0:T(8,128)}) custom-call(bf16[8,160,256]{2,1,0:T(8,128)(2,1)} %bitcast.139, bf16[2,2,4,2,40,1280]{5,4,3,2,1,0:T(8,128)(2,1)} %bitcast.126), custom_call_target="tpu_custom_call" | custom-call | tf_op jit(solution)/shard_map/move_3/pallas_call | solution.py:417
  281.1 10.8 %slopes.1 = (bf16[8,160,256]{2,1,0:T(8,128)(2,1)}, bf16[8,160,256]{2,1,0:T(8,128)(2,1)}, bf16[8,160,256]{2,1,0:T(8,128)(2,1)}) custom-call(bf16[8,160,256]{2,1,0:T(8,128)(2,1)} %get-tuple-element.48.q_ref, bf16[8,160,256]{2,1,0:T(8,128)(2,1)} %get-tuple-element.49.k_ref, bf16[8,160,256]{2,1,0:T(8,128)(2,1)} %get-tuple-element.50.v_ref, ...), custom_call_target="tpu_custom_call" | custom-call | tf_op jit(solution)/shard_map/slopes/pallas_call | solution.py:552
  291.9 4.3 convolution_convert_fusion.4
  296.2 2.7 convolution_convert_fusion.3
  298.9 65.8 %move_4.1 = (bf16[8,160,256]{2,1,0:T(8,128)(2,1)}, bf16[8,160,256]{2,1,0:T(8,128)(2,1)}, bf16[8,160,256]{2,1,0:T(8,128)(2,1)}, f32[40,1280]{1,0:T(8,128)}, f32[40,1280]{1,0:T(8,128)}) custom-call(bf16[8,160,256]{2,1,0:T(8,128)(2,1)} %get-tuple-element.59.refs_0_, bf16[8,160,256]{2,1,0:T(8,128)(2,1)} %get-tuple-element.60.refs_1_, ...), custom_call_target="tpu_custom_call" | custom-call | tf_op jit(solution)/shard_map/move_4/pallas_call | solution.py:417
  364.8 3.3 fusion.11
  370.3 1.4 multiply_reduce_fusion.2
  371.7 1.2 add_convert_fusion
  372.9 2.8 convolution_convert_fusion.2
  375.7 2.8 convolution_convert_fusion.1
  378.5 2.8 convolution_convert_fusion
  382.9 1.8 multiply_reduce_fusion
  385.5 55.4 %move_5.1 = (f32[40,1280]{1,0:T(8,128)}, f32[40,1280]{1,0:T(8,128)}, f32[40,1280]{1,0:T(8,128)}, f32[8,128]{1,0:T(8,128)}) custom-call(bf16[2,2,4,2,40,1280]{5,4,3,2,1,0:T(8,128)(2,1)} %bitcast.116, bf16[2,2,4,2,40,1280]{5,4,3,2,1,0:T(8,128)(2,1)} %bitcast.117, bf16[2,2,4,2,40,1280]{5,4,3,2,1,0:T(8,128)(2,1)} %bitcast.118, f32[2,2,4,2,8,128]{5,4,3,2,1,0:T(8,128)} %bitcast.140), custom_call_target="tpu_custom_call" | custom-call | tf_op jit(solution)/shard_map/move_5/pallas_call | solution.py:417
  440.9 1.5 slice_bitcast_fusion
  442.4 1.2 divide_multiply_fusion
  443.6 1.6 copy.44
  445.2 1.6 copy.45
  446.8 1.6 copy.46
  (80 shorter events, 14.0 us)
Async XLA Ops:
  0.6 63.8 %copy-start = (bf16[2,128,1,1280]{3,1,2,0:T(8,128)(2,1)S(1)}, bf16[2,128,1,1280]{3,1,2,0:T(8,128)(2,1)}, u32[]{:S(2)}) copy-start(bf16[2,128,1,1280]{3,1,2,0:T(8,128)(2,1)} %param.16) | copy-start | bytes 1966084
  64.9 4.6 %copy-start.3 = (bf16[2,2,4,2,40,1280]{5,4,3,2,1,0:T(8,128)(2,1)S(1)}, bf16[2,2,4,2,40,1280]{5,4,3,2,1,0:T(8,128)(2,1)}, u32[]{:S(2)}) copy-start(bf16[2,2,4,2,40,1280]{5,4,3,2,1,0:T(8,128)(2,1)} %get-tuple-element.46) | copy-start | bytes 9830404
  229.9 6.8 %copy-start.2 = (f32[256,1280]{1,0:T(8,128)}, f32[256,1280]{1,0:T(8,128)S(1)}, u32[]{:S(2)}) copy-start(f32[256,1280]{1,0:T(8,128)S(1)} %get-tuple-element.129) | copy-start | bytes 3932164
  230.2 3.2 copy-start.17
  233.4 2.1 copy-start.6
  235.5 1.9 copy-start.16
  238.6 2.3 copy-start.15
  245.9 34.4 %copy-start.18 = (bf16[80]{0:T(256)(128)(2,1)S(1)}, bf16[80]{0:T(256)(128)(2,1)}, u32[]{:S(2)}) copy-start(bf16[80]{0:T(256)(128)(2,1)} %param.31) | copy-start | bytes 484
  291.9 4.3 copy-start.10
  364.7 3.4 copy-start.4
  364.7 3.4 copy-start.5
  368.1 1.1 copy-start.8
  368.1 2.1 copy-start.14
  371.7 1.3 copy-start.1
  378.5 2.9 copy-start.9
  381.3 1.2 copy-start.7
  440.9 7.6 %copy-start.13 = (f32[40,1280]{1,0:T(8,128)S(1)}, f32[40,1280]{1,0:T(8,128)}, u32[]{:S(2)}) copy-start(f32[40,1280]{1,0:T(8,128)} %get-tuple-element.160) | copy-start | bytes 614404
  440.9 8.2 %copy-start.12 = (f32[40,1280]{1,0:T(8,128)S(1)}, f32[40,1280]{1,0:T(8,128)}, u32[]{:S(2)}) copy-start(f32[40,1280]{1,0:T(8,128)} %get-tuple-element.163) | copy-start | bytes 614404
  440.9 8.9 %copy-start.11 = (f32[40,1280]{1,0:T(8,128)S(1)}, f32[40,1280]{1,0:T(8,128)}, u32[]{:S(2)}) copy-start(f32[40,1280]{1,0:T(8,128)} %get-tuple-element.165) | copy-start | bytes 614404

commit v3 on v2

--- a/solution.py
+++ b/solution.py
@@ -16,6 +16,7 @@
 EPSILON = 1e-06
 MESH = pl.DeviceIdType.MESH
 VMEM_BYTES = 60 * 1024 * 1024
+FEED_STEPS = 4
 
 
 class Place:
@@ -98,7 +99,7 @@
         self.open = {}
         self.every = []
 
-    def put(self, key, device, source, target):
+    def put(self, key, device, source, target, leaves=None, comes=None):
         at = next(self.count)
         copy = pltpu.make_async_remote_copy(
             src_ref=source,
@@ -108,9 +109,15 @@
             device_id=device,
             device_id_type=MESH,
         )
-        copy.start()
-        self.open.setdefault(key, []).append(copy)
-        self.every.append(copy)
+        self.guard(leaves, copy.start)
+        self.open.setdefault(key, []).append((comes, copy))
+        self.every.append((leaves, copy))
+
+    def guard(self, when, act):
+        if when is None:
+            act()
+        else:
+            pl.when(when)(act)
 
     def go(self, key, axis, source, target):
         self.open[key] = []
@@ -118,49 +125,89 @@
             peer = self.place.shift(self.spot, axis, step)
             self.put(key, self.place.device(peer), source(peer), target(step))
 
+    def chain(self, key, turn, own, slot):
+        levels, z = self.place.levels, self.spot["z"]
+        self.open[key] = []
+
+        def inside(at):
+            return jnp.logical_and(at >= 0, at < levels)
+
+        for way in (1, -1):
+            shard, to, back = z - turn * way, z + way, z - (turn + 1) * way
+            part = slot(lax.rem(shard + levels, levels))
+            peer = dict(self.spot, z=lax.rem(to + levels, levels))
+            self.put(
+                key,
+                self.place.device(peer),
+                own if turn == 0 else part,
+                part,
+                jnp.logical_and(inside(shard), inside(to)),
+                inside(back),
+            )
+
     def landed(self, key):
-        for copy in self.open[key]:
-            copy.wait_recv()
+        for comes, copy in self.open[key]:
+            self.guard(comes, copy.wait_recv)
 
     def finish(self):
-        for copy in self.every:
-            copy.wait_send()
+        for leaves, copy in self.every:
+            self.guard(leaves, copy.wait_send)
 
 
 class Gather:
-    def __init__(self, place, spot, lean, shards, wholes, own_sem):
-        self.place, self.spot, self.lean = place, spot, lean
+    def __init__(self, place, spot, lean, tails, shards, wholes, own_sem):
+        self.place, self.spot, self.lean, self.tails = place, spot, lean, tails
         self.shards, self.wholes = shards, wholes
-        self.jobs = [(n, r) for n, s in enumerate(shards) for r in chunks_of(s.shape[0])]
         y, c, z, x = (spot[k] for k in "yczx")
         self.own = []
         for n, shard in enumerate(shards):
-            copy = pltpu.make_async_copy(shard, wholes[n].at[y, c, z, x], own_sem[n])
+            if n >= len(shards) - tails:
+                target = wholes[n].at[z]
+            elif len(shard.shape) == 3:
+                target = wholes[n].at[y, c, :, x]
+            else:
+                target = wholes[n].at[y, c, z, x]
+            copy = pltpu.make_async_copy(shard, target, own_sem[n])
             copy.start()
             self.own.append(copy)
 
-    def run(self, out):
+    def run(self, out, feed):
         shards, wholes = self.shards, self.wholes
-        y, c, z, x = (self.spot[k] for k in "yczx")
+        y, c, _, x = (self.spot[k] for k in "yczx")
+        turns = self.place.levels - 1
+        full = len(shards) - self.tails
+        raw = [n for n, s in enumerate(shards) if len(s.shape) == 2]
+        jobs = [(n, r) for n in range(full) for r in chunks_of(shards[n].shape[-2])]
         filled = set()
 
         def halves(n):
             return enumerate(halves_of(shards[n].shape[-1], self.lean))
 
-        def one(job, n, rows):
-            part = wholes[n].at[y, c, z, x, rows]
-            out.go((job, "z"), "z", lambda peer: shards[n].at[rows], lambda step: part)
-
-        def two(job, n, rows):
-            out.landed((job, "z"))
+        def along(turn, n):
+            def slot(level):
+                return wholes[n].at[y, c, level, x] if n < full else wholes[n].at[level]
+
+            if turn > 0:
+                out.landed(("z", n, turn - 1))
+            if turn < turns:
+                out.chain(("z", n, turn), turn, shards[n], slot)
+
+        def fill(n):
             if n not in filled:
                 filled.add(n)
                 self.own[n].wait()
+
+        def two(job, n, rows):
+            lined = len(shards[n].shape) == 3
+            if not lined:
+                fill(n)
             for half, (cols, order) in halves(n):
                 part = wholes[n].at[y, c, :, x, rows, cols]
-                out.go((job, half, 2), order[0], lambda peer: part, lambda step: part)
+                source = shards[n].at[:, rows, cols] if lined else part
+                out.go((job, half, 2), order[0], lambda peer: source, lambda step: part)
 
         def three(job, n, rows):
+            fill(n)
             for half, (cols, order) in halves(n):
                 out.landed((job, half, 2))
                 if order == "xy":
@@ -179,18 +226,29 @@
             for half, _ in halves(n):
                 out.landed((job, half, 4))
 
-        jobs = [(("gather", at),) + job for at, job in enumerate(self.jobs)]
-        ahead = min(3, len(jobs))
-        for job in jobs[:ahead]:
-            one(*job)
-        for step in range(len(jobs) + 3):
-            if step < len(jobs):
-                two(*jobs[step])
-            if step + ahead < len(jobs):
-                one(*jobs[step + ahead])
-            for stage, late in ((three, 1), (four, 2), (five, 3)):
-                if 0 <= step - late < len(jobs):
-                    stage(*jobs[step - late])
+        steps = iter(range(len(jobs) + 3))
+
+        def advance():
+            step = next(steps, None)
+            if step is not None:
+                for stage, late in ((two, 0), (three, 1), (four, 2), (five, 3)):
+                    if 0 <= step - late < len(jobs):
+                        stage(("gather", step - late), *jobs[step - late])
+
+        if raw:
+            for time in range(len(raw) + turns):
+                for turn in range(turns + 1):
+                    if 0 <= time - turn < len(raw):
+                        along(turn, raw[time - turn])
+                done = time - turns
+                if 0 <= done < full:
+                    for _ in chunks_of(shards[raw[done]].shape[-2]):
+                        advance()
+        for _ in range(len(jobs) + 3):
+            advance()
+            feed()
+        for n in range(len(shards)):
+            fill(n)
 
 
 def total(values):
@@ -222,7 +280,7 @@
             copy.start()
             self.own.append(copy)
 
-    def run(self, out):
+    def run(self, out, feed):
         place, parts, sums = self.place, self.parts, self.sums
         cores, results = self.cores, self.results
         y, c, z, x = (self.spot[k] for k in "yczx")
@@ -335,6 +393,7 @@
             for stage, late in ((one, 0), (two, 1), (three, 2), (four, 3), (five, 4)):
                 if 0 <= step - late < len(jobs):
                     stage(*jobs[step - late])
+            feed()
         last = []
         for n, result in enumerate(results):
             copy = pltpu.make_async_copy(result, self.totals[n], self.own_sem[n])
@@ -359,7 +418,7 @@
     return [block, block] + first + later + [last, pltpu.VMEM((rows, cols), jnp.float32)]
 
 
-def move_kernel(place, counts, lean, *refs):
+def move_kernel(place, counts, lean, tails, *refs):
     refs = list(refs)
     swaps, gathers, scatters = counts
     whole = swaps + gathers + scatters
@@ -376,19 +435,28 @@
         own.append(copy)
     cut = swaps + gathers
     gather = Gather(
-        place, spot, lean, ins[swaps:cut], outs[swaps:cut], [own_sem.at[n] for n in range(swaps, cut)]
+        place, spot, lean, tails, ins[swaps:cut], outs[swaps:cut], [own_sem.at[n] for n in range(swaps, cut)]
     )
     scatter = Scatter(
         place, spot, lean, ins[cut:], outs[cut:], rest[:-3], [own_sem.at[n] for n in range(cut, whole)]
     )
     place.greet(spot, swaps > 0)
     out = Sender(place, spot, send_sem, recv_sem)
-    for n in range(swaps):
-        for step in range(1, devices):
+    pending = [(n, step) for n in range(swaps) for step in range(1, devices)]
+    each = pl.cdiv(len(pending), FEED_STEPS)
+
+    def feed():
+        for n, step in pending[:each]:
             peer = lax.rem(me + step, devices)
             out.put("swap", (dp, peer), sent[n].at[peer], got[n].at[me])
-    gather.run(out)
-    scatter.run(out)
+        del pending[:each]
+
+    if gathers:
+        gather.run(out, feed)
+    if scatters:
+        scatter.run(out, feed)
+    while pending:
+        feed()
     for copy in own:
         copy.wait()
     if swaps:
@@ -396,27 +464,32 @@
     out.finish()
 
 
-def move(place, collective_id, swaps=(), gathers=(), scatters=()):
+def move(place, collective_id, swaps=(), gathers=(), scatters=(), tails=0):
     lean = len(swaps) > 0
     copies = len(swaps) * (place.levels * place.across - 1)
     boxes = []
     lines, cores, levels, across = place.grid()
-    for shard in gathers:
-        count = (levels - 1) + len(halves_of(shard.shape[-1], lean)) * (
-            across + lines + cores - 3
-        )
-        copies += len(chunks_of(shard.shape[0])) * count
+    shapes = [jax.ShapeDtypeStruct(a.shape, a.dtype) for a in swaps]
+    for n, shard in enumerate(gathers):
+        rows, cols = shard.shape[-2:]
+        if shard.ndim == 2:
+            copies += 2 * (levels - 1)
+        grid = place.grid()
+        if n < len(gathers) - tails:
+            count = len(halves_of(cols, lean)) * (across + lines + cores - 3)
+            copies += len(chunks_of(rows)) * count
+        else:
+            grid = (levels,)
+        shapes.append(jax.ShapeDtypeStruct(grid + (rows, cols), shard.dtype))
     for part in scatters:
         count = (levels - 1) + (cores - 1)
         count += len(halves_of(part.shape[-1], lean)) * (lines + across - 2)
         copies += len(chunks_of(part.shape[-2])) * count
         boxes += scatter_boxes(place, part, lean)
-    shapes = [jax.ShapeDtypeStruct(a.shape, a.dtype) for a in swaps]
-    shapes += [jax.ShapeDtypeStruct(place.grid() + s.shape, s.dtype) for s in gathers]
     shapes += [jax.ShapeDtypeStruct(p.shape[-2:], jnp.float32) for p in scatters]
     return pl.pallas_call(
         functools.partial(
-            move_kernel, place, (len(swaps), len(gathers), len(scatters)), lean
+            move_kernel, place, (len(swaps), len(gathers), len(scatters)), lean, tails
         ),
         out_shape=shapes,
         in_specs=[pl.BlockSpec(memory_space=pl.ANY)] * len(shapes),
@@ -592,11 +665,18 @@
     vectors = (norm_one, query_add, value_add, output_add, norm_two, hidden_add, project_add)
     share = norm_one.shape[0]
     small = jnp.pad(jnp.stack(vectors), ((0, 16 - len(vectors)), (0, 128 - share)))
-    gathered = move(place, 0, gathers=(small, query_mat, key_mat, value_mat))
-    small = gathered[0].reshape(-1, 16, 128)[:, : len(vectors), :share]
+    query_mat, small, key_mat, value_mat, output_mat, hidden_mat, project_mat = move(
+        place,
+        0,
+        gathers=(query_mat, small, key_mat, value_mat, output_mat, hidden_mat, project_mat),
+        tails=3,
+    )
+    small = small.reshape(-1, 16, 128)[:, : len(vectors), :share]
     small = small.transpose(1, 0, 2).reshape(len(vectors), width).astype(jnp.float32)
     gain_one, query_add, value_add, output_add, gain_two, hidden_add, project_add = small
-    query_mat, key_mat, value_mat = (g.reshape(width, width) for g in gathered[1:])
+    query_mat, key_mat, value_mat = (
+        g.reshape(width, width) for g in (query_mat, key_mat, value_mat)
+    )
 
     def to_rows(array):
         return array.transpose(0, 2, 1, 3).reshape(rows, width)

time: 451 us -> 411 us (0.911)
  Pallas kernels: 378 us -> 338 us
    pallas_call x6, Pallas kernels: 360 us -> 320 us  [move(): pl.pallas_call(functools.partial(move_kernel, place, (len(swaps), len(gat...]
where the time goes in v3:
time: 411 us
  Pallas kernels  338 us (82%)
  matrix products  47.4 us (12%)
  local copies, waits for them, and re-layouts  14.6 us (4%)
  other arithmetic  9.59 us (2%)
    pallas_call x6, Pallas kernels, move(): pl.pallas_call(functools.partial(move_kernel, place, (len(swaps), len(gat...  320 us
    dot_general x18, matrix products, contract(): return jnp.einsum(spec, left, right, preferred_element_type=jnp.float32)  47.4 us
    pallas_call x1, Pallas kernels, slopes(): pl.pallas_call(slopes_kernel, grid=grid, out_shape=[jax.ShapeDtypeStruct(...  10.9 us
    unnamed x44, local copies, waits for them, and re-layouts  9.09 us

profile of v3, /device:TPU:0, one launch (start us, length us, event | category | flops | bytes accessed | tf_op | source)
XLA Modules:
  0.0 410.7 jit_solution(974246821920553676)
XLA Ops:
  2.1 65.1 %move_0.1 = (bf16[2,2,4,2,40,1280]{5,4,3,2,1,0:T(8,128)(2,1)}, bf16[2,2,4,2,16,128]{5,4,3,2,1,0:T(8,128)(2,1)}, bf16[2,2,4,2,40,1280]{5,4,3,2,1,0:T(8,128)(2,1)}...) custom-call(bf16[40,1280]{1,0:T(8,128)(2,1)} %refs_0_.1, ...), custom_call_target="tpu_custom_call" | custom-call | tf_op jit(solution)/shard_map/move_0/pallas_call | solution.py:490
  69.9 4.6 %multiply_convert_fusion.2 = (bf16[1280,256]{1,0:T(8,128)(2,1)}, f32[1280,256]{1,0:T(8,128)}) fusion(f32[1280]{0:T(1024)S(1)} %mul.163, f32[1280]{0:T(1024)S(1)} %add.108, bf16[1280,1280]{1,0:T(8,128)(2,1)} %bitcast.152, bf16[256,1280]{1,0:T(8,128)(2,1)S(1)} %bitcast.110), kind=kOutput, calls=%fused_computation.40 | convolution fusion | flops 839843840 | bytes 5908480 | tf_op jit(solution)/shard_map/df,rd->fr/dot_general | solution.py:642
  74.5 1.9 convolution_convert_fusion.7
  76.5 3.9 fusion.5
  80.4 59.4 %move_1.1 = (bf16[8,160,256]{2,1,0:T(8,128)(2,1)}, bf16[8,160,256]{2,1,0:T(8,128)(2,1)}, bf16[8,160,256]{2,1,0:T(8,128)(2,1)}, bf16[2,2,4,2,40,1280]{5,4,3,2,1,0:T(8,128)(2,1)}, bf16[2,2,4,2,40,1280]{5,4,3,2,1,0:T(8,128)(2,1)}) custom-call(bf16[8,160,256]{2,1,0:T(8,128)(2,1)} %bitcast.136, bf16[8,160,256]{2,1,0:T(8,128)(2,1)} %bitcast.137, ...), custom_call_target="tpu_custom_call" | custom-call | tf_op jit(solution)/shard_map/move_1/pallas_call | solution.py:490
  139.8 7.2 %attend.1 = (bf16[8,160,256]{2,1,0:T(8,128)(2,1)}, f32[8,160,256]{2,1,0:T(8,128)}, f32[2,2,1,1024]{3,2,1,0:T(1,128)}) custom-call(bf16[8,160,256]{2,1,0:T(8,128)(2,1)} %get-tuple-element.53.q_ref, bf16[8,160,256]{2,1,0:T(8,128)(2,1)} %get-tuple-element.54.k_ref, bf16[8,160,256]{2,1,0:T(8,128)(2,1)} %get-tuple-element.55.v_ref), custom_call_target="tpu_custom_call" | custom-call | tf_op jit(solution)/shard_map/attend/pallas_call | solution.py:561
  147.0 39.5 %move_2.1 = (bf16[8,160,256]{2,1,0:T(8,128)(2,1)}, bf16[2,2,4,2,40,1280]{5,4,3,2,1,0:T(8,128)(2,1)}) custom-call(bf16[8,160,256]{2,1,0:T(8,128)(2,1)} %get-tuple-element.56.refs_0_, bf16[4,40,1280]{2,1,0:T(8,128)(2,1)} %get-tuple-element.57.refs_1_), custom_call_target="tpu_custom_call" | custom-call | tf_op jit(solution)/shard_map/move_2/pallas_call | solution.py:490
  186.6 3.3 multiply_reduce_fusion.5
  190.2 3.2 convolution_add_fusion.3
  193.4 2.1 fusion.6
  195.5 1.2 convert_reduce_fusion.1
  198.6 1.9 convert_reduce_fusion.2
  200.9 1.9 convolution_convert_fusion.6
  202.8 3.0 convolution_convert_fusion.5
  205.9 31.8 %move_3.1 = (bf16[8,160,256]{2,1,0:T(8,128)(2,1)}, f32[40,1280]{1,0:T(8,128)}) custom-call(bf16[8,160,256]{2,1,0:T(8,128)(2,1)} %bitcast.139, bf16[2,2,4,2,40,1280]{5,4,3,2,1,0:T(8,128)(2,1)} %bitcast.126), custom_call_target="tpu_custom_call" | custom-call | tf_op jit(solution)/shard_map/move_3/pallas_call | solution.py:490
  238.4 10.9 %slopes.1 = (bf16[8,160,256]{2,1,0:T(8,128)(2,1)}, bf16[8,160,256]{2,1,0:T(8,128)(2,1)}, bf16[8,160,256]{2,1,0:T(8,128)(2,1)}) custom-call(bf16[8,160,256]{2,1,0:T(8,128)(2,1)} %get-tuple-element.53.q_ref, bf16[8,160,256]{2,1,0:T(8,128)(2,1)} %get-tuple-element.54.k_ref, bf16[8,160,256]{2,1,0:T(8,128)(2,1)} %get-tuple-element.55.v_ref, ...), custom_call_target="tpu_custom_call" | custom-call | tf_op jit(solution)/shard_map/slopes/pallas_call | solution.py:625
  249.3 4.3 %convolution_convert_fusion.4 = bf16[1280,1280]{1,0:T(8,128)(2,1)} fusion(bf16[256,1280]{1,0:T(8,128)(2,1)S(1)} %get-tuple-element.139, f32[256,1280]{1,0:T(8,128)} %copy-done.2, f32[1280]{0:T(1024)S(1)} %mul.169, f32[256]{0:T(256)S(1)} %add_rsqrt_fusion), kind=kOutput, calls=%fused_computation.4 | convolution fusion | flops 841482240 | bytes 5249024 | tf_op jit(solution)/shard_map/rd,rf->df/dot_general | solution.py:642
  253.6 2.7 convolution_convert_fusion.3
  256.2 69.5 %move_4.1 = (bf16[8,160,256]{2,1,0:T(8,128)(2,1)}, bf16[8,160,256]{2,1,0:T(8,128)(2,1)}, bf16[8,160,256]{2,1,0:T(8,128)(2,1)}, f32[40,1280]{1,0:T(8,128)}, f32[40,1280]{1,0:T(8,128)}) custom-call(bf16[8,160,256]{2,1,0:T(8,128)(2,1)} %get-tuple-element.65.refs_0_, bf16[8,160,256]{2,1,0:T(8,128)(2,1)} %get-tuple-element.66.refs_1_, ...), custom_call_target="tpu_custom_call" | custom-call | tf_op jit(solution)/shard_map/move_4/pallas_call | solution.py:490
  325.8 3.3 fusion.11
  331.3 1.4 multiply_reduce_fusion.2
  332.7 1.2 add_convert_fusion
  333.9 2.8 convolution_convert_fusion.2
  336.7 2.8 convolution_convert_fusion.1
  339.5 2.8 convolution_convert_fusion
  343.9 1.8 multiply_reduce_fusion
  346.5 54.5 %move_5.1 = (f32[40,1280]{1,0:T(8,128)}, f32[40,1280]{1,0:T(8,128)}, f32[40,1280]{1,0:T(8,128)}, f32[8,128]{1,0:T(8,128)}) custom-call(bf16[2,2,4,2,40,1280]{5,4,3,2,1,0:T(8,128)(2,1)} %bitcast.116, bf16[2,2,4,2,40,1280]{5,4,3,2,1,0:T(8,128)(2,1)} %bitcast.117, bf16[2,2,4,2,40,1280]{5,4,3,2,1,0:T(8,128)(2,1)} %bitcast.118, f32[2,2,4,2,8,128]{5,4,3,2,1,0:T(8,128)} %bitcast.140), custom_call_target="tpu_custom_call" | custom-call | tf_op jit(solution)/shard_map/move_5/pallas_call | solution.py:490
  401.1 1.5 slice_bitcast_fusion
  402.6 1.2 divide_multiply_fusion
  403.8 1.6 copy.44
  405.4 1.6 copy.45
  407.0 1.6 copy.46
  (80 shorter events, 14.0 us)
Async XLA Ops:
  0.6 68.8 %copy-start = (bf16[2,128,1,1280]{3,1,2,0:T(8,128)(2,1)S(1)}, bf16[2,128,1,1280]{3,1,2,0:T(8,128)(2,1)}, u32[]{:S(2)}) copy-start(bf16[2,128,1,1280]{3,1,2,0:T(8,128)(2,1)} %param.16) | copy-start | bytes 1966084
  69.9 4.6 %copy-start.3 = (bf16[2,2,4,2,40,1280]{5,4,3,2,1,0:T(8,128)(2,1)S(1)}, bf16[2,2,4,2,40,1280]{5,4,3,2,1,0:T(8,128)(2,1)}, u32[]{:S(2)}) copy-start(bf16[2,2,4,2,40,1280]{5,4,3,2,1,0:T(8,128)(2,1)} %get-tuple-element.49) | copy-start | bytes 9830404
  189.9 6.8 %copy-start.2 = (f32[256,1280]{1,0:T(8,128)}, f32[256,1280]{1,0:T(8,128)S(1)}, u32[]{:S(2)}) copy-start(f32[256,1280]{1,0:T(8,128)S(1)} %get-tuple-element.135) | copy-start | bytes 3932164
  190.2 3.2 copy-start.17
  193.4 2.1 copy-start.6
  195.5 1.9 copy-start.16
  198.6 2.3 copy-start.15
  205.9 31.8 %copy-start.18 = (bf16[80]{0:T(256)(128)(2,1)S(1)}, bf16[80]{0:T(256)(128)(2,1)}, u32[]{:S(2)}) copy-start(bf16[80]{0:T(256)(128)(2,1)} %param.31) | copy-start | bytes 484
  249.3 4.3 %copy-start.10 = (bf16[8,160,256]{2,1,0:T(8,128)(2,1)S(1)}, bf16[8,160,256]{2,1,0:T(8,128)(2,1)}, u32[]{:S(2)}) copy-start(bf16[8,160,256]{2,1,0:T(8,128)(2,1)} %get-tuple-element.58) | copy-start | bytes 1966084
  325.8 3.4 copy-start.4
  325.8 3.4 copy-start.5
  329.1 1.1 copy-start.8
  329.2 2.1 copy-start.14
  332.7 1.3 copy-start.1
  339.5 2.9 copy-start.9
  342.3 1.2 copy-start.7
  401.1 7.6 %copy-start.13 = (f32[40,1280]{1,0:T(8,128)S(1)}, f32[40,1280]{1,0:T(8,128)}, u32[]{:S(2)}) copy-start(f32[40,1280]{1,0:T(8,128)} %get-tuple-element.166) | copy-start | bytes 614404
  401.1 8.2 %copy-start.12 = (f32[40,1280]{1,0:T(8,128)S(1)}, f32[40,1280]{1,0:T(8,128)}, u32[]{:S(2)}) copy-start(f32[40,1280]{1,0:T(8,128)} %get-tuple-element.169) | copy-start | bytes 614404
  401.1 8.9 %copy-start.11 = (f32[40,1280]{1,0:T(8,128)S(1)}, f32[40,1280]{1,0:T(8,128)}, u32[]{:S(2)}) copy-start(f32[40,1280]{1,0:T(8,128)} %get-tuple-element.171) | copy-start | bytes 614404

commit v4 on v3

--- a/solution.py
+++ b/solution.py
@@ -259,24 +259,38 @@
 
 
 class Scatter:
-    def __init__(self, place, spot, lean, parts, totals, boxes, own_sem):
+    def __init__(self, place, spot, lean, held, parts, totals, boxes, own_sem):
         self.place, self.spot, self.lean = place, spot, lean
         self.parts, self.totals = parts, totals
-        self.jobs = [(n, r) for n, p in enumerate(parts) for r in chunks_of(p.shape[-2])]
+        self.full = len(parts) - held
+        self.jobs = [
+            (n, r)
+            for n, p in enumerate(parts)
+            if len(p.shape) > 3
+            for r in chunks_of(p.shape[-2])
+        ]
         self.own_sem = own_sem
         self.sums, self.cores, self.seconds, self.thirds, self.fourths = [], [], [], [], []
         self.results, self.own = [], []
         for n, part in enumerate(parts):
             self.sums.append(boxes.pop(0))
-            self.cores.append(boxes.pop(0))
-            halves = halves_of(part.shape[-1], lean)
-            self.seconds.append([boxes.pop(0) for _ in halves])
-            self.thirds.append([boxes.pop(0) for _ in halves])
-            self.fourths.append(boxes.pop(0))
-            self.results.append(boxes.pop(0))
-            copy = pltpu.make_async_copy(
-                part.at[:, spot["c"]], self.sums[n], own_sem[n]
-            )
+            if len(part.shape) > 3:
+                self.cores.append(boxes.pop(0))
+                halves = halves_of(part.shape[-1], lean)
+                self.seconds.append([boxes.pop(0) for _ in halves])
+                self.thirds.append([boxes.pop(0) for _ in halves])
+                mine = part.at[:, spot["c"]]
+            else:
+                for boxed in (self.cores, self.seconds, self.thirds):
+                    boxed.append(None)
+                mine = part.at[spot["z"]]
+            if n < self.full:
+                self.fourths.append(boxes.pop(0))
+                self.results.append(boxes.pop(0))
+            else:
+                self.fourths.append(None)
+                self.results.append(self.sums[n].at[spot["y"], :, spot["x"]])
+            copy = pltpu.make_async_copy(mine, self.sums[n], own_sem[n])
             copy.start()
             self.own.append(copy)
 
@@ -375,21 +389,43 @@
                     values += [box[k, zz, rows] for k in range(box.shape[0])]
                     sums[n][y, zz, x, rows, cols] = total(values).astype(sums[n].dtype)
 
-            out.go(
-                (job, 4),
-                "z",
-                lambda peer: sums[n].at[y, peer["z"], x, rows],
-                lambda step: self.fourths[n].at[step - 1, rows],
-            )
+            if n < self.full:
+                out.go(
+                    (job, 4),
+                    "z",
+                    lambda peer: sums[n].at[y, peer["z"], x, rows],
+                    lambda step: self.fourths[n].at[step - 1, rows],
+                )
 
         def five(job, n, rows):
+            if n >= self.full:
+                return
             out.landed((job, 4))
             values = [sums[n][y, z, x, rows]]
             values += [self.fourths[n][k, rows] for k in range(levels - 1)]
             results[n][rows] = total(values)
 
+        def first(n):
+            out.go(
+                ("tail", n),
+                "z",
+                lambda peer: parts[n].at[peer["z"]],
+                lambda step: self.fourths[n].at[step - 1],
+            )
+
+        def final(n):
+            self.own[n].wait()
+            out.landed(("tail", n))
+            values = [sums[n][...]] + [self.fourths[n][k] for k in range(levels - 1)]
+            results[n][...] = total(values)
+
         jobs = [(("scatter", at),) + job for at, job in enumerate(self.jobs)]
+        tails = [n for n, p in enumerate(parts) if len(p.shape) == 3]
+        for n in tails:
+            first(n)
         for step in range(len(jobs) + 4):
+            if step > 2 and tails:
+                final(tails.pop(0))
             for stage, late in ((one, 0), (two, 1), (three, 2), (four, 3), (five, 4)):
                 if 0 <= step - late < len(jobs):
                     stage(*jobs[step - late])
@@ -403,9 +439,15 @@
             copy.wait()
 
 
-def scatter_boxes(place, part, lean):
+def scatter_boxes(place, part, lean, held):
     lines, _, levels, across = place.grid()
     rows, cols = part.shape[-2:]
+    final = [
+        pltpu.VMEM((levels - 1, rows, cols), part.dtype),
+        pltpu.VMEM((rows, cols), jnp.float32),
+    ]
+    if part.ndim == 3:
+        return [pltpu.VMEM((rows, cols), part.dtype)] + final
     block = pltpu.VMEM((lines, levels, across, rows, cols), part.dtype)
     first, later = [], []
     for piece, order in halves_of(cols, lean):
@@ -414,11 +456,10 @@
         middle = (levels, across) if order == "xy" else (lines, levels)
         first.append(pltpu.VMEM((steps[0],) + middle + size, part.dtype))
         later.append(pltpu.VMEM((steps[1], levels) + size, part.dtype))
-    last = pltpu.VMEM((levels - 1, rows, cols), part.dtype)
-    return [block, block] + first + later + [last, pltpu.VMEM((rows, cols), jnp.float32)]
-
-
-def move_kernel(place, counts, lean, tails, *refs):
+    return [block, block] + first + later + ([] if held else final)
+
+
+def move_kernel(place, counts, lean, tails, held, *refs):
     refs = list(refs)
     swaps, gathers, scatters = counts
     whole = swaps + gathers + scatters
@@ -438,7 +479,7 @@
         place, spot, lean, tails, ins[swaps:cut], outs[swaps:cut], [own_sem.at[n] for n in range(swaps, cut)]
     )
     scatter = Scatter(
-        place, spot, lean, ins[cut:], outs[cut:], rest[:-3], [own_sem.at[n] for n in range(cut, whole)]
+        place, spot, lean, held, ins[cut:], outs[cut:], rest[:-3], [own_sem.at[n] for n in range(cut, whole)]
     )
     place.greet(spot, swaps > 0)
     out = Sender(place, spot, send_sem, recv_sem)
@@ -464,7 +505,7 @@
     out.finish()
 
 
-def move(place, collective_id, swaps=(), gathers=(), scatters=(), tails=0):
+def move(place, collective_id, swaps=(), gathers=(), scatters=(), tails=0, held=0):
     lean = len(swaps) > 0
     copies = len(swaps) * (place.levels * place.across - 1)
     boxes = []
@@ -481,19 +522,34 @@
         else:
             grid = (levels,)
         shapes.append(jax.ShapeDtypeStruct(grid + (rows, cols), shard.dtype))
-    for part in scatters:
-        count = (levels - 1) + (cores - 1)
-        count += len(halves_of(part.shape[-1], lean)) * (lines + across - 2)
-        copies += len(chunks_of(part.shape[-2])) * count
-        boxes += scatter_boxes(place, part, lean)
-    shapes += [jax.ShapeDtypeStruct(p.shape[-2:], jnp.float32) for p in scatters]
+    for n, part in enumerate(scatters):
+        rows, cols = part.shape[-2:]
+        keeps = n >= len(scatters) - held
+        count = 0 if keeps else levels - 1
+        if part.ndim > 3:
+            count += (cores - 1) + len(halves_of(cols, lean)) * (lines + across - 2)
+            count *= len(chunks_of(rows))
+        copies += count
+        boxes += scatter_boxes(place, part, lean, keeps)
+        shapes.append(
+            jax.ShapeDtypeStruct((levels, rows, cols), part.dtype)
+            if keeps
+            else jax.ShapeDtypeStruct((rows, cols), jnp.float32)
+        )
+
+    def is_result(a):
+        return a.dtype == jnp.float32 and a.shape[-1] > 128
+
     return pl.pallas_call(
         functools.partial(
-            move_kernel, place, (len(swaps), len(gathers), len(scatters)), lean, tails
+            move_kernel, place, (len(swaps), len(gathers), len(scatters)), lean, tails, held
         ),
         out_shape=shapes,
         in_specs=[pl.BlockSpec(memory_space=pl.ANY)] * len(shapes),
-        out_specs=[pl.BlockSpec(memory_space=pl.ANY)] * len(shapes),
+        out_specs=[
+            pl.BlockSpec(memory_space=pltpu.HBM if is_result(a) else pl.ANY)
+            for a in shapes
+        ],
         scratch_shapes=boxes
         + [
             pltpu.SemaphoreType.DMA((len(shapes),)),
@@ -697,13 +753,18 @@
     def split(array):
         return array.reshape(devices, width // devices, rows)
 
-    q_in, k_in, v_in, output_mat, hidden_mat = move(
-        place, 1, (split(queries), split(keys), split(values)), (output_mat, hidden_mat)
-    )
-    output_mat, hidden_mat = (g.reshape(width, width) for g in (output_mat, hidden_mat))
+    q_in, k_in, v_in, output_mat, hidden_mat, project_mat = move(
+        place,
+        1,
+        (split(queries), split(keys), split(values)),
+        (output_mat, hidden_mat, project_mat),
+    )
+    output_mat, hidden_mat, project_mat = (
+        g.reshape(width, width) for g in (output_mat, hidden_mat, project_mat)
+    )
     mixed, full, sums = attend(q_in, k_in, v_in, tokens)
-    mixed, project_mat = move(place, 2, (mixed,), (project_mat,))
-    mixed, project_mat = mixed.reshape(width, rows), project_mat.reshape(width, width)
+    (mixed,) = move(place, 2, (mixed,))
+    mixed = mixed.reshape(width, rows)
     residual = xfloat + (contract("fr,fd->rd", mixed, output_mat) + output_add)
     inv_two = rms_scale(residual)
     second = (residual * inv_two * gain_two).astype(jnp.bfloat16)
@@ -740,11 +801,12 @@
         )
 
     merged = share % 8 == 0
-    early = as_parts(project_grad) if merged else ()
-    do_in, *early = move(place, 3, (split(mixed_grad),), (), early)
+    (do_in,) = move(place, 3, (split(mixed_grad),))
     slopes_out = slopes(q_in, k_in, v_in, do_in, full, sums, rate[:, None], tokens)
-    middle = as_parts(hidden_mat_grad, output_mat_grad) if merged else ()
-    query_slope, key_grad, value_grad, *middle = move(place, 4, slopes_out, (), middle)
+    early = as_parts(output_mat_grad, hidden_mat_grad, project_grad) if merged else ()
+    query_slope, key_grad, value_grad, *early = move(
+        place, 4, slopes_out, (), early, held=2 if merged else 0
+    )
     query_slope, key_grad, value_grad = (
         a.reshape(width, rows) for a in (query_slope, key_grad, value_grad)
     )
@@ -788,15 +850,16 @@
     vector_grads = vector_grads.reshape(place.grid() + (8, 128))
     late = as_parts(query_mat_grad, key_mat_grad, value_mat_grad)
     if merged:
-        *late, vector_sums = move(place, 5, scatters=late + (vector_grads,))
+        output_mat_grad, *early = early
+        hidden_mat_grad, project_grad, *late, vector_sums = move(
+            place, 5, scatters=(*early, *late, vector_grads)
+        )
     else:
         (vector_sums,) = move(place, 5, scatters=(vector_grads,))
-        early = as_parts(project_grad, hidden_mat_grad, output_mat_grad)
-        early, *middle = ([move(place, 6, scatters=(p,))[0] for p in early])
-        early = [early]
+        early = as_parts(output_mat_grad, hidden_mat_grad, project_grad)
+        early = [move(place, 6, scatters=(p,))[0] for p in early]
+        output_mat_grad, hidden_mat_grad, project_grad = early
         late = [move(place, 6, scatters=(p,))[0] for p in late]
-    (project_grad,) = early
-    hidden_mat_grad, output_mat_grad = middle
     query_mat_grad, key_mat_grad, value_mat_grad = late
     g_one, g_query, g_value, g_output, g_two, g_hidden, g_project = (
         vector_sums[n, :share] for n in range(7)

time: 411 us -> 401 us (0.976)
  Pallas kernels: 338 us -> 329 us
    pallas_call x6, Pallas kernels: 320 us -> 311 us  [move(): pl.pallas_call(functools.partial(move_kernel, place, (len(swaps), len(gat...]
    unnamed x44 -> x56, local copies, waits for them, and re-layouts: 9.09 us -> 9.1 us
where the time goes in v4:
time: 401 us
  Pallas kernels  329 us (82%)
  matrix products  46 us (11%)
  local copies, waits for them, and re-layouts  14.6 us (4%)
  other arithmetic  9.58 us (2%)
    pallas_call x6, Pallas kernels, move(): pl.pallas_call(functools.partial(move_kernel, place, (len(swaps), len(gat...  311 us
    dot_general x18, matrix products, contract(): return jnp.einsum(spec, left, right, preferred_element_type=jnp.float32)  46 us
    pallas_call x1, Pallas kernels, slopes(): pl.pallas_call(slopes_kernel, grid=grid, out_shape=[jax.ShapeDtypeStruct(...  10.9 us
    unnamed x56, local copies, waits for them, and re-layouts  9.1 us

profile of v4, /device:TPU:0, one launch (start us, length us, event | category | flops | bytes accessed | tf_op | source)
XLA Modules:
  0.0 400.8 jit_solution(2229129332782306481)
XLA Ops:
  2.1 65.1 %move_0.1 = (bf16[2,2,4,2,40,1280]{5,4,3,2,1,0:T(8,128)(2,1)}, bf16[2,2,4,2,16,128]{5,4,3,2,1,0:T(8,128)(2,1)}, bf16[2,2,4,2,40,1280]{5,4,3,2,1,0:T(8,128)(2,1)}...) custom-call(bf16[40,1280]{1,0:T(8,128)(2,1)} %refs_0_.1, ...), custom_call_target="tpu_custom_call" | custom-call | tf_op jit(solution)/shard_map/move_0/pallas_call | solution.py:543
  69.9 4.6 %multiply_convert_fusion.2 = (bf16[1280,256]{1,0:T(8,128)(2,1)}, f32[1280,256]{1,0:T(8,128)}) fusion(f32[1280]{0:T(1024)S(1)} %mul.163, f32[1280]{0:T(1024)S(1)} %add.108, bf16[1280,1280]{1,0:T(8,128)(2,1)} %bitcast.152, bf16[256,1280]{1,0:T(8,128)(2,1)S(1)} %bitcast.110), kind=kOutput, calls=%fused_computation.40 | convolution fusion | flops 839843840 | bytes 5908480 | tf_op jit(solution)/shard_map/df,rd->fr/dot_general | solution.py:698
  74.5 1.9 convolution_convert_fusion.7
  76.5 3.9 fusion.5
  80.4 74.7 %move_1.1 = (bf16[8,160,256]{2,1,0:T(8,128)(2,1)}, bf16[8,160,256]{2,1,0:T(8,128)(2,1)}, bf16[8,160,256]{2,1,0:T(8,128)(2,1)}, bf16[2,2,4,2,40,1280]{5,4,3,2,1,0...) custom-call(bf16[8,160,256]{2,1,0:T(8,128)(2,1)} %bitcast.137, ...), custom_call_target="tpu_custom_call" | custom-call | tf_op jit(solution)/shard_map/move_1/pallas_call | solution.py:543
  155.1 7.2 %attend.1 = (bf16[8,160,256]{2,1,0:T(8,128)(2,1)}, f32[8,160,256]{2,1,0:T(8,128)}, f32[2,2,1,1024]{3,2,1,0:T(1,128)}) custom-call(bf16[8,160,256]{2,1,0:T(8,128)(2,1)} %get-tuple-element.54.q_ref, bf16[8,160,256]{2,1,0:T(8,128)(2,1)} %get-tuple-element.55.k_ref, bf16[8,160,256]{2,1,0:T(8,128)(2,1)} %get-tuple-element.56.v_ref), custom_call_target="tpu_custom_call" | custom-call | tf_op jit(solution)/shard_map/attend/pallas_call | solution.py:617
  162.4 14.7 %move_2.1 = bf16[8,160,256]{2,1,0:T(8,128)(2,1)} custom-call(bf16[8,160,256]{2,1,0:T(8,128)(2,1)} %get-tuple-element.57.refs_0_), custom_call_target="tpu_custom_call" | custom-call | tf_op jit(solution)/shard_map/move_2/pallas_call | solution.py:543
  177.0 3.3 multiply_reduce_fusion.5
  180.6 3.2 convolution_add_fusion.3
  183.9 2.1 fusion.6
  186.0 1.2 convert_reduce_fusion.1
  189.1 1.9 convert_reduce_fusion.2
  191.4 1.9 convolution_convert_fusion.6
  193.4 18.2 %move_3.1.do_ref = bf16[8,160,256]{2,1,0:T(8,128)(2,1)} custom-call(bf16[8,160,256]{2,1,0:T(8,128)(2,1)} %bitcast.136), custom_call_target="tpu_custom_call" | custom-call | tf_op jit(solution)/shard_map/move_3/pallas_call | solution.py:543
  212.3 10.9 %slopes.1 = (bf16[8,160,256]{2,1,0:T(8,128)(2,1)}, bf16[8,160,256]{2,1,0:T(8,128)(2,1)}, bf16[8,160,256]{2,1,0:T(8,128)(2,1)}) custom-call(bf16[8,160,256]{2,1,0:T(8,128)(2,1)} %get-tuple-element.54.q_ref, bf16[8,160,256]{2,1,0:T(8,128)(2,1)} %get-tuple-element.55.k_ref, bf16[8,160,256]{2,1,0:T(8,128)(2,1)} %get-tuple-element.56.v_ref, ...), custom_call_target="tpu_custom_call" | custom-call | tf_op jit(solution)/shard_map/slopes/pallas_call | solution.py:681
  223.2 2.7 convolution_convert_fusion.5
  226.0 2.8 convolution_convert_fusion.4
  228.8 3.0 convolution_convert_fusion.3
  231.8 77.5 %move_4.1 = (bf16[8,160,256]{2,1,0:T(8,128)(2,1)}, bf16[8,160,256]{2,1,0:T(8,128)(2,1)}, bf16[8,160,256]{2,1,0:T(8,128)(2,1)}, f32[40,1280]{1,0:T(8,128)}, bf16[...) custom-call(bf16[8,160,256]{2,1,0:T(8,128)(2,1)} %get-tuple-element.63.refs_0_, ...), custom_call_target="tpu_custom_call" | custom-call | tf_op jit(solution)/shard_map/move_4/pallas_call | solution.py:543
  309.4 3.3 fusion.11
  314.9 1.4 multiply_reduce_fusion.2
  316.3 1.2 add_convert_fusion
  317.5 2.8 convolution_convert_fusion.2
  320.3 2.8 convolution_convert_fusion.1
  323.1 2.8 convolution_convert_fusion
  327.5 1.8 multiply_reduce_fusion
  330.1 61.0 %move_5.1 = (f32[40,1280]{1,0:T(8,128)}, f32[40,1280]{1,0:T(8,128)}, f32[40,1280]{1,0:T(8,128)}, f32[40,1280]{1,0:T(8,128)}, f32[40,1280]{1,0:T(8,128)}, /*index=5*/f32[8,128]{1,0:T(8,128)}) custom-call(bf16[4,40,1280]{2,1,0:T(8,128)(2,1)} %get-tuple-element.69.refs_0_, bf16[4,40,1280]{2,1,0:T(8,128)(2,1)} %get-tuple-element.70.refs_1_, ...), custom_call_target="tpu_custom_call" | custom-call | tf_op jit(solution)/shard_map/move_5/pallas_call | solution.py:543
  391.2 1.5 slice_bitcast_fusion
  392.7 1.2 divide_multiply_fusion
  393.9 1.6 copy.44
  395.5 1.6 copy.45
  397.1 1.6 copy.46
  (92 shorter events, 14.0 us)
Async XLA Ops:
  0.6 68.8 %copy-start = (bf16[2,128,1,1280]{3,1,2,0:T(8,128)(2,1)S(1)}, bf16[2,128,1,1280]{3,1,2,0:T(8,128)(2,1)}, u32[]{:S(2)}) copy-start(bf16[2,128,1,1280]{3,1,2,0:T(8,128)(2,1)} %param.16) | copy-start | bytes 1966084
  69.9 4.6 %copy-start.5 = (bf16[2,2,4,2,40,1280]{5,4,3,2,1,0:T(8,128)(2,1)S(1)}, bf16[2,2,4,2,40,1280]{5,4,3,2,1,0:T(8,128)(2,1)}, u32[]{:S(2)}) copy-start(bf16[2,2,4,2,40,1280]{5,4,3,2,1,0:T(8,128)(2,1)} %get-tuple-element.49) | copy-start | bytes 9830404
  180.4 6.9 %copy-start.2 = (f32[256,1280]{1,0:T(8,128)}, f32[256,1280]{1,0:T(8,128)S(1)}, u32[]{:S(2)}) copy-start(f32[256,1280]{1,0:T(8,128)S(1)} %get-tuple-element.135) | copy-start | bytes 3932164
  180.6 3.2 copy-start.21
  183.9 2.1 copy-start.23
  183.9 2.1 copy-start.8
  186.0 1.9 copy-start.20
  187.2 1.9 copy-start.13
  189.1 2.3 copy-start.19
  193.3 18.2 %copy-start.22 = (bf16[80]{0:T(256)(128)(2,1)S(1)}, bf16[80]{0:T(256)(128)(2,1)}, u32[]{:S(2)}) copy-start(bf16[80]{0:T(256)(128)(2,1)} %param.31) | copy-start | bytes 484
  212.3 10.9 %copy-start.4 = (bf16[8,160,256]{2,1,0:T(8,128)(2,1)S(1)}, bf16[8,160,256]{2,1,0:T(8,128)(2,1)}, u32[]{:S(2)}) copy-start(bf16[8,160,256]{2,1,0:T(8,128)(2,1)} %move_2.1) | copy-start | bytes 1966084
  223.2 2.8 copy-start.3
  223.2 2.7 copy-start.14
  225.9 2.8 copy-start.9
  226.0 2.8 copy-start.24
  309.3 3.4 copy-start.6
  309.4 3.4 copy-start.7
  312.7 1.1 copy-start.11
  312.7 2.1 copy-start.18
  316.3 1.3 copy-start.1
  323.1 2.9 copy-start.12
  325.9 1.2 copy-start.10
  391.2 7.6 %copy-start.15 = (f32[40,1280]{1,0:T(8,128)S(1)}, f32[40,1280]{1,0:T(8,128)}, u32[]{:S(2)}) copy-start(f32[40,1280]{1,0:T(8,128)} %get-tuple-element.166) | copy-start | bytes 614404
  391.2 8.2 %copy-start.17 = (f32[40,1280]{1,0:T(8,128)S(1)}, f32[40,1280]{1,0:T(8,128)}, u32[]{:S(2)}) copy-start(f32[40,1280]{1,0:T(8,128)} %get-tuple-element.169) | copy-start | bytes 614404
  391.2 8.9 %copy-start.16 = (f32[40,1280]{1,0:T(8,128)S(1)}, f32[40,1280]{1,0:T(8,128)}, u32[]{:S(2)}) copy-start(f32[40,1280]{1,0:T(8,128)} %get-tuple-element.171) | copy-start | bytes 614404

commit v5 on v4

--- a/solution.py
+++ b/solution.py
@@ -16,7 +16,6 @@
 EPSILON = 1e-06
 MESH = pl.DeviceIdType.MESH
 VMEM_BYTES = 60 * 1024 * 1024
-FEED_STEPS = 4
 
 
 class Place:
@@ -465,6 +464,8 @@
     whole = swaps + gathers + scatters
     ins, outs, rest = refs[:whole], refs[whole : 2 * whole], refs[2 * whole :]
     own_sem, send_sem, recv_sem = rest[-3:]
+    staged = swaps > 0 and whole > swaps
+    relays, boxes = rest[: swaps * staged], rest[swaps * staged : -3]
     spot = place.here()
     dp, me = place.device(spot)
     devices = place.levels * place.across
@@ -479,18 +480,55 @@
         place, spot, lean, tails, ins[swaps:cut], outs[swaps:cut], [own_sem.at[n] for n in range(swaps, cut)]
     )
     scatter = Scatter(
-        place, spot, lean, held, ins[cut:], outs[cut:], rest[:-3], [own_sem.at[n] for n in range(cut, whole)]
-    )
-    place.greet(spot, swaps > 0)
+        place, spot, lean, held, ins[cut:], outs[cut:], boxes, [own_sem.at[n] for n in range(cut, whole)]
+    )
+    place.greet(spot, swaps > 0 and not staged)
     out = Sender(place, spot, send_sem, recv_sem)
-    pending = [(n, step) for n in range(swaps) for step in range(1, devices)]
-    each = pl.cdiv(len(pending), FEED_STEPS)
-
-    def feed():
-        for n, step in pending[:each]:
+    levels, across = place.levels, place.across
+    z, x = spot["z"], spot["x"]
+
+    def straight(n):
+        for step in range(1, devices):
             peer = lax.rem(me + step, devices)
             out.put("swap", (dp, peer), sent[n].at[peer], got[n].at[me])
-        del pending[:each]
+
+    def along_x(n):
+        for skip in range(1, across):
+            peer = place.shift(spot, "x", skip)
+            device = place.device(peer)
+            out.put("swap", device, sent[n].at[device[1]], got[n].at[me])
+            for step in range(1, levels):
+                piece = place.device(place.shift(peer, "z", step))[1]
+                out.put(
+                    ("relay", n), device, sent[n].at[piece], relays[n].at[skip - 1, step - 1]
+                )
+
+    def along_z(n):
+        for step in range(1, levels):
+            device = place.device(place.shift(spot, "z", step))
+            out.put("swap", device, sent[n].at[device[1]], got[n].at[me])
+
+    def pass_on(n):
+        out.landed(("relay", n))
+        for skip in range(1, across):
+            source = place.device(place.shift(spot, "x", across - skip))[1]
+            for step in range(1, levels):
+                device = place.device(place.shift(spot, "z", step))
+                out.put("swap", device, relays[n].at[skip - 1, step - 1], got[n].at[source])
+
+    if staged:
+        pending = []
+        for time in range(swaps + 2):
+            acts = [(pass_on, time - 2), (along_x, time), (along_z, time + 1)]
+            if time == 0:
+                acts.insert(0, (along_z, 0))
+            pending.append([(act, n) for act, n in acts if 0 <= n < swaps])
+    else:
+        pending = [[(straight, n)] for n in range(swaps)]
+
+    def feed():
+        for act, n in pending.pop(0) if pending else ():
+            act(n)
 
     if gathers:
         gather.run(out, feed)
@@ -507,9 +545,11 @@
 
 def move(place, collective_id, swaps=(), gathers=(), scatters=(), tails=0, held=0):
     lean = len(swaps) > 0
-    copies = len(swaps) * (place.levels * place.across - 1)
+    lines, cores, levels, across = place.grid()
+    copies = len(swaps) * (2 * levels * across - across - 1)
     boxes = []
-    lines, cores, levels, across = place.grid()
+    if len(swaps) > 0 and len(gathers) + len(scatters) > 0:
+        boxes += [pltpu.VMEM((across - 1, levels - 1) + a.shape[1:], a.dtype) for a in swaps]
     shapes = [jax.ShapeDtypeStruct(a.shape, a.dtype) for a in swaps]
     for n, shard in enumerate(gathers):
         rows, cols = shard.shape[-2:]

time: 401 us -> 395 us (0.985)
  Pallas kernels: 329 us -> 322 us
    pallas_call x6, Pallas kernels: 311 us -> 304 us  [move(): pl.pallas_call(functools.partial(move_kernel, place, (len(swaps), len(gat...]
where the time goes in v5:
time: 395 us; the launch traced here: 394 us
  Pallas kernels  322 us (82%)
  matrix products  46 us (12%)
  local copies, waits for them, and re-layouts  14.6 us (4%)
  other arithmetic  9.58 us (2%)
    pallas_call x6, Pallas kernels, move(): pl.pallas_call(functools.partial(move_kernel, place, (len(swaps), len(gat...  304 us
    dot_general x18, matrix products, contract(): return jnp.einsum(spec, left, right, preferred_element_type=jnp.float32)  46 us
    pallas_call x1, Pallas kernels, slopes(): pl.pallas_call(slopes_kernel, grid=grid, out_shape=[jax.ShapeDtypeStruct(...  10.9 us
    unnamed x56, local copies, waits for them, and re-layouts  9.1 us

profile of v5, /device:TPU:0, one launch (start us, length us, event | category | flops | bytes accessed | tf_op | source)
XLA Modules:
  0.0 393.8 jit_solution(5717412845612858649)
XLA Ops:
  2.1 65.1 %move_0.1 = (bf16[2,2,4,2,40,1280]{5,4,3,2,1,0:T(8,128)(2,1)}, bf16[2,2,4,2,16,128]{5,4,3,2,1,0:T(8,128)(2,1)}, bf16[2,2,4,2,40,1280]{5,4,3,2,1,0:T(8,128)(2,1)}...) custom-call(bf16[40,1280]{1,0:T(8,128)(2,1)} %refs_0_.1, ...), custom_call_target="tpu_custom_call" | custom-call | tf_op jit(solution)/shard_map/move_0/pallas_call | solution.py:583
  69.9 4.6 %multiply_convert_fusion.2 = (bf16[1280,256]{1,0:T(8,128)(2,1)}, f32[1280,256]{1,0:T(8,128)}) fusion(f32[1280]{0:T(1024)S(1)} %mul.163, f32[1280]{0:T(1024)S(1)} %add.108, bf16[1280,1280]{1,0:T(8,128)(2,1)} %bitcast.152, bf16[256,1280]{1,0:T(8,128)(2,1)S(1)} %bitcast.110), kind=kOutput, calls=%fused_computation.40 | convolution fusion | flops 839843840 | bytes 5908480 | tf_op jit(solution)/shard_map/df,rd->fr/dot_general | solution.py:738
  74.5 1.9 convolution_convert_fusion.7
  76.5 3.9 fusion.5
  80.4 77.7 %move_1.1 = (bf16[8,160,256]{2,1,0:T(8,128)(2,1)}, bf16[8,160,256]{2,1,0:T(8,128)(2,1)}, bf16[8,160,256]{2,1,0:T(8,128)(2,1)}, bf16[2,2,4,2,40,1280]{5,4,3,2,1,0...) custom-call(bf16[8,160,256]{2,1,0:T(8,128)(2,1)} %bitcast.137, ...), custom_call_target="tpu_custom_call" | custom-call | tf_op jit(solution)/shard_map/move_1/pallas_call | solution.py:583
  158.0 7.2 %attend.1 = (bf16[8,160,256]{2,1,0:T(8,128)(2,1)}, f32[8,160,256]{2,1,0:T(8,128)}, f32[2,2,1,1024]{3,2,1,0:T(1,128)}) custom-call(bf16[8,160,256]{2,1,0:T(8,128)(2,1)} %get-tuple-element.54.q_ref, bf16[8,160,256]{2,1,0:T(8,128)(2,1)} %get-tuple-element.55.k_ref, bf16[8,160,256]{2,1,0:T(8,128)(2,1)} %get-tuple-element.56.v_ref), custom_call_target="tpu_custom_call" | custom-call | tf_op jit(solution)/shard_map/attend/pallas_call | solution.py:657
  165.3 14.8 %move_2.1 = bf16[8,160,256]{2,1,0:T(8,128)(2,1)} custom-call(bf16[8,160,256]{2,1,0:T(8,128)(2,1)} %get-tuple-element.57.refs_0_), custom_call_target="tpu_custom_call" | custom-call | tf_op jit(solution)/shard_map/move_2/pallas_call | solution.py:583
  180.1 3.3 multiply_reduce_fusion.5
  183.7 3.2 convolution_add_fusion.3
  187.0 2.1 fusion.6
  189.0 1.2 convert_reduce_fusion.1
  192.2 1.9 convert_reduce_fusion.2
  194.5 1.9 convolution_convert_fusion.6
  196.4 17.6 %move_3.1.do_ref = bf16[8,160,256]{2,1,0:T(8,128)(2,1)} custom-call(bf16[8,160,256]{2,1,0:T(8,128)(2,1)} %bitcast.136), custom_call_target="tpu_custom_call" | custom-call | tf_op jit(solution)/shard_map/move_3/pallas_call | solution.py:583
  214.8 10.9 %slopes.1 = (bf16[8,160,256]{2,1,0:T(8,128)(2,1)}, bf16[8,160,256]{2,1,0:T(8,128)(2,1)}, bf16[8,160,256]{2,1,0:T(8,128)(2,1)}) custom-call(bf16[8,160,256]{2,1,0:T(8,128)(2,1)} %get-tuple-element.54.q_ref, bf16[8,160,256]{2,1,0:T(8,128)(2,1)} %get-tuple-element.55.k_ref, bf16[8,160,256]{2,1,0:T(8,128)(2,1)} %get-tuple-element.56.v_ref, ...), custom_call_target="tpu_custom_call" | custom-call | tf_op jit(solution)/shard_map/slopes/pallas_call | solution.py:721
  225.7 2.7 convolution_convert_fusion.5
  228.5 2.8 convolution_convert_fusion.4
  231.3 3.0 convolution_convert_fusion.3
  234.3 69.1 %move_4.1 = (bf16[8,160,256]{2,1,0:T(8,128)(2,1)}, bf16[8,160,256]{2,1,0:T(8,128)(2,1)}, bf16[8,160,256]{2,1,0:T(8,128)(2,1)}, f32[40,1280]{1,0:T(8,128)}, bf16[...) custom-call(bf16[8,160,256]{2,1,0:T(8,128)(2,1)} %get-tuple-element.63.refs_0_, ...), custom_call_target="tpu_custom_call" | custom-call | tf_op jit(solution)/shard_map/move_4/pallas_call | solution.py:583
  303.5 3.3 fusion.11
  309.0 1.4 multiply_reduce_fusion.2
  310.4 1.2 add_convert_fusion
  311.6 2.8 convolution_convert_fusion.2
  314.4 2.8 convolution_convert_fusion.1
  317.2 2.8 convolution_convert_fusion
  321.6 1.8 multiply_reduce_fusion
  324.2 60.0 %move_5.1 = (f32[40,1280]{1,0:T(8,128)}, f32[40,1280]{1,0:T(8,128)}, f32[40,1280]{1,0:T(8,128)}, f32[40,1280]{1,0:T(8,128)}, f32[40,1280]{1,0:T(8,128)}, /*index=5*/f32[8,128]{1,0:T(8,128)}) custom-call(bf16[4,40,1280]{2,1,0:T(8,128)(2,1)} %get-tuple-element.69.refs_0_, bf16[4,40,1280]{2,1,0:T(8,128)(2,1)} %get-tuple-element.70.refs_1_, ...), custom_call_target="tpu_custom_call" | custom-call | tf_op jit(solution)/shard_map/move_5/pallas_call | solution.py:583
  384.2 1.5 slice_bitcast_fusion
  385.7 1.2 divide_multiply_fusion
  386.9 1.6 copy.44
  388.5 1.6 copy.45
  390.1 1.6 copy.46
  (92 shorter events, 14.0 us)
Async XLA Ops:
  0.6 68.8 %copy-start = (bf16[2,128,1,1280]{3,1,2,0:T(8,128)(2,1)S(1)}, bf16[2,128,1,1280]{3,1,2,0:T(8,128)(2,1)}, u32[]{:S(2)}) copy-start(bf16[2,128,1,1280]{3,1,2,0:T(8,128)(2,1)} %param.16) | copy-start | bytes 1966084
  69.9 4.6 %copy-start.5 = (bf16[2,2,4,2,40,1280]{5,4,3,2,1,0:T(8,128)(2,1)S(1)}, bf16[2,2,4,2,40,1280]{5,4,3,2,1,0:T(8,128)(2,1)}, u32[]{:S(2)}) copy-start(bf16[2,2,4,2,40,1280]{5,4,3,2,1,0:T(8,128)(2,1)} %get-tuple-element.49) | copy-start | bytes 9830404
  183.4 6.9 %copy-start.2 = (f32[256,1280]{1,0:T(8,128)}, f32[256,1280]{1,0:T(8,128)S(1)}, u32[]{:S(2)}) copy-start(f32[256,1280]{1,0:T(8,128)S(1)} %get-tuple-element.135) | copy-start | bytes 3932164
  183.7 3.2 copy-start.21
  186.9 2.1 copy-start.23
  187.0 2.1 copy-start.8
  189.0 1.9 copy-start.20
  190.3 1.9 copy-start.13
  192.2 2.3 copy-start.19
  196.4 17.6 %copy-start.22 = (bf16[80]{0:T(256)(128)(2,1)S(1)}, bf16[80]{0:T(256)(128)(2,1)}, u32[]{:S(2)}) copy-start(bf16[80]{0:T(256)(128)(2,1)} %param.31) | copy-start | bytes 484
  214.8 10.9 %copy-start.4 = (bf16[8,160,256]{2,1,0:T(8,128)(2,1)S(1)}, bf16[8,160,256]{2,1,0:T(8,128)(2,1)}, u32[]{:S(2)}) copy-start(bf16[8,160,256]{2,1,0:T(8,128)(2,1)} %move_2.1) | copy-start | bytes 1966084
  225.7 2.8 copy-start.3
  225.7 2.7 copy-start.14
  228.5 2.8 copy-start.9
  228.5 2.8 copy-start.24
  303.5 3.4 copy-start.6
  303.5 3.4 copy-start.7
  306.8 1.1 copy-start.11
  306.9 2.1 copy-start.18
  310.4 1.3 copy-start.1
  317.2 2.9 copy-start.12
  320.0 1.2 copy-start.10
  384.2 7.6 %copy-start.15 = (f32[40,1280]{1,0:T(8,128)S(1)}, f32[40,1280]{1,0:T(8,128)}, u32[]{:S(2)}) copy-start(f32[40,1280]{1,0:T(8,128)} %get-tuple-element.166) | copy-start | bytes 614404
  384.2 8.2 %copy-start.17 = (f32[40,1280]{1,0:T(8,128)S(1)}, f32[40,1280]{1,0:T(8,128)}, u32[]{:S(2)}) copy-start(f32[40,1280]{1,0:T(8,128)} %get-tuple-element.169) | copy-start | bytes 614404
  384.2 8.9 %copy-start.16 = (f32[40,1280]{1,0:T(8,128)S(1)}, f32[40,1280]{1,0:T(8,128)}, u32[]{:S(2)}) copy-start(f32[40,1280]{1,0:T(8,128)} %get-tuple-element.171) | copy-start | bytes 614404

commit v6 on v5

--- a/solution.py
+++ b/solution.py
@@ -81,11 +81,11 @@
     return ((slice(0, cut), "xy"), (slice(cut, cols), "yx"))
 
 
-def chunks_of(rows):
-    if rows % 8 == 0 and rows >= 32:
-        cut = rows // 32 * 16
-        return (slice(0, cut), slice(cut, rows))
-    return (slice(0, rows),)
+def chunks_of(rows, first=0):
+    if rows % 8 or rows < 32:
+        return (slice(0, rows),)
+    starts = [0] + list(range(first or 16, rows, 16))
+    return tuple(slice(p, q) for p, q in zip(starts, starts[1:] + [rows]))
 
 
 class Sender:
@@ -176,7 +176,7 @@
         turns = self.place.levels - 1
         full = len(shards) - self.tails
         raw = [n for n, s in enumerate(shards) if len(s.shape) == 2]
-        jobs = [(n, r) for n in range(full) for r in chunks_of(shards[n].shape[-2])]
+        jobs = [(n, r) for n in range(full) for r in chunks_of(shards[n].shape[-2], 8)]
         filled = set()
 
         def halves(n):
@@ -241,7 +241,7 @@
                         along(turn, raw[time - turn])
                 done = time - turns
                 if 0 <= done < full:
-                    for _ in chunks_of(shards[raw[done]].shape[-2]):
+                    for _ in chunks_of(shards[raw[done]].shape[-2], 8):
                         advance()
         for _ in range(len(jobs) + 3):
             advance()
@@ -517,12 +517,13 @@
                 out.put("swap", device, relays[n].at[skip - 1, step - 1], got[n].at[source])
 
     if staged:
-        pending = []
-        for time in range(swaps + 2):
-            acts = [(pass_on, time - 2), (along_x, time), (along_z, time + 1)]
-            if time == 0:
-                acts.insert(0, (along_z, 0))
-            pending.append([(act, n) for act, n in acts if 0 <= n < swaps])
+        apart = 3 if gathers else 1
+        pending = [[] for _ in range(apart * (swaps - 1) + 3)]
+        for n in range(swaps):
+            pending[0 if gathers else max(n - 1, 0)].append((along_z, n))
+        for n in range(swaps):
+            pending[apart * n].append((along_x, n))
+            pending[apart * n + 2].append((pass_on, n))
     else:
         pending = [[(straight, n)] for n in range(swaps)]
 
@@ -558,7 +559,7 @@
         grid = place.grid()
         if n < len(gathers) - tails:
             count = len(halves_of(cols, lean)) * (across + lines + cores - 3)
-            copies += len(chunks_of(rows)) * count
+            copies += len(chunks_of(rows, 8)) * count
         else:
             grid = (levels,)
         shapes.append(jax.ShapeDtypeStruct(grid + (rows, cols), shard.dtype))

time: 395 us -> 416 us (1.053)
  Pallas kernels: 322 us -> 344 us
    pallas_call x6, Pallas kernels: 304 us -> 326 us  [move(): pl.pallas_call(functools.partial(move_kernel, place, (len(swaps), len(gat...]
where the time goes in v6:
time: 416 us
  Pallas kernels  344 us (83%)
  matrix products  46.1 us (11%)
  local copies, waits for them, and re-layouts  14.6 us (4%)
  other arithmetic  9.58 us (2%)
    pallas_call x6, Pallas kernels, move(): pl.pallas_call(functools.partial(move_kernel, place, (len(swaps), len(gat...  326 us
    dot_general x18, matrix products, contract(): return jnp.einsum(spec, left, right, preferred_element_type=jnp.float32)  46.1 us
    pallas_call x1, Pallas kernels, slopes(): pl.pallas_call(slopes_kernel, grid=grid, out_shape=[jax.ShapeDtypeStruct(...  10.9 us
    unnamed x56, local copies, waits for them, and re-layouts  9.09 us

profile of v6, /device:TPU:0, one launch (start us, length us, event | category | flops | bytes accessed | tf_op | source)
XLA Modules:
  0.0 415.8 jit_solution(12343470367969224830)
XLA Ops:
  2.1 68.9 %move_0.1 = (bf16[2,2,4,2,40,1280]{5,4,3,2,1,0:T(8,128)(2,1)}, bf16[2,2,4,2,16,128]{5,4,3,2,1,0:T(8,128)(2,1)}, bf16[2,2,4,2,40,1280]{5,4,3,2,1,0:T(8,128)(2,1)}...) custom-call(bf16[40,1280]{1,0:T(8,128)(2,1)} %refs_0_.1, ...), custom_call_target="tpu_custom_call" | custom-call | tf_op jit(solution)/shard_map/move_0/pallas_call | solution.py:584
  73.7 4.6 %multiply_convert_fusion.2 = (bf16[1280,256]{1,0:T(8,128)(2,1)}, f32[1280,256]{1,0:T(8,128)}) fusion(f32[1280]{0:T(1024)S(1)} %mul.163, f32[1280]{0:T(1024)S(1)} %add.108, bf16[1280,1280]{1,0:T(8,128)(2,1)} %bitcast.152, bf16[256,1280]{1,0:T(8,128)(2,1)S(1)} %bitcast.110), kind=kOutput, calls=%fused_computation.40 | convolution fusion | flops 839843840 | bytes 5908480 | tf_op jit(solution)/shard_map/df,rd->fr/dot_general | solution.py:739
  78.3 1.9 convolution_convert_fusion.7
  80.3 3.9 fusion.5
  84.2 77.4 %move_1.1 = (bf16[8,160,256]{2,1,0:T(8,128)(2,1)}, bf16[8,160,256]{2,1,0:T(8,128)(2,1)}, bf16[8,160,256]{2,1,0:T(8,128)(2,1)}, bf16[2,2,4,2,40,1280]{5,4,3,2,1,0...) custom-call(bf16[8,160,256]{2,1,0:T(8,128)(2,1)} %bitcast.137, ...), custom_call_target="tpu_custom_call" | custom-call | tf_op jit(solution)/shard_map/move_1/pallas_call | solution.py:584
  161.6 7.2 %attend.1 = (bf16[8,160,256]{2,1,0:T(8,128)(2,1)}, f32[8,160,256]{2,1,0:T(8,128)}, f32[2,2,1,1024]{3,2,1,0:T(1,128)}) custom-call(bf16[8,160,256]{2,1,0:T(8,128)(2,1)} %get-tuple-element.54.q_ref, bf16[8,160,256]{2,1,0:T(8,128)(2,1)} %get-tuple-element.55.k_ref, bf16[8,160,256]{2,1,0:T(8,128)(2,1)} %get-tuple-element.56.v_ref), custom_call_target="tpu_custom_call" | custom-call | tf_op jit(solution)/shard_map/attend/pallas_call | solution.py:658
  168.8 14.8 %move_2.1 = bf16[8,160,256]{2,1,0:T(8,128)(2,1)} custom-call(bf16[8,160,256]{2,1,0:T(8,128)(2,1)} %get-tuple-element.57.refs_0_), custom_call_target="tpu_custom_call" | custom-call | tf_op jit(solution)/shard_map/move_2/pallas_call | solution.py:584
  183.6 3.3 multiply_reduce_fusion.5
  187.3 3.2 convolution_add_fusion.3
  190.5 2.1 fusion.6
  192.6 1.2 convert_reduce_fusion.1
  194.5 1.2 multiply_reduce_fusion.1
  195.8 1.9 convert_reduce_fusion.2
  198.1 1.9 convolution_convert_fusion.6
  200.0 18.2 %move_3.1.do_ref = bf16[8,160,256]{2,1,0:T(8,128)(2,1)} custom-call(bf16[8,160,256]{2,1,0:T(8,128)(2,1)} %bitcast.136), custom_call_target="tpu_custom_call" | custom-call | tf_op jit(solution)/shard_map/move_3/pallas_call | solution.py:584
  218.9 10.9 %slopes.1 = (bf16[8,160,256]{2,1,0:T(8,128)(2,1)}, bf16[8,160,256]{2,1,0:T(8,128)(2,1)}, bf16[8,160,256]{2,1,0:T(8,128)(2,1)}) custom-call(bf16[8,160,256]{2,1,0:T(8,128)(2,1)} %get-tuple-element.54.q_ref, bf16[8,160,256]{2,1,0:T(8,128)(2,1)} %get-tuple-element.55.k_ref, bf16[8,160,256]{2,1,0:T(8,128)(2,1)} %get-tuple-element.56.v_ref, ...), custom_call_target="tpu_custom_call" | custom-call | tf_op jit(solution)/shard_map/slopes/pallas_call | solution.py:722
  229.8 2.7 convolution_convert_fusion.5
  232.6 2.8 convolution_convert_fusion.4
  235.4 3.0 convolution_convert_fusion.3
  238.4 81.6 %move_4.1 = (bf16[8,160,256]{2,1,0:T(8,128)(2,1)}, bf16[8,160,256]{2,1,0:T(8,128)(2,1)}, bf16[8,160,256]{2,1,0:T(8,128)(2,1)}, f32[40,1280]{1,0:T(8,128)}, bf16[...) custom-call(bf16[8,160,256]{2,1,0:T(8,128)(2,1)} %get-tuple-element.63.refs_0_, ...), custom_call_target="tpu_custom_call" | custom-call | tf_op jit(solution)/shard_map/move_4/pallas_call | solution.py:584
  320.0 3.3 fusion.11
  325.5 1.4 multiply_reduce_fusion.2
  326.9 1.2 add_convert_fusion
  328.2 2.8 convolution_convert_fusion.2
  330.9 2.8 convolution_convert_fusion.1
  333.7 2.8 convolution_convert_fusion
  338.2 1.8 multiply_reduce_fusion
  340.8 65.4 %move_5.1 = (f32[40,1280]{1,0:T(8,128)}, f32[40,1280]{1,0:T(8,128)}, f32[40,1280]{1,0:T(8,128)}, f32[40,1280]{1,0:T(8,128)}, f32[40,1280]{1,0:T(8,128)}, /*index=5*/f32[8,128]{1,0:T(8,128)}) custom-call(bf16[4,40,1280]{2,1,0:T(8,128)(2,1)} %get-tuple-element.69.refs_0_, bf16[4,40,1280]{2,1,0:T(8,128)(2,1)} %get-tuple-element.70.refs_1_, ...), custom_call_target="tpu_custom_call" | custom-call | tf_op jit(solution)/shard_map/move_5/pallas_call | solution.py:584
  406.2 1.5 slice_bitcast_fusion
  408.8 1.6 copy.44
  410.5 1.6 copy.45
  412.1 1.6 copy.46
  (92 shorter events, 14.0 us)
Async XLA Ops:
  0.6 72.6 %copy-start = (bf16[2,128,1,1280]{3,1,2,0:T(8,128)(2,1)S(1)}, bf16[2,128,1,1280]{3,1,2,0:T(8,128)(2,1)}, u32[]{:S(2)}) copy-start(bf16[2,128,1,1280]{3,1,2,0:T(8,128)(2,1)} %param.16) | copy-start | bytes 1966084
  73.7 4.6 %copy-start.5 = (bf16[2,2,4,2,40,1280]{5,4,3,2,1,0:T(8,128)(2,1)S(1)}, bf16[2,2,4,2,40,1280]{5,4,3,2,1,0:T(8,128)(2,1)}, u32[]{:S(2)}) copy-start(bf16[2,2,4,2,40,1280]{5,4,3,2,1,0:T(8,128)(2,1)} %get-tuple-element.49) | copy-start | bytes 9830404
  187.0 6.9 %copy-start.2 = (f32[256,1280]{1,0:T(8,128)}, f32[256,1280]{1,0:T(8,128)S(1)}, u32[]{:S(2)}) copy-start(f32[256,1280]{1,0:T(8,128)S(1)} %get-tuple-element.135) | copy-start | bytes 3932164
  187.2 3.2 copy-start.21
  190.5 2.1 copy-start.23
  190.5 2.1 copy-start.8
  192.6 1.9 copy-start.20
  193.8 1.9 copy-start.13
  195.7 2.3 copy-start.19
  200.0 18.2 %copy-start.22 = (bf16[80]{0:T(256)(128)(2,1)S(1)}, bf16[80]{0:T(256)(128)(2,1)}, u32[]{:S(2)}) copy-start(bf16[80]{0:T(256)(128)(2,1)} %param.31) | copy-start | bytes 484
  218.9 10.9 %copy-start.4 = (bf16[8,160,256]{2,1,0:T(8,128)(2,1)S(1)}, bf16[8,160,256]{2,1,0:T(8,128)(2,1)}, u32[]{:S(2)}) copy-start(bf16[8,160,256]{2,1,0:T(8,128)(2,1)} %move_2.1) | copy-start | bytes 1966084
  229.8 2.8 copy-start.3
  229.8 2.7 copy-start.14
  232.5 2.8 copy-start.9
  232.5 2.8 copy-start.24
  320.0 3.4 copy-start.6
  320.0 3.4 copy-start.7
  323.4 1.1 copy-start.11
  323.4 2.1 copy-start.18
  326.9 1.3 copy-start.1
  333.7 2.9 copy-start.12
  336.6 1.2 copy-start.10
  406.1 7.6 %copy-start.15 = (f32[40,1280]{1,0:T(8,128)S(1)}, f32[40,1280]{1,0:T(8,128)}, u32[]{:S(2)}) copy-start(f32[40,1280]{1,0:T(8,128)} %get-tuple-element.166) | copy-start | bytes 614404
  406.1 8.2 %copy-start.17 = (f32[40,1280]{1,0:T(8,128)S(1)}, f32[40,1280]{1,0:T(8,128)}, u32[]{:S(2)}) copy-start(f32[40,1280]{1,0:T(8,128)} %get-tuple-element.169) | copy-start | bytes 614404
  406.2 8.9 %copy-start.16 = (f32[40,1280]{1,0:T(8,128)S(1)}, f32[40,1280]{1,0:T(8,128)}, u32[]{:S(2)}) copy-start(f32[40,1280]{1,0:T(8,128)} %get-tuple-element.171) | copy-start | bytes 614404

commit v7 on v5

--- a/solution.py
+++ b/solution.py
@@ -16,6 +16,7 @@
 EPSILON = 1e-06
 MESH = pl.DeviceIdType.MESH
 VMEM_BYTES = 60 * 1024 * 1024
+LAG = 2
 
 
 class Place:
@@ -225,12 +226,12 @@
             for half, _ in halves(n):
                 out.landed((job, half, 4))
 
-        steps = iter(range(len(jobs) + 3))
+        steps = iter(range(len(jobs) + 3 * LAG))
 
         def advance():
             step = next(steps, None)
             if step is not None:
-                for stage, late in ((two, 0), (three, 1), (four, 2), (five, 3)):
+                for stage, late in ((two, 0), (three, LAG), (four, 2 * LAG), (five, 3 * LAG)):
                     if 0 <= step - late < len(jobs):
                         stage(("gather", step - late), *jobs[step - late])
 
@@ -243,7 +244,7 @@
                 if 0 <= done < full:
                     for _ in chunks_of(shards[raw[done]].shape[-2]):
                         advance()
-        for _ in range(len(jobs) + 3):
+        for _ in range(len(jobs) + 3 * LAG):
             advance()
             feed()
         for n in range(len(shards)):
@@ -422,10 +423,11 @@
         tails = [n for n, p in enumerate(parts) if len(p.shape) == 3]
         for n in tails:
             first(n)
-        for step in range(len(jobs) + 4):
+        for step in range(len(jobs) + 4 * LAG):
             if step > 2 and tails:
                 final(tails.pop(0))
-            for stage, late in ((one, 0), (two, 1), (three, 2), (four, 3), (five, 4)):
+            for turn, stage in enumerate((one, two, three, four, five)):
+                late = turn * LAG
                 if 0 <= step - late < len(jobs):
                     stage(*jobs[step - late])
             feed()
@@ -517,12 +519,13 @@
                 out.put("swap", device, relays[n].at[skip - 1, step - 1], got[n].at[source])
 
     if staged:
-        pending = []
-        for time in range(swaps + 2):
-            acts = [(pass_on, time - 2), (along_x, time), (along_z, time + 1)]
-            if time == 0:
-                acts.insert(0, (along_z, 0))
-            pending.append([(act, n) for act, n in acts if 0 <= n < swaps])
+        apart = 2 if gathers else 1
+        pending = [[] for _ in range(apart * (swaps - 1) + LAG + 2)]
+        for n in range(swaps):
+            pending[0 if gathers else max(n - 1, 0)].append((along_z, n))
+        for n in range(swaps):
+            pending[apart * n].append((along_x, n))
+            pending[apart * n + LAG + 1].append((pass_on, n))
     else:
         pending = [[(straight, n)] for n in range(swaps)]
 

time: 395 us -> 391 us (0.990)
  no operation moved by 1% of the time
where the time goes in v7:
time: 391 us; the launch traced here: 390 us
  Pallas kernels  319 us (82%)
  matrix products  46 us (12%)
  local copies, waits for them, and re-layouts  14.6 us (4%)
  other arithmetic  9.58 us (2%)
    pallas_call x6, Pallas kernels, move(): pl.pallas_call(functools.partial(move_kernel, place, (len(swaps), len(gat...  301 us
    dot_general x18, matrix products, contract(): return jnp.einsum(spec, left, right, preferred_element_type=jnp.float32)  46 us
    pallas_call x1, Pallas kernels, slopes(): pl.pallas_call(slopes_kernel, grid=grid, out_shape=[jax.ShapeDtypeStruct(...  10.9 us
    unnamed x56, local copies, waits for them, and re-layouts  9.1 us

profile of v7, /device:TPU:0, one launch (start us, length us, event | category | flops | bytes accessed | tf_op | source)
XLA Modules:
  0.0 390.4 jit_solution(16195943506813260971)
XLA Ops:
  2.1 65.4 %move_0.1 = (bf16[2,2,4,2,40,1280]{5,4,3,2,1,0:T(8,128)(2,1)}, bf16[2,2,4,2,16,128]{5,4,3,2,1,0:T(8,128)(2,1)}, bf16[2,2,4,2,40,1280]{5,4,3,2,1,0:T(8,128)(2,1)}...) custom-call(bf16[40,1280]{1,0:T(8,128)(2,1)} %refs_0_.1, ...), custom_call_target="tpu_custom_call" | custom-call | tf_op jit(solution)/shard_map/move_0/pallas_call | solution.py:586
  70.2 4.6 %multiply_convert_fusion.2 = (bf16[1280,256]{1,0:T(8,128)(2,1)}, f32[1280,256]{1,0:T(8,128)}) fusion(f32[1280]{0:T(1024)S(1)} %mul.163, f32[1280]{0:T(1024)S(1)} %add.108, bf16[1280,1280]{1,0:T(8,128)(2,1)} %bitcast.152, bf16[256,1280]{1,0:T(8,128)(2,1)S(1)} %bitcast.110), kind=kOutput, calls=%fused_computation.40 | convolution fusion | flops 839843840 | bytes 5908480 | tf_op jit(solution)/shard_map/df,rd->fr/dot_general | solution.py:741
  74.7 1.9 convolution_convert_fusion.7
  76.7 3.9 fusion.5
  80.6 71.9 %move_1.1 = (bf16[8,160,256]{2,1,0:T(8,128)(2,1)}, bf16[8,160,256]{2,1,0:T(8,128)(2,1)}, bf16[8,160,256]{2,1,0:T(8,128)(2,1)}, bf16[2,2,4,2,40,1280]{5,4,3,2,1,0...) custom-call(bf16[8,160,256]{2,1,0:T(8,128)(2,1)} %bitcast.137, ...), custom_call_target="tpu_custom_call" | custom-call | tf_op jit(solution)/shard_map/move_1/pallas_call | solution.py:586
  152.6 7.2 %attend.1 = (bf16[8,160,256]{2,1,0:T(8,128)(2,1)}, f32[8,160,256]{2,1,0:T(8,128)}, f32[2,2,1,1024]{3,2,1,0:T(1,128)}) custom-call(bf16[8,160,256]{2,1,0:T(8,128)(2,1)} %get-tuple-element.54.q_ref, bf16[8,160,256]{2,1,0:T(8,128)(2,1)} %get-tuple-element.55.k_ref, bf16[8,160,256]{2,1,0:T(8,128)(2,1)} %get-tuple-element.56.v_ref), custom_call_target="tpu_custom_call" | custom-call | tf_op jit(solution)/shard_map/attend/pallas_call | solution.py:660
  159.8 14.8 %move_2.1 = bf16[8,160,256]{2,1,0:T(8,128)(2,1)} custom-call(bf16[8,160,256]{2,1,0:T(8,128)(2,1)} %get-tuple-element.57.refs_0_), custom_call_target="tpu_custom_call" | custom-call | tf_op jit(solution)/shard_map/move_2/pallas_call | solution.py:586
  174.6 3.3 multiply_reduce_fusion.5
  178.2 3.2 convolution_add_fusion.3
  181.5 2.1 fusion.6
  183.6 1.2 convert_reduce_fusion.1
  186.7 1.9 convert_reduce_fusion.2
  189.1 1.9 convolution_convert_fusion.6
  191.0 18.5 %move_3.1.do_ref = bf16[8,160,256]{2,1,0:T(8,128)(2,1)} custom-call(bf16[8,160,256]{2,1,0:T(8,128)(2,1)} %bitcast.136), custom_call_target="tpu_custom_call" | custom-call | tf_op jit(solution)/shard_map/move_3/pallas_call | solution.py:586
  210.2 10.9 %slopes.1 = (bf16[8,160,256]{2,1,0:T(8,128)(2,1)}, bf16[8,160,256]{2,1,0:T(8,128)(2,1)}, bf16[8,160,256]{2,1,0:T(8,128)(2,1)}) custom-call(bf16[8,160,256]{2,1,0:T(8,128)(2,1)} %get-tuple-element.54.q_ref, bf16[8,160,256]{2,1,0:T(8,128)(2,1)} %get-tuple-element.55.k_ref, bf16[8,160,256]{2,1,0:T(8,128)(2,1)} %get-tuple-element.56.v_ref, ...), custom_call_target="tpu_custom_call" | custom-call | tf_op jit(solution)/shard_map/slopes/pallas_call | solution.py:724
  221.1 2.7 convolution_convert_fusion.5
  223.9 2.8 convolution_convert_fusion.4
  226.7 3.0 convolution_convert_fusion.3
  229.7 65.0 %move_4.1 = (bf16[8,160,256]{2,1,0:T(8,128)(2,1)}, bf16[8,160,256]{2,1,0:T(8,128)(2,1)}, bf16[8,160,256]{2,1,0:T(8,128)(2,1)}, f32[40,1280]{1,0:T(8,128)}, bf16[...) custom-call(bf16[8,160,256]{2,1,0:T(8,128)(2,1)} %get-tuple-element.63.refs_0_, ...), custom_call_target="tpu_custom_call" | custom-call | tf_op jit(solution)/shard_map/move_4/pallas_call | solution.py:586
  294.8 3.3 fusion.11
  300.3 1.4 multiply_reduce_fusion.2
  301.7 1.2 add_convert_fusion
  302.9 2.8 convolution_convert_fusion.2
  305.7 2.8 convolution_convert_fusion.1
  308.5 2.8 convolution_convert_fusion
  312.9 1.8 multiply_reduce_fusion
  315.5 65.3 %move_5.1 = (f32[40,1280]{1,0:T(8,128)}, f32[40,1280]{1,0:T(8,128)}, f32[40,1280]{1,0:T(8,128)}, f32[40,1280]{1,0:T(8,128)}, f32[40,1280]{1,0:T(8,128)}, /*index=5*/f32[8,128]{1,0:T(8,128)}) custom-call(bf16[4,40,1280]{2,1,0:T(8,128)(2,1)} %get-tuple-element.69.refs_0_, bf16[4,40,1280]{2,1,0:T(8,128)(2,1)} %get-tuple-element.70.refs_1_, ...), custom_call_target="tpu_custom_call" | custom-call | tf_op jit(solution)/shard_map/move_5/pallas_call | solution.py:586
  380.8 1.5 slice_bitcast_fusion
  382.3 1.2 divide_multiply_fusion
  383.5 1.6 copy.44
  385.1 1.6 copy.45
  386.7 1.6 copy.46
  (92 shorter events, 14.0 us)
Async XLA Ops:
  0.6 69.0 %copy-start = (bf16[2,128,1,1280]{3,1,2,0:T(8,128)(2,1)S(1)}, bf16[2,128,1,1280]{3,1,2,0:T(8,128)(2,1)}, u32[]{:S(2)}) copy-start(bf16[2,128,1,1280]{3,1,2,0:T(8,128)(2,1)} %param.16) | copy-start | bytes 1966084
  70.1 4.6 %copy-start.5 = (bf16[2,2,4,2,40,1280]{5,4,3,2,1,0:T(8,128)(2,1)S(1)}, bf16[2,2,4,2,40,1280]{5,4,3,2,1,0:T(8,128)(2,1)}, u32[]{:S(2)}) copy-start(bf16[2,2,4,2,40,1280]{5,4,3,2,1,0:T(8,128)(2,1)} %get-tuple-element.49) | copy-start | bytes 9830404
  178.0 6.9 %copy-start.2 = (f32[256,1280]{1,0:T(8,128)}, f32[256,1280]{1,0:T(8,128)S(1)}, u32[]{:S(2)}) copy-start(f32[256,1280]{1,0:T(8,128)S(1)} %get-tuple-element.135) | copy-start | bytes 3932164
  178.2 3.2 copy-start.21
  181.5 2.1 copy-start.23
  181.5 2.1 copy-start.8
  183.6 1.9 copy-start.20
  184.8 1.9 copy-start.13
  186.7 2.3 copy-start.19
  191.0 18.5 %copy-start.22 = (bf16[80]{0:T(256)(128)(2,1)S(1)}, bf16[80]{0:T(256)(128)(2,1)}, u32[]{:S(2)}) copy-start(bf16[80]{0:T(256)(128)(2,1)} %param.31) | copy-start | bytes 484
  210.2 10.9 %copy-start.4 = (bf16[8,160,256]{2,1,0:T(8,128)(2,1)S(1)}, bf16[8,160,256]{2,1,0:T(8,128)(2,1)}, u32[]{:S(2)}) copy-start(bf16[8,160,256]{2,1,0:T(8,128)(2,1)} %move_2.1) | copy-start | bytes 1966084
  221.1 2.8 copy-start.3
  221.1 2.7 copy-start.14
  223.9 2.8 copy-start.9
  223.9 2.8 copy-start.24
  294.8 3.4 copy-start.6
  294.8 3.4 copy-start.7
  298.1 1.1 copy-start.11
  298.2 2.1 copy-start.18
  301.7 1.3 copy-start.1
  308.5 2.9 copy-start.12
  311.3 1.2 copy-start.10
  380.8 7.6 %copy-start.15 = (f32[40,1280]{1,0:T(8,128)S(1)}, f32[40,1280]{1,0:T(8,128)}, u32[]{:S(2)}) copy-start(f32[40,1280]{1,0:T(8,128)} %get-tuple-element.166) | copy-start | bytes 614404
  380.8 8.2 %copy-start.17 = (f32[40,1280]{1,0:T(8,128)S(1)}, f32[40,1280]{1,0:T(8,128)}, u32[]{:S(2)}) copy-start(f32[40,1280]{1,0:T(8,128)} %get-tuple-element.169) | copy-start | bytes 614404
  380.8 8.9 %copy-start.16 = (f32[40,1280]{1,0:T(8,128)S(1)}, f32[40,1280]{1,0:T(8,128)}, u32[]{:S(2)}) copy-start(f32[40,1280]{1,0:T(8,128)} %get-tuple-element.171) | copy-start | bytes 614404

commit v8 on v7

--- a/solution.py
+++ b/solution.py
@@ -82,9 +82,11 @@
     return ((slice(0, cut), "xy"), (slice(cut, cols), "yx"))
 
 
-def chunks_of(rows):
+def chunks_of(rows, short_last=False):
     if rows % 8 == 0 and rows >= 32:
         cut = rows // 32 * 16
+        if short_last:
+            cut = rows - cut
         return (slice(0, cut), slice(cut, rows))
     return (slice(0, rows),)
 
@@ -177,7 +179,7 @@
         turns = self.place.levels - 1
         full = len(shards) - self.tails
         raw = [n for n, s in enumerate(shards) if len(s.shape) == 2]
-        jobs = [(n, r) for n in range(full) for r in chunks_of(shards[n].shape[-2])]
+        jobs = [(n, r) for n in range(full) for r in chunks_of(shards[n].shape[-2], True)]
         filled = set()
 
         def halves(n):
@@ -423,11 +425,12 @@
         tails = [n for n, p in enumerate(parts) if len(p.shape) == 3]
         for n in tails:
             first(n)
-        for step in range(len(jobs) + 4 * LAG):
+        lag = LAG if self.lean else 1
+        for step in range(len(jobs) + 4 * lag):
             if step > 2 and tails:
                 final(tails.pop(0))
             for turn, stage in enumerate((one, two, three, four, five)):
-                late = turn * LAG
+                late = turn * lag
                 if 0 <= step - late < len(jobs):
                     stage(*jobs[step - late])
             feed()

time: 391 us -> 382 us (0.977)
  Pallas kernels: 319 us -> 310 us
    pallas_call x6, Pallas kernels: 301 us -> 292 us  [move(): pl.pallas_call(functools.partial(move_kernel, place, (len(swaps), len(gat...]
where the time goes in v8:
time: 382 us
  Pallas kernels  310 us (81%)
  matrix products  46 us (12%)
  local copies, waits for them, and re-layouts  14.6 us (4%)
  other arithmetic  9.58 us (3%)
    pallas_call x6, Pallas kernels, move(): pl.pallas_call(functools.partial(move_kernel, place, (len(swaps), len(gat...  292 us
    dot_general x18, matrix products, contract(): return jnp.einsum(spec, left, right, preferred_element_type=jnp.float32)  46 us
    pallas_call x1, Pallas kernels, slopes(): pl.pallas_call(slopes_kernel, grid=grid, out_shape=[jax.ShapeDtypeStruct(...  10.9 us
    unnamed x56, local copies, waits for them, and re-layouts  9.1 us

profile of v8, /device:TPU:0, one launch (start us, length us, event | category | flops | bytes accessed | tf_op | source)
XLA Modules:
  0.0 381.5 jit_solution(740578742399544629)
XLA Ops:
  2.1 64.2 %move_0.1 = (bf16[2,2,4,2,40,1280]{5,4,3,2,1,0:T(8,128)(2,1)}, bf16[2,2,4,2,16,128]{5,4,3,2,1,0:T(8,128)(2,1)}, bf16[2,2,4,2,40,1280]{5,4,3,2,1,0:T(8,128)(2,1)}...) custom-call(bf16[40,1280]{1,0:T(8,128)(2,1)} %refs_0_.1, ...), custom_call_target="tpu_custom_call" | custom-call | tf_op jit(solution)/shard_map/move_0/pallas_call | solution.py:589
  69.0 4.6 %multiply_convert_fusion.2 = (bf16[1280,256]{1,0:T(8,128)(2,1)}, f32[1280,256]{1,0:T(8,128)}) fusion(f32[1280]{0:T(1024)S(1)} %mul.163, f32[1280]{0:T(1024)S(1)} %add.108, bf16[1280,1280]{1,0:T(8,128)(2,1)} %bitcast.152, bf16[256,1280]{1,0:T(8,128)(2,1)S(1)} %bitcast.110), kind=kOutput, calls=%fused_computation.40 | convolution fusion | flops 839843840 | bytes 5908480 | tf_op jit(solution)/shard_map/df,rd->fr/dot_general | solution.py:744
  73.6 1.9 convolution_convert_fusion.7
  75.6 3.9 %fusion.5 = bf16[1280,256]{1,0:T(8,128)(2,1)} fusion(bf16[1280,1280]{1,0:T(8,128)(2,1)} %bitcast.150, bf16[256,1280]{1,0:T(8,128)(2,1)S(1)} %bitcast.112, f32[1280]{0:T(1024)S(1)} %add.112), kind=kOutput, calls=%fused_computation.19 | convolution fusion | flops 839516160 | bytes 4592640 | tf_op jit(solution)/shard_map/df,rd->fr/dot_general | solution.py:744
  79.5 71.1 %move_1.1 = (bf16[8,160,256]{2,1,0:T(8,128)(2,1)}, bf16[8,160,256]{2,1,0:T(8,128)(2,1)}, bf16[8,160,256]{2,1,0:T(8,128)(2,1)}, bf16[2,2,4,2,40,1280]{5,4,3,2,1,0...) custom-call(bf16[8,160,256]{2,1,0:T(8,128)(2,1)} %bitcast.137, ...), custom_call_target="tpu_custom_call" | custom-call | tf_op jit(solution)/shard_map/move_1/pallas_call | solution.py:589
  150.6 7.2 %attend.1 = (bf16[8,160,256]{2,1,0:T(8,128)(2,1)}, f32[8,160,256]{2,1,0:T(8,128)}, f32[2,2,1,1024]{3,2,1,0:T(1,128)}) custom-call(bf16[8,160,256]{2,1,0:T(8,128)(2,1)} %get-tuple-element.54.q_ref, bf16[8,160,256]{2,1,0:T(8,128)(2,1)} %get-tuple-element.55.k_ref, bf16[8,160,256]{2,1,0:T(8,128)(2,1)} %get-tuple-element.56.v_ref), custom_call_target="tpu_custom_call" | custom-call | tf_op jit(solution)/shard_map/attend/pallas_call | solution.py:663
  157.8 14.8 %move_2.1 = bf16[8,160,256]{2,1,0:T(8,128)(2,1)} custom-call(bf16[8,160,256]{2,1,0:T(8,128)(2,1)} %get-tuple-element.57.refs_0_), custom_call_target="tpu_custom_call" | custom-call | tf_op jit(solution)/shard_map/move_2/pallas_call | solution.py:589
  172.7 3.3 multiply_reduce_fusion.5
  176.3 3.2 convolution_add_fusion.3
  179.5 2.1 fusion.6
  181.6 1.2 convert_reduce_fusion.1
  184.7 1.9 convert_reduce_fusion.2
  187.1 1.9 convolution_convert_fusion.6
  189.0 18.9 %move_3.1.do_ref = bf16[8,160,256]{2,1,0:T(8,128)(2,1)} custom-call(bf16[8,160,256]{2,1,0:T(8,128)(2,1)} %bitcast.136), custom_call_target="tpu_custom_call" | custom-call | tf_op jit(solution)/shard_map/move_3/pallas_call | solution.py:589
  208.6 10.9 %slopes.1 = (bf16[8,160,256]{2,1,0:T(8,128)(2,1)}, bf16[8,160,256]{2,1,0:T(8,128)(2,1)}, bf16[8,160,256]{2,1,0:T(8,128)(2,1)}) custom-call(bf16[8,160,256]{2,1,0:T(8,128)(2,1)} %get-tuple-element.54.q_ref, bf16[8,160,256]{2,1,0:T(8,128)(2,1)} %get-tuple-element.55.k_ref, bf16[8,160,256]{2,1,0:T(8,128)(2,1)} %get-tuple-element.56.v_ref, ...), custom_call_target="tpu_custom_call" | custom-call | tf_op jit(solution)/shard_map/slopes/pallas_call | solution.py:727
  219.5 2.7 convolution_convert_fusion.5
  222.2 2.8 convolution_convert_fusion.4
  225.1 3.0 convolution_convert_fusion.3
  228.1 65.0 %move_4.1 = (bf16[8,160,256]{2,1,0:T(8,128)(2,1)}, bf16[8,160,256]{2,1,0:T(8,128)(2,1)}, bf16[8,160,256]{2,1,0:T(8,128)(2,1)}, f32[40,1280]{1,0:T(8,128)}, bf16[...) custom-call(bf16[8,160,256]{2,1,0:T(8,128)(2,1)} %get-tuple-element.63.refs_0_, ...), custom_call_target="tpu_custom_call" | custom-call | tf_op jit(solution)/shard_map/move_4/pallas_call | solution.py:589
  293.1 3.3 fusion.11
  298.6 1.4 multiply_reduce_fusion.2
  300.0 1.2 add_convert_fusion
  301.3 2.8 convolution_convert_fusion.2
  304.1 2.8 convolution_convert_fusion.1
  306.8 2.8 convolution_convert_fusion
  311.3 1.8 multiply_reduce_fusion
  313.9 58.0 %move_5.1 = (f32[40,1280]{1,0:T(8,128)}, f32[40,1280]{1,0:T(8,128)}, f32[40,1280]{1,0:T(8,128)}, f32[40,1280]{1,0:T(8,128)}, f32[40,1280]{1,0:T(8,128)}, /*index=5*/f32[8,128]{1,0:T(8,128)}) custom-call(bf16[4,40,1280]{2,1,0:T(8,128)(2,1)} %get-tuple-element.69.refs_0_, bf16[4,40,1280]{2,1,0:T(8,128)(2,1)} %get-tuple-element.70.refs_1_, ...), custom_call_target="tpu_custom_call" | custom-call | tf_op jit(solution)/shard_map/move_5/pallas_call | solution.py:589
  371.9 1.5 slice_bitcast_fusion
  373.4 1.2 divide_multiply_fusion
  374.6 1.6 copy.44
  376.2 1.6 copy.45
  377.9 1.6 copy.46
  (92 shorter events, 14.0 us)
Async XLA Ops:
  0.6 67.9 %copy-start = (bf16[2,128,1,1280]{3,1,2,0:T(8,128)(2,1)S(1)}, bf16[2,128,1,1280]{3,1,2,0:T(8,128)(2,1)}, u32[]{:S(2)}) copy-start(bf16[2,128,1,1280]{3,1,2,0:T(8,128)(2,1)} %param.16) | copy-start | bytes 1966084
  69.0 4.6 %copy-start.5 = (bf16[2,2,4,2,40,1280]{5,4,3,2,1,0:T(8,128)(2,1)S(1)}, bf16[2,2,4,2,40,1280]{5,4,3,2,1,0:T(8,128)(2,1)}, u32[]{:S(2)}) copy-start(bf16[2,2,4,2,40,1280]{5,4,3,2,1,0:T(8,128)(2,1)} %get-tuple-element.49) | copy-start | bytes 9830404
  176.0 6.9 %copy-start.2 = (f32[256,1280]{1,0:T(8,128)}, f32[256,1280]{1,0:T(8,128)S(1)}, u32[]{:S(2)}) copy-start(f32[256,1280]{1,0:T(8,128)S(1)} %get-tuple-element.135) | copy-start | bytes 3932164
  176.2 3.2 copy-start.21
  179.5 2.1 copy-start.23
  179.5 2.1 copy-start.8
  181.6 1.9 copy-start.20
  182.8 1.9 copy-start.13
  184.7 2.3 copy-start.19
  189.0 18.9 %copy-start.22 = (bf16[80]{0:T(256)(128)(2,1)S(1)}, bf16[80]{0:T(256)(128)(2,1)}, u32[]{:S(2)}) copy-start(bf16[80]{0:T(256)(128)(2,1)} %param.31) | copy-start | bytes 484
  208.6 10.9 %copy-start.4 = (bf16[8,160,256]{2,1,0:T(8,128)(2,1)S(1)}, bf16[8,160,256]{2,1,0:T(8,128)(2,1)}, u32[]{:S(2)}) copy-start(bf16[8,160,256]{2,1,0:T(8,128)(2,1)} %move_2.1) | copy-start | bytes 1966084
  219.5 2.8 copy-start.3
  219.5 2.7 copy-start.14
  222.2 2.8 copy-start.9
  222.2 2.8 copy-start.24
  293.1 3.4 copy-start.6
  293.1 3.4 copy-start.7
  296.5 1.1 copy-start.11
  296.5 2.1 copy-start.18
  300.0 1.3 copy-start.1
  306.8 2.9 copy-start.12
  309.7 1.2 copy-start.10
  371.9 7.6 %copy-start.15 = (f32[40,1280]{1,0:T(8,128)S(1)}, f32[40,1280]{1,0:T(8,128)}, u32[]{:S(2)}) copy-start(f32[40,1280]{1,0:T(8,128)} %get-tuple-element.166) | copy-start | bytes 614404
  371.9 8.2 %copy-start.17 = (f32[40,1280]{1,0:T(8,128)S(1)}, f32[40,1280]{1,0:T(8,128)}, u32[]{:S(2)}) copy-start(f32[40,1280]{1,0:T(8,128)} %get-tuple-element.169) | copy-start | bytes 614404
  371.9 8.9 %copy-start.16 = (f32[40,1280]{1,0:T(8,128)S(1)}, f32[40,1280]{1,0:T(8,128)}, u32[]{:S(2)}) copy-start(f32[40,1280]{1,0:T(8,128)} %get-tuple-element.171) | copy-start | bytes 614404

commit v9 on v8

--- a/solution.py
+++ b/solution.py
@@ -897,8 +897,8 @@
     late = as_parts(query_mat_grad, key_mat_grad, value_mat_grad)
     if merged:
         output_mat_grad, *early = early
-        hidden_mat_grad, project_grad, *late, vector_sums = move(
-            place, 5, scatters=(*early, *late, vector_grads)
+        hidden_mat_grad, project_grad, vector_sums, *late = move(
+            place, 5, scatters=(*early, vector_grads, *late)
         )
     else:
         (vector_sums,) = move(place, 5, scatters=(vector_grads,))

time: 382 us -> 385 us (level)
  Pallas kernels: 310 us -> 314 us
    unnamed x56 -> x60, local copies, waits for them, and re-layouts: 9.1 us -> 9.1 us
where the time goes in v9:
time: 385 us
  Pallas kernels  314 us (82%)
  matrix products  46 us (12%)
  local copies, waits for them, and re-layouts  14.6 us (4%)
  other arithmetic  9.48 us (2%)
    pallas_call x6, Pallas kernels, move(): pl.pallas_call(functools.partial(move_kernel, place, (len(swaps), len(gat...  296 us
    dot_general x18, matrix products, contract(): return jnp.einsum(spec, left, right, preferred_element_type=jnp.float32)  46 us
    pallas_call x1, Pallas kernels, slopes(): pl.pallas_call(slopes_kernel, grid=grid, out_shape=[jax.ShapeDtypeStruct(...  10.9 us
    unnamed x60, local copies, waits for them, and re-layouts  9.1 us

profile of v9, /device:TPU:0, one launch (start us, length us, event | category | flops | bytes accessed | tf_op | source)
XLA Modules:
  0.0 385.0 jit_solution(18225176621531119294)
XLA Ops:
  2.1 64.2 %move_0.1 = (bf16[2,2,4,2,40,1280]{5,4,3,2,1,0:T(8,128)(2,1)}, bf16[2,2,4,2,16,128]{5,4,3,2,1,0:T(8,128)(2,1)}, bf16[2,2,4,2,40,1280]{5,4,3,2,1,0:T(8,128)(2,1)}...) custom-call(bf16[40,1280]{1,0:T(8,128)(2,1)} %refs_0_.1, ...), custom_call_target="tpu_custom_call" | custom-call | tf_op jit(solution)/shard_map/move_0/pallas_call | solution.py:589
  69.0 4.6 %multiply_convert_fusion.2 = (bf16[1280,256]{1,0:T(8,128)(2,1)}, f32[1280,256]{1,0:T(8,128)}) fusion(f32[1280]{0:T(1024)S(1)} %mul.163, f32[1280]{0:T(1024)S(1)} %add.108, bf16[1280,1280]{1,0:T(8,128)(2,1)} %bitcast.152, bf16[256,1280]{1,0:T(8,128)(2,1)S(1)} %bitcast.110), kind=kOutput, calls=%fused_computation.40 | convolution fusion | flops 839843840 | bytes 5908480 | tf_op jit(solution)/shard_map/df,rd->fr/dot_general | solution.py:744
  73.6 1.9 convolution_convert_fusion.7
  75.6 3.9 %fusion.5 = bf16[1280,256]{1,0:T(8,128)(2,1)} fusion(bf16[1280,1280]{1,0:T(8,128)(2,1)} %bitcast.150, bf16[256,1280]{1,0:T(8,128)(2,1)S(1)} %bitcast.112, f32[1280]{0:T(1024)S(1)} %add.112), kind=kOutput, calls=%fused_computation.19 | convolution fusion | flops 839516160 | bytes 4592640 | tf_op jit(solution)/shard_map/df,rd->fr/dot_general | solution.py:744
  79.5 71.1 %move_1.1 = (bf16[8,160,256]{2,1,0:T(8,128)(2,1)}, bf16[8,160,256]{2,1,0:T(8,128)(2,1)}, bf16[8,160,256]{2,1,0:T(8,128)(2,1)}, bf16[2,2,4,2,40,1280]{5,4,3,2,1,0...) custom-call(bf16[8,160,256]{2,1,0:T(8,128)(2,1)} %bitcast.137, ...), custom_call_target="tpu_custom_call" | custom-call | tf_op jit(solution)/shard_map/move_1/pallas_call | solution.py:589
  150.6 7.2 %attend.1 = (bf16[8,160,256]{2,1,0:T(8,128)(2,1)}, f32[8,160,256]{2,1,0:T(8,128)}, f32[2,2,1,1024]{3,2,1,0:T(1,128)}) custom-call(bf16[8,160,256]{2,1,0:T(8,128)(2,1)} %get-tuple-element.54.q_ref, bf16[8,160,256]{2,1,0:T(8,128)(2,1)} %get-tuple-element.55.k_ref, bf16[8,160,256]{2,1,0:T(8,128)(2,1)} %get-tuple-element.56.v_ref), custom_call_target="tpu_custom_call" | custom-call | tf_op jit(solution)/shard_map/attend/pallas_call | solution.py:663
  157.8 14.8 %move_2.1 = bf16[8,160,256]{2,1,0:T(8,128)(2,1)} custom-call(bf16[8,160,256]{2,1,0:T(8,128)(2,1)} %get-tuple-element.57.refs_0_), custom_call_target="tpu_custom_call" | custom-call | tf_op jit(solution)/shard_map/move_2/pallas_call | solution.py:589
  172.7 3.3 multiply_reduce_fusion.5
  176.3 3.2 convolution_add_fusion.3
  179.5 2.1 fusion.6
  181.6 1.2 convert_reduce_fusion.1
  184.7 1.9 convert_reduce_fusion.2
  187.1 1.9 convolution_convert_fusion.6
  189.0 18.8 %move_3.1.do_ref = bf16[8,160,256]{2,1,0:T(8,128)(2,1)} custom-call(bf16[8,160,256]{2,1,0:T(8,128)(2,1)} %bitcast.136), custom_call_target="tpu_custom_call" | custom-call | tf_op jit(solution)/shard_map/move_3/pallas_call | solution.py:589
  208.6 10.9 %slopes.1 = (bf16[8,160,256]{2,1,0:T(8,128)(2,1)}, bf16[8,160,256]{2,1,0:T(8,128)(2,1)}, bf16[8,160,256]{2,1,0:T(8,128)(2,1)}) custom-call(bf16[8,160,256]{2,1,0:T(8,128)(2,1)} %get-tuple-element.54.q_ref, bf16[8,160,256]{2,1,0:T(8,128)(2,1)} %get-tuple-element.55.k_ref, bf16[8,160,256]{2,1,0:T(8,128)(2,1)} %get-tuple-element.56.v_ref, ...), custom_call_target="tpu_custom_call" | custom-call | tf_op jit(solution)/shard_map/slopes/pallas_call | solution.py:727
  219.5 2.7 convolution_convert_fusion.5
  222.2 2.8 convolution_convert_fusion.4
  225.1 3.0 convolution_convert_fusion.3
  228.1 65.0 %move_4.1 = (bf16[8,160,256]{2,1,0:T(8,128)(2,1)}, bf16[8,160,256]{2,1,0:T(8,128)(2,1)}, bf16[8,160,256]{2,1,0:T(8,128)(2,1)}, f32[40,1280]{1,0:T(8,128)}, bf16[...) custom-call(bf16[8,160,256]{2,1,0:T(8,128)(2,1)} %get-tuple-element.63.refs_0_, ...), custom_call_target="tpu_custom_call" | custom-call | tf_op jit(solution)/shard_map/move_4/pallas_call | solution.py:589
  293.1 3.3 fusion.11
  298.6 1.4 multiply_reduce_fusion.2
  300.0 1.2 add_convert_fusion
  301.4 1.8 convert_reduce_fusion.3
  305.4 2.8 convolution_convert_fusion.2
  308.1 2.8 convolution_convert_fusion.1
  310.9 2.8 convolution_convert_fusion
  313.8 61.6 %move_5.1 = (f32[40,1280]{1,0:T(8,128)}, f32[40,1280]{1,0:T(8,128)}, f32[8,128]{1,0:T(8,128)}, f32[40,1280]{1,0:T(8,128)}, f32[40,1280]{1,0:T(8,128)}, /*index=5*/f32[40,1280]{1,0:T(8,128)}) custom-call(bf16[4,40,1280]{2,1,0:T(8,128)(2,1)} %get-tuple-element.69.refs_0_, bf16[4,40,1280]{2,1,0:T(8,128)(2,1)} %get-tuple-element.70.refs_1_, ...), custom_call_target="tpu_custom_call" | custom-call | tf_op jit(solution)/shard_map/move_5/pallas_call | solution.py:589
  375.4 1.5 slice_bitcast_fusion
  376.8 1.2 divide_multiply_fusion
  378.1 1.6 copy.44
  379.7 1.6 copy.45
  381.3 1.6 copy.46
  (96 shorter events, 13.8 us)
Async XLA Ops:
  0.6 67.9 %copy-start = (bf16[2,128,1,1280]{3,1,2,0:T(8,128)(2,1)S(1)}, bf16[2,128,1,1280]{3,1,2,0:T(8,128)(2,1)}, u32[]{:S(2)}) copy-start(bf16[2,128,1,1280]{3,1,2,0:T(8,128)(2,1)} %param.16) | copy-start | bytes 1966084
  69.0 4.6 %copy-start.5 = (bf16[2,2,4,2,40,1280]{5,4,3,2,1,0:T(8,128)(2,1)S(1)}, bf16[2,2,4,2,40,1280]{5,4,3,2,1,0:T(8,128)(2,1)}, u32[]{:S(2)}) copy-start(bf16[2,2,4,2,40,1280]{5,4,3,2,1,0:T(8,128)(2,1)} %get-tuple-element.49) | copy-start | bytes 9830404
  176.0 6.9 %copy-start.2 = (f32[256,1280]{1,0:T(8,128)}, f32[256,1280]{1,0:T(8,128)S(1)}, u32[]{:S(2)}) copy-start(f32[256,1280]{1,0:T(8,128)S(1)} %get-tuple-element.135) | copy-start | bytes 3932164
  176.2 3.2 copy-start.23
  179.5 2.1 copy-start.25
  179.5 2.1 copy-start.9
  181.6 1.9 copy-start.22
  182.8 1.9 copy-start.15
  184.7 2.3 copy-start.21
  189.0 18.8 %copy-start.24 = (bf16[80]{0:T(256)(128)(2,1)S(1)}, bf16[80]{0:T(256)(128)(2,1)}, u32[]{:S(2)}) copy-start(bf16[80]{0:T(256)(128)(2,1)} %param.31) | copy-start | bytes 484
  208.6 10.9 %copy-start.4 = (bf16[8,160,256]{2,1,0:T(8,128)(2,1)S(1)}, bf16[8,160,256]{2,1,0:T(8,128)(2,1)}, u32[]{:S(2)}) copy-start(bf16[8,160,256]{2,1,0:T(8,128)(2,1)} %move_2.1) | copy-start | bytes 1966084
  219.5 2.8 copy-start.3
  219.5 2.7 copy-start.16
  222.2 2.8 copy-start.10
  222.2 2.8 copy-start.26
  293.1 3.4 copy-start.6
  293.1 3.4 copy-start.7
  296.5 1.1 copy-start.12
  296.5 2.1 copy-start.20
  300.0 1.4 copy-start.1
  301.3 2.4 copy-start.11
  301.3 2.8 copy-start.14
  305.4 2.8 copy-start.8
  308.1 2.8 copy-start.13
  375.3 7.6 %copy-start.17 = (f32[40,1280]{1,0:T(8,128)S(1)}, f32[40,1280]{1,0:T(8,128)}, u32[]{:S(2)}) copy-start(f32[40,1280]{1,0:T(8,128)} %get-tuple-element.166) | copy-start | bytes 614404
  375.4 8.2 %copy-start.19 = (f32[40,1280]{1,0:T(8,128)S(1)}, f32[40,1280]{1,0:T(8,128)}, u32[]{:S(2)}) copy-start(f32[40,1280]{1,0:T(8,128)} %get-tuple-element.169) | copy-start | bytes 614404
  375.4 8.9 %copy-start.18 = (f32[40,1280]{1,0:T(8,128)S(1)}, f32[40,1280]{1,0:T(8,128)}, u32[]{:S(2)}) copy-start(f32[40,1280]{1,0:T(8,128)} %get-tuple-element.171) | copy-start | bytes 614404

commit v10 on v8

--- a/solution.py
+++ b/solution.py
@@ -767,10 +767,10 @@
     vectors = (norm_one, query_add, value_add, output_add, norm_two, hidden_add, project_add)
     share = norm_one.shape[0]
     small = jnp.pad(jnp.stack(vectors), ((0, 16 - len(vectors)), (0, 128 - share)))
-    query_mat, small, key_mat, value_mat, output_mat, hidden_mat, project_mat = move(
+    query_mat, key_mat, value_mat, small, output_mat, hidden_mat, project_mat = move(
         place,
         0,
-        gathers=(query_mat, small, key_mat, value_mat, output_mat, hidden_mat, project_mat),
+        gathers=(query_mat, key_mat, value_mat, small, output_mat, hidden_mat, project_mat),
         tails=3,
     )
     small = small.reshape(-1, 16, 128)[:, : len(vectors), :share]

time: 382 us -> 383 us (level)
  no operation moved by 1% of the time
where the time goes in v10:
time: 383 us
  Pallas kernels  311 us (81%)
  matrix products  46.1 us (12%)
  local copies, waits for them, and re-layouts  14.6 us (4%)
  other arithmetic  9.58 us (3%)
    pallas_call x6, Pallas kernels, move(): pl.pallas_call(functools.partial(move_kernel, place, (len(swaps), len(gat...  293 us
    dot_general x18, matrix products, contract(): return jnp.einsum(spec, left, right, preferred_element_type=jnp.float32)  46.1 us
    pallas_call x1, Pallas kernels, slopes(): pl.pallas_call(slopes_kernel, grid=grid, out_shape=[jax.ShapeDtypeStruct(...  10.9 us
    unnamed x56, local copies, waits for them, and re-layouts  9.09 us

profile of v10, /device:TPU:0, one launch (start us, length us, event | category | flops | bytes accessed | tf_op | source)
XLA Modules:
  0.0 382.8 jit_solution(6844411153365935733)
XLA Ops:
  2.1 66.0 %move_0.1 = (bf16[2,2,4,2,40,1280]{5,4,3,2,1,0:T(8,128)(2,1)}, bf16[2,2,4,2,40,1280]{5,4,3,2,1,0:T(8,128)(2,1)}, bf16[2,2,4,2,40,1280]{5,4,3,2,1,0:T(8,128)(2,1)...) custom-call(bf16[40,1280]{1,0:T(8,128)(2,1)} %refs_0_.1, ...), custom_call_target="tpu_custom_call" | custom-call | tf_op jit(solution)/shard_map/move_0/pallas_call | solution.py:589
  70.7 4.6 %multiply_convert_fusion.2 = (bf16[1280,256]{1,0:T(8,128)(2,1)}, f32[1280,256]{1,0:T(8,128)}) fusion(f32[1280]{0:T(1024)S(1)} %mul.163, f32[1280]{0:T(1024)S(1)} %add.108, bf16[1280,1280]{1,0:T(8,128)(2,1)} %bitcast.152, bf16[256,1280]{1,0:T(8,128)(2,1)S(1)} %bitcast.110), kind=kOutput, calls=%fused_computation.40 | convolution fusion | flops 839843840 | bytes 5908480 | tf_op jit(solution)/shard_map/df,rd->fr/dot_general | solution.py:744
  75.3 1.9 convolution_convert_fusion.7
  77.3 3.9 %fusion.5 = bf16[1280,256]{1,0:T(8,128)(2,1)} fusion(bf16[1280,1280]{1,0:T(8,128)(2,1)} %bitcast.150, bf16[256,1280]{1,0:T(8,128)(2,1)S(1)} %bitcast.112, f32[1280]{0:T(1024)S(1)} %add.112), kind=kOutput, calls=%fused_computation.19 | convolution fusion | flops 839516160 | bytes 4592640 | tf_op jit(solution)/shard_map/df,rd->fr/dot_general | solution.py:744
  81.2 71.6 %move_1.1 = (bf16[8,160,256]{2,1,0:T(8,128)(2,1)}, bf16[8,160,256]{2,1,0:T(8,128)(2,1)}, bf16[8,160,256]{2,1,0:T(8,128)(2,1)}, bf16[2,2,4,2,40,1280]{5,4,3,2,1,0...) custom-call(bf16[8,160,256]{2,1,0:T(8,128)(2,1)} %bitcast.137, ...), custom_call_target="tpu_custom_call" | custom-call | tf_op jit(solution)/shard_map/move_1/pallas_call | solution.py:589
  152.9 7.2 %attend.1 = (bf16[8,160,256]{2,1,0:T(8,128)(2,1)}, f32[8,160,256]{2,1,0:T(8,128)}, f32[2,2,1,1024]{3,2,1,0:T(1,128)}) custom-call(bf16[8,160,256]{2,1,0:T(8,128)(2,1)} %get-tuple-element.54.q_ref, bf16[8,160,256]{2,1,0:T(8,128)(2,1)} %get-tuple-element.55.k_ref, bf16[8,160,256]{2,1,0:T(8,128)(2,1)} %get-tuple-element.56.v_ref), custom_call_target="tpu_custom_call" | custom-call | tf_op jit(solution)/shard_map/attend/pallas_call | solution.py:663
  160.1 14.8 %move_2.1 = bf16[8,160,256]{2,1,0:T(8,128)(2,1)} custom-call(bf16[8,160,256]{2,1,0:T(8,128)(2,1)} %get-tuple-element.57.refs_0_), custom_call_target="tpu_custom_call" | custom-call | tf_op jit(solution)/shard_map/move_2/pallas_call | solution.py:589
  174.9 3.3 multiply_reduce_fusion.5
  178.5 3.2 convolution_add_fusion.3
  181.8 2.1 fusion.6
  183.9 1.2 convert_reduce_fusion.1
  185.8 1.2 multiply_reduce_fusion.1
  187.0 1.9 convert_reduce_fusion.2
  189.3 1.9 convolution_convert_fusion.6
  191.2 17.8 %move_3.1.do_ref = bf16[8,160,256]{2,1,0:T(8,128)(2,1)} custom-call(bf16[8,160,256]{2,1,0:T(8,128)(2,1)} %bitcast.136), custom_call_target="tpu_custom_call" | custom-call | tf_op jit(solution)/shard_map/move_3/pallas_call | solution.py:589
  209.8 10.9 %slopes.1 = (bf16[8,160,256]{2,1,0:T(8,128)(2,1)}, bf16[8,160,256]{2,1,0:T(8,128)(2,1)}, bf16[8,160,256]{2,1,0:T(8,128)(2,1)}) custom-call(bf16[8,160,256]{2,1,0:T(8,128)(2,1)} %get-tuple-element.54.q_ref, bf16[8,160,256]{2,1,0:T(8,128)(2,1)} %get-tuple-element.55.k_ref, bf16[8,160,256]{2,1,0:T(8,128)(2,1)} %get-tuple-element.56.v_ref, ...), custom_call_target="tpu_custom_call" | custom-call | tf_op jit(solution)/shard_map/slopes/pallas_call | solution.py:727
  220.7 2.7 convolution_convert_fusion.5
  223.4 2.8 convolution_convert_fusion.4
  226.3 3.0 convolution_convert_fusion.3
  229.3 65.0 %move_4.1 = (bf16[8,160,256]{2,1,0:T(8,128)(2,1)}, bf16[8,160,256]{2,1,0:T(8,128)(2,1)}, bf16[8,160,256]{2,1,0:T(8,128)(2,1)}, f32[40,1280]{1,0:T(8,128)}, bf16[...) custom-call(bf16[8,160,256]{2,1,0:T(8,128)(2,1)} %get-tuple-element.63.refs_0_, ...), custom_call_target="tpu_custom_call" | custom-call | tf_op jit(solution)/shard_map/move_4/pallas_call | solution.py:589
  294.3 3.3 fusion.11
  299.8 1.4 multiply_reduce_fusion.2
  301.2 1.2 add_convert_fusion
  302.5 2.8 convolution_convert_fusion.2
  305.2 2.8 convolution_convert_fusion.1
  308.0 2.8 convolution_convert_fusion
  312.5 1.8 multiply_reduce_fusion
  315.1 58.1 %move_5.1 = (f32[40,1280]{1,0:T(8,128)}, f32[40,1280]{1,0:T(8,128)}, f32[40,1280]{1,0:T(8,128)}, f32[40,1280]{1,0:T(8,128)}, f32[40,1280]{1,0:T(8,128)}, /*index=5*/f32[8,128]{1,0:T(8,128)}) custom-call(bf16[4,40,1280]{2,1,0:T(8,128)(2,1)} %get-tuple-element.69.refs_0_, bf16[4,40,1280]{2,1,0:T(8,128)(2,1)} %get-tuple-element.70.refs_1_, ...), custom_call_target="tpu_custom_call" | custom-call | tf_op jit(solution)/shard_map/move_5/pallas_call | solution.py:589
  373.2 1.5 slice_bitcast_fusion
  375.9 1.6 copy.44
  377.5 1.6 copy.45
  379.1 1.6 copy.46
  (92 shorter events, 14.0 us)
Async XLA Ops:
  0.6 69.6 %copy-start = (bf16[2,128,1,1280]{3,1,2,0:T(8,128)(2,1)S(1)}, bf16[2,128,1,1280]{3,1,2,0:T(8,128)(2,1)}, u32[]{:S(2)}) copy-start(bf16[2,128,1,1280]{3,1,2,0:T(8,128)(2,1)} %param.16) | copy-start | bytes 1966084
  70.7 4.6 %copy-start.5 = (bf16[2,2,4,2,40,1280]{5,4,3,2,1,0:T(8,128)(2,1)S(1)}, bf16[2,2,4,2,40,1280]{5,4,3,2,1,0:T(8,128)(2,1)}, u32[]{:S(2)}) copy-start(bf16[2,2,4,2,40,1280]{5,4,3,2,1,0:T(8,128)(2,1)} %get-tuple-element.49) | copy-start | bytes 9830404
  178.2 6.9 %copy-start.2 = (f32[256,1280]{1,0:T(8,128)}, f32[256,1280]{1,0:T(8,128)S(1)}, u32[]{:S(2)}) copy-start(f32[256,1280]{1,0:T(8,128)S(1)} %get-tuple-element.135) | copy-start | bytes 3932164
  178.5 3.2 copy-start.21
  181.8 2.1 copy-start.23
  181.8 2.1 copy-start.8
  183.9 1.9 copy-start.20
  185.1 1.9 copy-start.13
  187.0 2.3 copy-start.19
  191.2 17.8 %copy-start.22 = (bf16[80]{0:T(256)(128)(2,1)S(1)}, bf16[80]{0:T(256)(128)(2,1)}, u32[]{:S(2)}) copy-start(bf16[80]{0:T(256)(128)(2,1)} %param.31) | copy-start | bytes 484
  209.8 10.9 %copy-start.4 = (bf16[8,160,256]{2,1,0:T(8,128)(2,1)S(1)}, bf16[8,160,256]{2,1,0:T(8,128)(2,1)}, u32[]{:S(2)}) copy-start(bf16[8,160,256]{2,1,0:T(8,128)(2,1)} %move_2.1) | copy-start | bytes 1966084
  220.7 2.8 copy-start.3
  220.7 2.7 copy-start.14
  223.4 2.8 copy-start.9
  223.4 2.8 copy-start.24
  294.3 3.4 copy-start.6
  294.3 3.4 copy-start.7
  297.7 1.1 copy-start.11
  297.7 2.1 copy-start.18
  301.2 1.3 copy-start.1
  308.0 2.9 copy-start.12
  310.9 1.2 copy-start.10
  373.2 7.6 %copy-start.15 = (f32[40,1280]{1,0:T(8,128)S(1)}, f32[40,1280]{1,0:T(8,128)}, u32[]{:S(2)}) copy-start(f32[40,1280]{1,0:T(8,128)} %get-tuple-element.166) | copy-start | bytes 614404
  373.2 8.2 %copy-start.17 = (f32[40,1280]{1,0:T(8,128)S(1)}, f32[40,1280]{1,0:T(8,128)}, u32[]{:S(2)}) copy-start(f32[40,1280]{1,0:T(8,128)} %get-tuple-element.169) | copy-start | bytes 614404
  373.2 8.9 %copy-start.16 = (f32[40,1280]{1,0:T(8,128)S(1)}, f32[40,1280]{1,0:T(8,128)}, u32[]{:S(2)}) copy-start(f32[40,1280]{1,0:T(8,128)} %get-tuple-element.171) | copy-start | bytes 614404
